TPU v7x, 8 devices: a whole 2x2x1 slice. The times are simulated.
8 devices in a mesh: dp: 1 (over z), tp: 8 (over y, x, core).
Axes of the slice: x: 2, y: 2, z: 1, core: 2. Of those that a mesh axis runs over, the one named last changes fastest.
Arguments:
- x_in: bfloat16 [256, 4096], P('dp')
- tok_pos: int32 [256], P('dp')
- conv_state: bfloat16 [2, 256, 3, 5632], P(None, 'dp', None, 'tp')
- lru_state: float32 [2, 256, 5632], P(None, 'dp', 'tp')
- k_cache: bfloat16 [256, 1024, 128], P('dp')
- v_cache: bfloat16 [256, 1024, 128], P('dp')
- slot_pos: int32 [256, 1024], P('dp')
- norm_scale: bfloat16 [3, 2, 4096], replicated
- rec_wx: bfloat16 [2, 4096, 5632], P(None, None, 'tp')
- rec_bx: bfloat16 [2, 5632], P(None, 'tp')
- rec_wy: bfloat16 [2, 4096, 5632], P(None, None, 'tp')
- rec_by: bfloat16 [2, 5632], P(None, 'tp')
- conv_w: bfloat16 [2, 4, 5632], P(None, None, 'tp')
- conv_b: bfloat16 [2, 5632], P(None, 'tp')
- gate_wa: bfloat16 [2, 32, 176, 176], P(None, 'tp')
- gate_ba: bfloat16 [2, 5632], P(None, 'tp')
- gate_wi: bfloat16 [2, 32, 176, 176], P(None, 'tp')
- gate_bi: bfloat16 [2, 5632], P(None, 'tp')
- a_param: float32 [2, 5632], P(None, 'tp')
- rec_wout: bfloat16 [2, 5632, 4096], P(None, 'tp')
- rec_bout: bfloat16 [2, 4096], replicated
- attn_wq: bfloat16 [4096, 4096], P(None, 'tp')
- attn_wk: bfloat16 [4096, 128], replicated
- attn_wv: bfloat16 [4096, 128], replicated
- attn_wo: bfloat16 [4096, 4096], P('tp')
- attn_bo: bfloat16 [4096], replicated
- mlp_w1: bfloat16 [3, 4096, 12288], P(None, None, 'tp')
- mlp_b1: bfloat16 [3, 12288], P(None, 'tp')
- mlp_w2: bfloat16 [3, 4096, 12288], P(None, None, 'tp')
- mlp_b2: bfloat16 [3, 12288], P(None, 'tp')
- mlp_wd: bfloat16 [3, 12288, 4096], P(None, 'tp')
- mlp_bd: bfloat16 [3, 4096], replicated
Outputs:
- output 1: bfloat16 [256, 4096], P('dp')
- output 2: bfloat16 [2, 256, 3, 5632], P(None, 'dp', None, 'tp')
- output 3: float32 [2, 256, 5632], P(None, 'dp', 'tp')
- output 4: bfloat16 [256, 1024, 128], P('dp')
- output 5: bfloat16 [256, 1024, 128], P('dp')
- output 6: int32 [256, 1024], P('dp')
All inputs are finite; a program needn't handle non-finite values.
Results may differ from a plain program's by a relative error of at most 0.02.
Values are sent between devices in bfloat16 or wider.
A program may use at most 1.75 GiB of HBM per device.

v0:
```python
import jax
import jax.numpy as jnp
from jax import lax
from jax.sharding import PartitionSpec as P

ROPE_BASE = 10000.0
NORM_EPS = 1e-6


def rms_norm(residual, scale):
    res_f = residual.astype(jnp.float32)
    mean_sq = jnp.mean(res_f * res_f, axis=-1, keepdims=True)
    return (res_f * lax.rsqrt(mean_sq + NORM_EPS) * (1.0 + scale.astype(jnp.float32))).astype(jnp.bfloat16)


def add_update(residual, update, out_bias):
    return (residual.astype(jnp.float32) + update.astype(jnp.bfloat16).astype(jnp.float32) + out_bias.astype(jnp.float32)).astype(jnp.bfloat16)


def rope_tables(tok_pos, head_dim):
    quarter = head_dim // 4
    inv_freq = ROPE_BASE ** (-jnp.arange(quarter, dtype=jnp.float32) / quarter)
    angles = tok_pos.astype(jnp.float32)[:, None] * inv_freq[None, :]
    return jnp.cos(angles), jnp.sin(angles)


def apply_rope(vectors, cosine, sine):
    quarter = vectors.shape[-1] // 4
    first = vectors[..., :quarter]
    second = vectors[..., quarter:2 * quarter]
    return jnp.concatenate([first * cosine - second * sine, second * cosine + first * sine, vectors[..., 2 * quarter:]], axis=-1)


def mlp_update(normed, w_up, b_up, w_lin, b_lin, w_down):
    gate_pre = jnp.dot(normed, w_up, preferred_element_type=jnp.float32) + b_up.astype(jnp.float32)
    lin_pre = jnp.dot(normed, w_lin, preferred_element_type=jnp.float32) + b_lin.astype(jnp.float32)
    hidden = (jax.nn.gelu(gate_pre, approximate=True) * lin_pre).astype(jnp.bfloat16)
    return jnp.dot(hidden, w_down, preferred_element_type=jnp.float32)


def recurrent_update(normed, tok_pos, conv_prev, lru_prev, rec_wx, rec_bx, rec_wy, rec_by, conv_w, conv_b, gate_wa, gate_ba, gate_wi, gate_bi, a_param, rec_wout):
    n_rows = normed.shape[0]
    n_blocks = gate_wa.shape[0]
    block_width = gate_wa.shape[1]
    x_branch = (jnp.dot(normed, rec_wx, preferred_element_type=jnp.float32) + rec_bx.astype(jnp.float32)).astype(jnp.bfloat16)
    y_branch = jax.nn.gelu(jnp.dot(normed, rec_wy, preferred_element_type=jnp.float32) + rec_by.astype(jnp.float32), approximate=True)
    tap_keep = tok_pos[:, None, None] >= jnp.arange(3, 0, -1, dtype=jnp.int32)[None, :, None]
    history = jnp.where(tap_keep, conv_prev.astype(jnp.float32), 0.0)
    tap_w = conv_w.astype(jnp.float32)
    conv_sum = conv_b.astype(jnp.float32) + tap_w[0] * x_branch.astype(jnp.float32) + jnp.sum(history * tap_w[:0:-1][None], axis=1)
    conv_x = conv_sum.astype(jnp.bfloat16)
    blocks = conv_x.reshape(n_rows, n_blocks, block_width)
    r_pre = jnp.einsum('bhi,hij->bhj', blocks, gate_wa, preferred_element_type=jnp.float32).reshape(n_rows, -1) + gate_ba.astype(jnp.float32)
    i_pre = jnp.einsum('bhi,hij->bhj', blocks, gate_wi, preferred_element_type=jnp.float32).reshape(n_rows, -1) + gate_bi.astype(jnp.float32)
    log_a = -8.0 * jax.nn.sigmoid(r_pre) * jax.nn.softplus(a_param)
    decay_gate = jnp.exp(log_a)
    in_scale = jnp.sqrt(1.0 - decay_gate * decay_gate)
    is_reset = (tok_pos == 0)[:, None]
    decay_gate = jnp.where(is_reset, 0.0, decay_gate)
    in_scale = jnp.where(is_reset, 1.0, in_scale)
    lru_new = decay_gate * lru_prev + in_scale * jax.nn.sigmoid(i_pre) * conv_x.astype(jnp.float32)
    gated_h = (lru_new * y_branch).astype(jnp.bfloat16)
    update = jnp.dot(gated_h, rec_wout, preferred_element_type=jnp.float32)
    conv_new = jnp.concatenate([conv_prev[:, 1:], x_branch[:, None, :]], axis=1)
    return update, conv_new, lru_new


def project_qkv(normed, tok_pos, attn_wq, attn_wk, attn_wv):
    n_rows = normed.shape[0]
    head_dim = attn_wk.shape[1]
    cosine, sine = rope_tables(tok_pos, head_dim)
    q_heads = jnp.dot(normed, attn_wq, preferred_element_type=jnp.float32).reshape(n_rows, -1, head_dim)
    q_heads = apply_rope(q_heads, cosine[:, None, :], sine[:, None, :]).astype(jnp.bfloat16)
    k_new = apply_rope(jnp.dot(normed, attn_wk, preferred_element_type=jnp.float32), cosine, sine).astype(jnp.bfloat16)
    v_new = jnp.dot(normed, attn_wv, preferred_element_type=jnp.float32).astype(jnp.bfloat16)
    return q_heads, k_new, v_new


def write_cache(tok_pos, k_new, v_new, k_cache, v_cache, slot_pos):
    window = k_cache.shape[1]
    target = jnp.arange(window, dtype=jnp.int32)[None, :] == (tok_pos % window)[:, None]
    k_next = jnp.where(target[:, :, None], k_new[:, None, :], k_cache)
    v_next = jnp.where(target[:, :, None], v_new[:, None, :], v_cache)
    slot_next = jnp.where(target, tok_pos[:, None], slot_pos)
    return k_next, v_next, slot_next


def attend(q_heads, tok_pos, k_next, v_next, slot_next, attn_wo):
    n_rows = q_heads.shape[0]
    window = k_next.shape[1]
    head_dim = k_next.shape[2]
    slot_age = tok_pos[:, None] - slot_next
    slot_valid = (slot_next >= 0) & (slot_age >= 0) & (slot_age < window)
    scores = jnp.einsum('bhd,bsd->bhs', q_heads, k_next, preferred_element_type=jnp.float32) * (head_dim ** -0.5)
    scores = jnp.where(slot_valid[:, None, :], scores, -jnp.inf)
    probs_bf = jax.nn.softmax(scores, axis=-1).astype(jnp.bfloat16)
    heads_out = jnp.einsum('bhs,bsd->bhd', probs_bf, v_next, preferred_element_type=jnp.float32).astype(jnp.bfloat16)
    return jnp.dot(heads_out.reshape(n_rows, -1), attn_wo, preferred_element_type=jnp.float32)


def io_specs():
    in_specs = (P('dp', None), P('dp'), P(None, 'dp', None, 'tp'), P(None, 'dp', 'tp'), P('dp', None, None), P('dp', None, None), P('dp', None),
                P(), P(None, None, 'tp'), P(None, 'tp'), P(None, None, 'tp'), P(None, 'tp'), P(None, None, 'tp'), P(None, 'tp'),
                P(None, 'tp', None, None), P(None, 'tp'), P(None, 'tp', None, None), P(None, 'tp'), P(None, 'tp'), P(None, 'tp', None), P(),
                P(None, 'tp'), P(), P(), P('tp', None), P(),
                P(None, None, 'tp'), P(None, 'tp'), P(None, None, 'tp'), P(None, 'tp'), P(None, 'tp', None), P())
    out_specs = (P('dp', None), P(None, 'dp', None, 'tp'), P(None, 'dp', 'tp'), P('dp', None, None), P('dp', None, None), P('dp', None))
    return in_specs, out_specs


def solution(mesh):
    in_specs, out_specs = io_specs()

    def local_step(x_in, tok_pos, conv_state, lru_state, k_cache, v_cache, slot_pos, norm_scale, rec_wx, rec_bx, rec_wy, rec_by, conv_w, conv_b, gate_wa, gate_ba, gate_wi, gate_bi, a_param, rec_wout, rec_bout, attn_wq, attn_wk, attn_wv, attn_wo, attn_bo, mlp_w1, mlp_b1, mlp_w2, mlp_b2, mlp_wd, mlp_bd):
        residual = x_in
        conv_list = []
        lru_list = []
        for layer_idx in range(3):
            normed = rms_norm(residual, norm_scale[layer_idx, 0])
            if layer_idx < 2:
                part_sum, conv_new, lru_new = recurrent_update(normed, tok_pos, conv_state[layer_idx], lru_state[layer_idx], rec_wx[layer_idx], rec_bx[layer_idx], rec_wy[layer_idx], rec_by[layer_idx], conv_w[layer_idx], conv_b[layer_idx], gate_wa[layer_idx], gate_ba[layer_idx], gate_wi[layer_idx], gate_bi[layer_idx], a_param[layer_idx], rec_wout[layer_idx])
                conv_list.append(conv_new)
                lru_list.append(lru_new)
                out_bias = rec_bout[layer_idx]
            else:
                q_heads, k_new, v_new = project_qkv(normed, tok_pos, attn_wq, attn_wk, attn_wv)
                k_next, v_next, slot_next = write_cache(tok_pos, k_new, v_new, k_cache, v_cache, slot_pos)
                part_sum = attend(q_heads, tok_pos, k_next, v_next, slot_next, attn_wo)
                out_bias = attn_bo
            residual = add_update(residual, lax.psum(part_sum.astype(jnp.bfloat16), 'tp'), out_bias)
            normed = rms_norm(residual, norm_scale[layer_idx, 1])
            part_sum = mlp_update(normed, mlp_w1[layer_idx], mlp_b1[layer_idx], mlp_w2[layer_idx], mlp_b2[layer_idx], mlp_wd[layer_idx])
            residual = add_update(residual, lax.psum(part_sum.astype(jnp.bfloat16), 'tp'), mlp_bd[layer_idx])
        return (residual, jnp.stack(conv_list), jnp.stack(lru_list), k_next, v_next, slot_next)

    return jax.shard_map(local_step, mesh=mesh, in_specs=in_specs, out_specs=out_specs, check_vma=False)
```

profile of v0, /device:TPU:1, one launch (start us, length us, event | category | flops | bytes accessed | tf_op | source)
XLA Modules:
  0.0 615.7 jit_solution(17779056859320283634)
XLA Ops:
  7.3 0.9 slice_convert_fusion.8
  8.5 0.7 broadcast_compare_fusion.1
  9.2 0.8 broadcast_compare_fusion
  10.0 1.5 convert_add_fusion.6
  11.5 2.1 fusion.61
  13.6 0.8 convert_reduce_fusion.9
  14.4 2.9 multiply_reduce_fusion
  17.4 5.3 add_convert_fusion.1
  23.6 1.7 fusion.228
  25.2 12.4 %fusion.46 = bf16[256,4096]{1,0:T(8,128)(2,1)} fusion(bf16[2,704,4096]{2,1,0:T(8,128)(2,1)} %param.51, f32[256,704]{0,1:T(8,128)} %fusion.228, bf16[2,4096,704]{1,2,0:T(8,128)(2,1)} %param.42, bf16[256,4096]{1,0:T(8,128)(2,1)S(1)} %copy-done.5, f32[4096]{0:T(1024)S(1)} %bitcast.292, f32[256]{0:T(256)S(1)} %add_rsqrt_fusion.5, f32[704]{0:T(1024)S(1)} %get-tuple-element.17), kind=kOutput, calls=%fused_computation.66 | convolution fusion | flops 2960015360 | bytes 16469760 | tf_op jit(solution)/shard_map/dot_general | solution.py:63
  39.2 49.5 %all-reduce.7.cloned.1.call-done = bf16[256,4096]{1,0:T(8,128)(2,1)} async-done(((bf16[256,4096]{1,0:T(8,128)(2,1)}), bf16[256,4096]{1,0:T(8,128)(2,1)}) %all-reduce.7.cloned.1.call-update) | async-done | bytes 2097168 | tf_op jit(solution)/shard_map/psum | solution.py:130
  88.6 2.7 fusion.66
  91.4 7.5 %fusion.139 = f32[256,1536]{1,0:T(8,128)S(1)} fusion(bf16[3,4096,1536]{2,1,0:T(8,128)(2,1)} %param.58, f32[1536]{0:T(1024)S(1)} %get-tuple-element.12, bf16[256,4096]{1,0:T(8,128)(2,1)S(1)} %get-tuple-element.37, f32[4096]{0:T(1024)S(1)} %bitcast.289, f32[256]{0:T(256)S(1)} %add_rsqrt_fusion.4), kind=kOutput, calls=%fused_computation.135 | convolution fusion | flops 3228958720 | bytes 16276480 | tf_op jit(solution)/shard_map/dot_general | solution.py:35
  98.9 16.2 %fusion.52 = bf16[256,4096]{1,0:T(8,128)(2,1)} fusion(bf16[3,1536,4096]{2,1,0:T(8,128)(2,1)} %param.62, f32[256,1536]{1,0:T(8,128)S(1)} %fusion.139, bf16[3,4096,1536]{2,1,0:T(8,128)(2,1)} %param.60, f32[1536]{0:T(1024)S(1)} %get-tuple-element.9, bf16[256,4096]{1,0:T(8,128)(2,1)} %copy-done.7, f32[4096]{0:T(1024)S(1)} %bitcast.290, f32[256]{0:T(256)S(1)} %add_rsqrt_fusion.4), kind=kOutput, calls=%fused_computation.68 | convolution fusion | flops 6448873472 | bytes 30956544 | tf_op jit(solution)/shard_map/dot_general | solution.py:38
  115.6 0.6 slice_convert_fusion.2
  116.2 48.3 %all-reduce.9.cloned.1.call-done = bf16[256,4096]{1,0:T(8,128)(2,1)} async-done(((bf16[256,4096]{1,0:T(8,128)(2,1)}), bf16[256,4096]{1,0:T(8,128)(2,1)}) %all-reduce.9.cloned.1.call-update) | async-done | bytes 2097168 | tf_op jit(solution)/shard_map/psum | solution.py:133
  164.6 3.3 fusion.71
  168.0 5.5 add_convert_fusion
  174.1 1.7 fusion.215
  175.8 12.4 %fusion.49 = bf16[256,4096]{1,0:T(8,128)(2,1)} fusion(bf16[2,704,4096]{2,1,0:T(8,128)(2,1)} %param.51, f32[256,704]{0,1:T(8,128)} %fusion.215, bf16[2,4096,704]{1,2,0:T(8,128)(2,1)} %param.42, bf16[256,4096]{1,0:T(8,128)(2,1)S(1)} %get-tuple-element.35, f32[4096]{0:T(1024)S(1)} %bitcast.288, f32[256]{0:T(256)S(1)} %add_rsqrt_fusion.3, ...), kind=kOutput, calls=%fused_computation.67 | convolution fusion | flops 2960015360 | bytes 16469760 | tf_op jit(solution)/shard_map/dot_general | solution.py:63
  188.4 49.2 %all-reduce.11.cloned.1.call-done = bf16[256,4096]{1,0:T(8,128)(2,1)} async-done(((bf16[256,4096]{1,0:T(8,128)(2,1)}), bf16[256,4096]{1,0:T(8,128)(2,1)}) %all-reduce.11.cloned.1.call-update) | async-done | bytes 2097168 | tf_op jit(solution)/shard_map/psum | solution.py:130
  237.6 2.7 fusion.76
  240.3 10.2 %fusion.148 = f32[256,1536]{1,0:T(8,128)} fusion(bf16[3,4096,1536]{2,1,0:T(8,128)(2,1)} %param.58, f32[1536]{0:T(1024)S(1)} %get-tuple-element.13, bf16[256,4096]{1,0:T(8,128)(2,1)S(1)} %get-tuple-element.33, f32[4096]{0:T(1024)S(1)} %bitcast.285, f32[256]{0:T(256)S(1)} %add_rsqrt_fusion.2), kind=kOutput, calls=%fused_computation.142 | convolution fusion | flops 3228958720 | bytes 16276480 | tf_op jit(solution)/shard_map/dot_general | solution.py:35
  250.5 16.7 %fusion.55 = bf16[256,4096]{1,0:T(8,128)(2,1)} fusion(bf16[3,1536,4096]{2,1,0:T(8,128)(2,1)} %param.62, f32[256,1536]{1,0:T(8,128)} %fusion.148, bf16[3,4096,1536]{2,1,0:T(8,128)(2,1)} %param.60, f32[1536]{0:T(1024)S(1)} %get-tuple-element.10, bf16[256,4096]{1,0:T(8,128)(2,1)} %copy-done.6, f32[4096]{0:T(1024)S(1)} %bitcast.286, f32[256]{0:T(256)S(1)} %add_rsqrt_fusion.2), kind=kOutput, calls=%fused_computation.69 | convolution fusion | flops 6448873472 | bytes 30956544 | tf_op jit(solution)/shard_map/dot_general | solution.py:38
  267.4 1.5 compare_and_fusion
  268.9 47.8 %all-reduce.13.cloned.1.call-done = bf16[256,4096]{1,0:T(8,128)(2,1)} async-done(((bf16[256,4096]{1,0:T(8,128)(2,1)}), bf16[256,4096]{1,0:T(8,128)(2,1)}) %all-reduce.13.cloned.1.call-update) | async-done | bytes 2097168 | tf_op jit(solution)/shard_map/psum | solution.py:133
  316.7 3.4 fusion.81
  320.2 1.4 convolution_convert_fusion.1
  321.6 1.0 fusion.307
  322.8 0.7 copy.44
  323.5 4.3 fusion.309
  327.8 1.2 reshape.296
  329.2 0.8 copy.43
  329.9 0.9 slice.491
  330.8 2.1 subtract_convert_fusion
  332.9 88.4 %broadcast_select_fusion.1 = (bf16[256,1024,128]{2,1,0:T(8,128)(2,1)}, bf16[256,1024,128]{2,1,0:T(8,128)(2,1)}) fusion(bf16[256,1024,128]{2,1,0:T(8,128)(2,1)} %param.36, pred[256,1024]{1,0:T(8,128)(4,1)S(1)} %copy-done.12, bf16[256,128]{1,0:T(8,128)(2,1)} %copy.44, bf16[256,1024,128]{2,1,0:T(8,128)(2,1)} %param.37, bf16[256,128]{1,0:T(8,128)(2,1)} %convolution_convert_fusion.1), kind=kLoop, calls=%fused_computation.2 | loop fusion | flops 67108864 | bytes 268828672 | tf_op jit(solution)/shard_map/jit(_where)/select_n | solution.py:82
  421.4 27.8 %fusion.317 = (f32[256,4]{1,0:T(8,128)S(1)}, f32[256,4,1024]{2,1,0:T(4,128)}) fusion(pred[256,1024]{1,0:T(8,128)(4,1)S(1)} %get-tuple-element.28, bf16[256,1024,128]{2,1,0:T(8,128)(2,1)} %get-tuple-element.42, bf16[256,4,64]{2,1,0:T(4,128)(2,1)S(1)} %copy-done.14, bf16[256,4,32]{2,1,0:T(4,128)(2,1)S(1)} %copy-done.13, ...), kind=kOutput, calls=%fused_computation.326 | convolution fusion | flops 273417216 | bytes 71831552 | tf_op jit(solution)/shard_map/sub | solution.py:96
  449.2 24.2 %fusion.178 = bf16[256,4,128]{2,1,0:T(4,128)(2,1)S(1)} fusion(bf16[256,1024,128]{2,1,0:T(8,128)(2,1)} %get-tuple-element.43, f32[256,4,1024]{2,1,0:T(4,128)} %get-tuple-element.71, f32[256,4]{1,0:T(8,128)S(1)} %get-tuple-element.70), kind=kOutput, calls=%fused_computation.157 | convolution fusion | flops 270663680 | bytes 71569408 | tf_op jit(solution)/shard_map/bhs,bsd->bhd/dot_general | solution.py:97
  473.5 2.6 convolution_convert_fusion
  476.2 49.4 %all-reduce.15.cloned.1.call-done = bf16[256,4096]{1,0:T(8,128)(2,1)} async-done(((bf16[256,4096]{1,0:T(8,128)(2,1)}), bf16[256,4096]{1,0:T(8,128)(2,1)}) %all-reduce.15.cloned.1.call-update) | async-done | bytes 2097168 | tf_op jit(solution)/shard_map/psum | solution.py:130
  525.5 2.7 fusion.86
  528.3 10.2 %fusion.157 = f32[256,1536]{1,0:T(8,128)} fusion(bf16[3,4096,1536]{2,1,0:T(8,128)(2,1)} %param.58, f32[1536]{0:T(1024)S(1)} %copy-done.33, bf16[256,4096]{1,0:T(8,128)(2,1)S(1)} %get-tuple-element.27, f32[4096]{0:T(1024)S(1)} %bitcast.280, f32[256]{0:T(256)S(1)} %add_rsqrt_fusion), kind=kOutput, calls=%fused_computation.149 | convolution fusion | flops 3228958720 | bytes 16276480 | tf_op jit(solution)/shard_map/dot_general | solution.py:35
  538.4 16.8 %fusion.58 = bf16[256,4096]{1,0:T(8,128)(2,1)} fusion(bf16[3,1536,4096]{2,1,0:T(8,128)(2,1)} %param.62, f32[256,1536]{1,0:T(8,128)} %fusion.157, bf16[3,4096,1536]{2,1,0:T(8,128)(2,1)} %param.60, f32[1536]{0:T(1024)S(1)} %copy-done.34, bf16[256,4096]{1,0:T(8,128)(2,1)} %copy-done.3, f32[4096]{0:T(1024)S(1)} %bitcast.281, f32[256]{0:T(256)S(1)} %add_rsqrt_fusion), kind=kOutput, calls=%fused_computation.70 | convolution fusion | flops 6448873472 | bytes 30956544 | tf_op jit(solution)/shard_map/dot_general | solution.py:38
  555.6 0.7 copy-done.20
  556.9 1.2 pad_maximum_fusion.1
  558.1 1.5 pad_maximum_fusion
  559.6 45.1 %all-reduce.17.cloned.1.call-done = bf16[256,4096]{1,0:T(8,128)(2,1)} async-done(((bf16[256,4096]{1,0:T(8,128)(2,1)}), bf16[256,4096]{1,0:T(8,128)(2,1)}) %all-reduce.17.cloned.1.call-update) | async-done | bytes 2097168 | tf_op jit(solution)/shard_map/psum | solution.py:133
  604.8 3.7 fusion.90
  (121 shorter events, 5.7 us)
Async XLA Ops:
  7.2 313.0 %copy-start = (bf16[4096,128]{1,0:T(8,128)(2,1)S(1)}, bf16[4096,128]{1,0:T(8,128)(2,1)}, u32[]{:S(2)}) copy-start(bf16[4096,128]{1,0:T(8,128)(2,1)} %param.55) | copy-start | bytes 3145732
  7.2 10.1 %copy-start.5 = (bf16[256,4096]{1,0:T(8,128)(2,1)S(1)}, bf16[256,4096]{1,0:T(8,128)(2,1)}, u32[]{:S(2)}) copy-start(bf16[256,4096]{1,0:T(8,128)(2,1)} %param.32) | copy-start | bytes 6291460
  7.2 81.5 %all-reduce.7.cloned.1.call-start = ((), (), s32[]{:S(2)}) async-start(), calls=%async_computation | async-start | bytes 4194304 | tf_op jit(solution)/shard_map/psum | solution.py:130
  17.3 5.4 copy-start.16
  17.3 5.7 copy-start.18
  17.3 6.1 copy-start.35
  17.3 6.1 copy-start.28
  17.3 6.2 %copy-start.29 = (bf16[2,704]{1,0:T(2,128)(2,1)S(1)}, bf16[2,704]{1,0:T(2,128)(2,1)}, u32[]{:S(2)}) copy-start(bf16[2,704]{1,0:T(2,128)(2,1)} %param.49) | copy-start | bytes 8452
  17.3 6.2 %copy-start.30 = (bf16[2,704]{1,0:T(2,128)(2,1)S(1)}, bf16[2,704]{1,0:T(2,128)(2,1)}, u32[]{:S(2)}) copy-start(bf16[2,704]{1,0:T(2,128)(2,1)} %param.47) | copy-start | bytes 8452
  17.4 6.2 %copy-start.10 = (f32[2,256,704]{1,2,0:T(8,128)S(1)}, f32[2,256,704]{1,2,0:T(8,128)}, u32[]{:S(2)}) copy-start(f32[2,256,704]{1,2,0:T(8,128)} %param.35) | copy-start | bytes 4325380
  25.2 12.7 %copy-start.25 = (bf16[3,1536]{1,0:T(4,128)(2,1)S(1)}, bf16[3,1536]{1,0:T(4,128)(2,1)}, u32[]{:S(2)}) copy-start(bf16[3,1536]{1,0:T(4,128)(2,1)} %param.59) | copy-start | bytes 27652
  25.2 13.3 %copy-start.26 = (bf16[3,1536]{1,0:T(4,128)(2,1)S(1)}, bf16[3,1536]{1,0:T(4,128)(2,1)}, u32[]{:S(2)}) copy-start(bf16[3,1536]{1,0:T(4,128)(2,1)} %param.61) | copy-start | bytes 27652
  25.2 13.9 %copy-start.24 = (bf16[2,4096]{1,0:T(2,128)(2,1)S(1)}, bf16[2,4096]{1,0:T(2,128)(2,1)}, u32[]{:S(2)}) copy-start(bf16[2,4096]{1,0:T(2,128)(2,1)} %param.52) | copy-start | bytes 49156
  37.6 126.9 %all-reduce.9.cloned.1.call-start = ((), (), s32[]{:S(2)}) async-start(), calls=%async_computation.1 | async-start | bytes 4194304 | tf_op jit(solution)/shard_map/psum | solution.py:133
  91.3 7.6 %copy-start.7 = (bf16[256,4096]{1,0:T(8,128)(2,1)}, bf16[256,4096]{1,0:T(8,128)(2,1)S(1)}, u32[]{:S(2)}) copy-start(bf16[256,4096]{1,0:T(8,128)(2,1)S(1)} %get-tuple-element.37) | copy-start | bytes 6291460
  98.9 16.7 %copy-start.22 = (bf16[3,4096]{1,0:T(4,128)(2,1)S(1)}, bf16[3,4096]{1,0:T(4,128)(2,1)}, u32[]{:S(2)}) copy-start(bf16[3,4096]{1,0:T(4,128)(2,1)} %param.63) | copy-start | bytes 73732
  115.1 122.5 %all-reduce.11.cloned.1.call-start = ((), (), s32[]{:S(2)}) async-start(), calls=%async_computation.2 | async-start | bytes 4194304 | tf_op jit(solution)/shard_map/psum | solution.py:130
  167.9 5.5 copy-start.17
  167.9 5.8 copy-start.19
  167.9 6.2 %copy-start.11 = (f32[2,256,704]{1,2,0:T(8,128)S(1)}, f32[2,256,704]{1,2,0:T(8,128)}, u32[]{:S(2)}) copy-start(f32[2,256,704]{1,2,0:T(8,128)} %param.35) | copy-start | bytes 4325380
  188.2 128.6 %all-reduce.13.cloned.1.call-start = ((), (), s32[]{:S(2)}) async-start(), calls=%async_computation.3 | async-start | bytes 4194304 | tf_op jit(solution)/shard_map/psum | solution.py:133
  240.3 10.2 %copy-start.6 = (bf16[256,4096]{1,0:T(8,128)(2,1)}, bf16[256,4096]{1,0:T(8,128)(2,1)S(1)}, u32[]{:S(2)}) copy-start(bf16[256,4096]{1,0:T(8,128)(2,1)S(1)} %get-tuple-element.33) | copy-start | bytes 6291460
  250.5 16.8 %copy-start.31 = (s32[256]{0:T(256)S(1)}, s32[256]{0:T(256)}, u32[]{:S(2)}) copy-start(s32[256]{0:T(256)} %param.33) | copy-start | bytes 3076
  250.5 16.9 %copy-start.15 = (s32[256,1024]{1,0:T(8,128)S(1)}, s32[256,1024]{1,0:T(8,128)}, u32[]{:S(2)}) copy-start(s32[256,1024]{1,0:T(8,128)} %param.38) | copy-start | bytes 3145732
  267.3 258.2 %all-reduce.15.cloned.1.call-start = ((), (), s32[]{:S(2)}) async-start(), calls=%async_computation.4 | async-start | bytes 4194304 | tf_op jit(solution)/shard_map/psum | solution.py:130
  316.7 4.9 copy-start.37
  323.5 9.4 %copy-start.12 = (pred[256,1024]{1,0:T(8,128)(4,1)S(1)}, pred[256,1024]{1,0:T(8,128)(4,1)}, u32[]{:S(2)}) copy-start(pred[256,1024]{1,0:T(8,128)(4,1)} %get-tuple-element.63) | copy-start | bytes 786436
  332.9 88.4 %copy-start.13 = (bf16[256,4,32]{2,1,0:T(4,128)(2,1)S(1)}, bf16[256,4,32]{2,1,0:T(4,128)(2,1)}, u32[]{:S(2)}) copy-start(bf16[256,4,32]{2,1,0:T(4,128)(2,1)} %get-tuple-element.41) | copy-start | bytes 196612
  332.9 88.4 %copy-start.14 = (bf16[256,4,64]{2,1,0:T(4,128)(2,1)S(1)}, bf16[256,4,64]{2,1,0:T(4,128)(2,1)}, u32[]{:S(2)}) copy-start(bf16[256,4,64]{2,1,0:T(4,128)(2,1)} %slice.491) | copy-start | bytes 393220
  449.2 24.3 %copy-start.36 = (bf16[512,4096]{1,0:T(8,128)(2,1)S(1)}, bf16[512,4096]{1,0:T(8,128)(2,1)}, u32[]{:S(2)}) copy-start(bf16[512,4096]{1,0:T(8,128)(2,1)} %param.56) | copy-start | bytes 12582916
  473.4 2.7 copy-start.32
  476.1 52.2 %copy-start.27 = (f32[1,1,4096]{2,1,0:T(1,128)S(1)}, f32[1,1,4096]{2,1,0:T(1,128)}, u32[]{:S(2)}) copy-start(f32[1,1,4096]{2,1,0:T(1,128)} %get-tuple-element.46) | copy-start | bytes 49156
  476.1 52.2 %copy-start.33 = (f32[1536]{0:T(1024)S(1)}, f32[1536]{0:T(1024)}, u32[]{:S(2)}) copy-start(f32[1536]{0:T(1024)} %get-tuple-element.11) | copy-start | bytes 18436
  476.1 128.7 %all-reduce.17.cloned.1.call-start = ((), (), s32[]{:S(2)}) async-start(), calls=%async_computation.5 | async-start | bytes 4194304 | tf_op jit(solution)/shard_map/psum | solution.py:133
  528.2 10.2 %copy-start.3 = (bf16[256,4096]{1,0:T(8,128)(2,1)}, bf16[256,4096]{1,0:T(8,128)(2,1)S(1)}, u32[]{:S(2)}) copy-start(bf16[256,4096]{1,0:T(8,128)(2,1)S(1)} %get-tuple-element.27) | copy-start | bytes 6291460
  528.3 10.2 %copy-start.34 = (f32[1536]{0:T(1024)S(1)}, f32[1536]{0:T(1024)}, u32[]{:S(2)}) copy-start(f32[1536]{0:T(1024)} %get-tuple-element.8) | copy-start | bytes 18436
  538.4 16.9 %copy-start.2 = (bf16[2,256,3,704]{1,3,2,0:T(8,128)(2,1)S(1)}, bf16[2,256,3,704]{1,3,2,0:T(8,128)(2,1)}, u32[]{:S(2)}) copy-start(bf16[2,256,3,704]{1,3,2,0:T(8,128)(2,1)} %param.34) | copy-start | bytes 6488068
  555.3 1.0 copy-start.20
  555.3 1.1 copy-start.21
  555.5 1.2 copy-start.8
  555.5 1.4 copy-start.9
  556.4 48.3 %copy-start.4 = (bf16[256,4096]{1,0:T(8,128)(2,1)S(1)}, bf16[256,4096]{1,0:T(8,128)(2,1)}, u32[]{:S(2)}) copy-start(bf16[256,4096]{1,0:T(8,128)(2,1)} %copy-done.3) | copy-start | bytes 6291460
  556.4 48.3 %copy-start.23 = (f32[1,4096]{1,0:T(1,128)S(1)}, f32[1,4096]{1,0:T(1,128)}, u32[]{:S(2)}) copy-start(f32[1,4096]{1,0:T(1,128)} %get-tuple-element.52) | copy-start | bytes 49156
  558.1 50.3 %copy-start.1 = (bf16[4096,128]{1,0:T(8,128)(2,1)S(1)}, bf16[4096,128]{1,0:T(8,128)(2,1)}, u32[]{:S(2)}) copy-start(bf16[4096,128]{1,0:T(8,128)(2,1)} %param.55) | copy-start | bytes 3145732
Sparse Core Ops, SparseCore 0:
  37.8 50.8 all-reduce.6
  115.2 49.2 all-reduce.8
  188.3 49.2 all-reduce.10
  267.4 49.2 all-reduce.12
  476.2 49.2 all-reduce.14
  555.4 49.2 all-reduce.16
where the time goes:
time: 625 us; the launch traced here: 616 us
  waiting for transfers between devices  289 us (46%)
  matrix products  176 us (28%)
  other arithmetic  129 us (21%)
  between operations  15.1 us (2%)
    psum x6, waiting for transfers between devices, local_step(): lax.psum(part_sum.astype(jnp.bfloat16), 'tp')  289 us
    select_n x1, other arithmetic, write_cache(): k_next = jnp.where(target[:, :, None], k_new[:, None, :], k_cache)  88.4 us
    dot_general x3, matrix products, mlp_update(): return jnp.dot(hidden, w_down, preferred_element_type=jnp.float32)  49.8 us
    dot_general x3, matrix products, mlp_update(): jnp.dot(normed, w_up, preferred_element_type=jnp.float32)  27.9 us
    sub x1, matrix products, attend(): probs_bf = jax.nn.softmax(scores, axis=-1).astype(jnp.bfloat16)  27.8 us
    dot_general x2, matrix products, recurrent_update(): update = jnp.dot(gated_h, rec_wout, preferred_element_type=jnp.float32)  24.7 us
    dot_general x1, matrix products, attend(): jnp.einsum('bhs,bsd->bhd', probs_bf, v_next, preferred_element_type=jnp.f...  24.2 us
    reduce_sum x6, other arithmetic, rms_norm(): mean_sq = jnp.mean(res_f * res_f, axis=-1, keepdims=True)  16.9 us
  transfers between devices with their start and end apart: 6, of which 6 were waited for; matrix products, arithmetic and copies ran while one was open for 1% of the time, Pallas kernels for 0%

commit v1 on v0

v1 whole, which is shorter than its diff:
```python
import functools

import jax
import jax.numpy as jnp
from jax import lax
from jax.experimental import pallas as pl
from jax.experimental.pallas import tpu as pltpu
from jax.sharding import PartitionSpec as P

ROPE_BASE = 10000.0
NORM_EPS = 1e-6
MESH = pl.DeviceIdType.MESH
BF = jnp.bfloat16
F32 = jnp.float32
ANY = pl.BlockSpec(memory_space=pl.ANY)
VM = pl.BlockSpec(memory_space=pltpu.VMEM)
B = 256
D = 4096
LC = 704
FC = 1536
W = 1024
HD = 128
G = 4
GC = D // G


def rms(x, scale):
    xf = x.astype(F32)
    mean_sq = jnp.mean(xf * xf, axis=-1, keepdims=True)
    return (xf * lax.rsqrt(mean_sq + NORM_EPS) * (1.0 + scale.astype(F32))).astype(BF)


def norm_into(n_s, x_ref, scale):
    for r in range(0, B, 32):
        n_s[r:r + 32, :] = rms(x_ref[r:r + 32, :], scale)


def ar_kernel(layer, part_ref, x_ref, b_ref, out_ref, xbuf, xown, recv1, send2, recv2, own,
              s1s, s1r, s2s, s2r, s3s, s3r, s4s, s4r, lsem, osem):
    t = lax.axis_index('tp')
    y = t // 4
    x = (t // 2) % 2
    c = t % 2
    q = 2 * y + x
    partner = 2 * q + 1 - c
    chips = [2 * y + (1 - x), 2 * (1 - y) + x, 2 * (1 - y) + (1 - x)]
    peers = [2 * qd + c for qd in chips]
    barrier = pltpu.get_barrier_semaphore()
    for dev in [partner] + peers:
        pl.semaphore_signal(barrier, inc=1, device_id={'tp': dev}, device_id_type=MESH)
    load_x = pltpu.make_async_copy(x_ref.at[q, c], xown, lsem)
    load_x.start()
    pl.semaphore_wait(barrier, 4)

    def remote(src, dst, ss, rs, dev):
        cp = pltpu.make_async_remote_copy(src_ref=src, dst_ref=dst, send_sem=ss, recv_sem=rs, device_id={'tp': dev}, device_id_type=MESH)
        cp.start()
        return cp

    cols = [pl.ds(g * GC, GC) for g in range(G)]
    cp1 = [remote(part_ref.at[:, 1 - c, :, cols[g]], recv1.at[:, :, cols[g]], s1s.at[g], s1r.at[g], partner) for g in range(G)]
    cp2 = []
    for g in range(G):
        cp1[g].wait_recv()
        row = []
        for k in (2, 0, 1):
            s = part_ref[chips[k], c, :, cols[g]].astype(F32) + recv1[chips[k], :, cols[g]].astype(F32)
            send2[k, :, cols[g]] = s.astype(BF)
            row.append((k, remote(send2.at[k, :, cols[g]], recv2.at[k, :, cols[g]], s2s.at[g, k], s2r.at[g, k], peers[k])))
        own[:, cols[g]] = part_ref[q, c, :, cols[g]].astype(F32) + recv1[q, :, cols[g]].astype(F32)
        cp2.append([cp for _, cp in sorted(row, key=lambda e: e[0])])
    load_x.wait()
    cp3 = []
    ocp = []
    for g in range(G):
        for k in range(3):
            cp2[g][k].wait_recv()
        tot = own[:, cols[g]]
        for k in range(3):
            tot = tot + recv2[k, :, cols[g]].astype(F32)
        bias = b_ref[...].astype(F32)[layer:layer + 1, g * GC:(g + 1) * GC]
        xn = (xown[:, cols[g]].astype(F32) + tot.astype(BF).astype(F32) + bias).astype(BF)
        xbuf[q, c, :, cols[g]] = xn
        place = xbuf.at[q, c, :, cols[g]]
        row = {}
        for k in (2, 0, 1):
            row[k] = remote(place, place, s3s.at[g, k], s3r.at[g, k], peers[k])
        row[3] = remote(place, place, s3s.at[g, 3], s3r.at[g, 3], partner)
        cp3.append(row)
    cp4 = []
    for g in range(G):
        for k in range(3):
            cp3[g][k].wait_recv()
            place = xbuf.at[chips[k], c, :, cols[g]]
            cp4.append(remote(place, place, s4s.at[g, k], s4r.at[g, k], partner))
    for g in range(G):
        cp3[g][3].wait_recv()
    for cp in cp4:
        cp.wait_recv()
    store = pltpu.make_async_copy(xbuf, out_ref, osem)
    store.start()
    for g in range(G):
        cp1[g].wait_send()
        for k in range(3):
            cp2[g][k].wait_send()
        for k in range(4):
            cp3[g][k].wait_send()
    for cp in cp4:
        cp.wait_send()
    store.wait()


def all_reduce(part, x, bias, layer, cid):
    out = pl.pallas_call(
        functools.partial(ar_kernel, layer),
        name=f'ar{cid}',
        out_shape=jax.ShapeDtypeStruct((4, 2, 32, D), BF),
        in_specs=[VM, ANY, VM],
        out_specs=ANY,
        scratch_shapes=[
            pltpu.VMEM((4, 2, 32, D), BF), pltpu.VMEM((32, D), BF), pltpu.VMEM((4, 32, D), BF),
            pltpu.VMEM((3, 32, D), BF), pltpu.VMEM((3, 32, D), BF), pltpu.VMEM((32, D), F32),
            pltpu.SemaphoreType.DMA((G,)), pltpu.SemaphoreType.DMA((G,)),
            pltpu.SemaphoreType.DMA((G, 3)), pltpu.SemaphoreType.DMA((G, 3)),
            pltpu.SemaphoreType.DMA((G, 4)), pltpu.SemaphoreType.DMA((G, 4)),
            pltpu.SemaphoreType.DMA((G, 3)), pltpu.SemaphoreType.DMA((G, 3)),
            pltpu.SemaphoreType.DMA, pltpu.SemaphoreType.DMA,
        ],
        compiler_params=pltpu.CompilerParams(collective_id=cid, has_side_effects=True),
        cost_estimate=pl.CostEstimate(flops=10**9, bytes_accessed=80 * 10**6, transcendentals=0),
    )(part.reshape(4, 2, 32, D), x.reshape(4, 2, 32, D), bias)
    return out.reshape(B, D)


def mlp_kernel(layer, nb, x_ref, sc_ref, w1_ref, b1_ref, w2_ref, b2_ref, wd_ref, out_ref, n_s, h_s):
    i = pl.program_id(0)

    @pl.when(i == 0)
    def _():
        norm_into(n_s, x_ref, sc_ref[...].astype(F32)[layer, 1:2, :])

    @pl.when(i < nb)
    def _():
        n = n_s[...]
        lanes = pl.ds(pl.multiple_of(i * 256, 256), 256)
        g = jnp.dot(n, w1_ref[0], preferred_element_type=F32) + b1_ref[:, lanes].astype(F32)[layer:layer + 1]
        u = jnp.dot(n, w2_ref[0], preferred_element_type=F32) + b2_ref[:, lanes].astype(F32)[layer:layer + 1]
        h_s[:, lanes] = (jax.nn.gelu(g, approximate=True) * u).astype(BF)

    @pl.when(i >= nb)
    def _():
        out_ref[...] = jnp.dot(h_s[...], wd_ref[0], preferred_element_type=F32).astype(BF)


def mlp(x, scale, w1, b1, w2, b2, wd, layer):
    nb = FC // 256
    nd = D // 512
    up = pl.BlockSpec((1, D, 256), lambda i: (layer, 0, jnp.minimum(i, nb - 1)))
    return pl.pallas_call(
        functools.partial(mlp_kernel, layer, nb),
        name=f'mlp{layer}',
        grid=(nb + nd,),
        out_shape=jax.ShapeDtypeStruct((B, D), BF),
        in_specs=[pl.BlockSpec((B, D), lambda i: (0, 0)), pl.BlockSpec(scale.shape, lambda i: (0, 0, 0)),
                  up, pl.BlockSpec(b1.shape, lambda i: (0, 0)), up, pl.BlockSpec(b2.shape, lambda i: (0, 0)),
                  pl.BlockSpec((1, FC, 512), lambda i: (layer, 0, jnp.maximum(i - nb, 0)))],
        out_specs=pl.BlockSpec((B, 512), lambda i: (0, jnp.maximum(i - nb, 0))),
        scratch_shapes=[pltpu.VMEM((B, D), BF), pltpu.VMEM((B, FC), BF)],
        cost_estimate=pl.CostEstimate(flops=2 * B * D * FC * 3, bytes_accessed=6 * D * FC, transcendentals=0),
    )(x, scale, w1, b1, w2, b2, wd)


RB = 352


def rec_kernel(layer, x_ref, sc_ref, wx_ref, wy_ref, conv_ref, lru_ref, wa_ref, wi_ref, pc_ref, tok_ref, wo_ref,
               out_ref, conv_out, lru_out, n_s, ht_s, hy_s):
    i = pl.program_id(0)
    nb = LC // RB

    @pl.when(i == 0)
    def _():
        norm_into(n_s, x_ref, sc_ref[...].astype(F32)[layer, 0:1, :])

    @pl.when(i < nb)
    def _():
        n = n_s[...]
        nt = (((1,), (1,)), ((), ()))
        pc = pc_ref[0]
        col = lambda k: pc[:, k:k + 1]
        tok = tok_ref[...]
        xb = (lax.dot_general(wx_ref[0], n, nt, preferred_element_type=F32) + col(0)).astype(BF)
        yb = jax.nn.gelu(lax.dot_general(wy_ref[0], n, nt, preferred_element_type=F32) + col(1), approximate=True)
        hist = jnp.zeros((RB, B), F32)
        for j in range(3):
            hj = jnp.where(tok >= 3 - j, conv_ref[0, j].astype(F32), 0.0)
            hist = hist + hj * col(5 - j)
        xc = (col(6) + col(2) * xb.astype(F32) + hist).astype(BF)
        conv_out[0, 0] = conv_ref[0, 1]
        conv_out[0, 1] = conv_ref[0, 2]
        conv_out[0, 2] = xb
        tn = (((0,), (0,)), ((), ()))
        fresh = tok == 0
        for h in range(RB // 176):
            rows = slice(176 * h, 176 * h + 176)
            xh = xc[rows]
            ph = pc[rows]
            rg = jax.nn.sigmoid(lax.dot_general(wa_ref[0, h], xh, tn, preferred_element_type=F32) + ph[:, 7:8])
            ig = jax.nn.sigmoid(lax.dot_general(wi_ref[0, h], xh, tn, preferred_element_type=F32) + ph[:, 8:9])
            a = jnp.exp(rg * ph[:, 9:10])
            sc = jnp.sqrt(1.0 - a * a)
            a = jnp.where(fresh, 0.0, a)
            sc = jnp.where(fresh, 1.0, sc)
            hn = a * lru_ref[0, rows, :] + sc * ig * xh.astype(F32)
            lru_out[0, rows, :] = hn
            ht_s[pl.ds(pl.multiple_of(i * RB, 16) + 176 * h, 176), :] = (hn * yb[rows]).astype(BF)

    @pl.when(i == nb)
    def _():
        ht_s[LC:, :] = jnp.zeros((64, B), BF)
        hy_s[...] = ht_s[...].T

    @pl.when(i >= nb)
    def _():
        out_ref[...] = jnp.dot(hy_s[:, :LC], wo_ref[0], preferred_element_type=F32).astype(BF)


def rec(x, scale, wxt, wyt, convt, lrut, wa, wi, pcols, tok, wout, layer):
    nb = LC // RB
    nd = D // 512
    up = pl.BlockSpec((1, RB, D), lambda i: (layer, jnp.minimum(i, nb - 1), 0))
    gate = pl.BlockSpec((1, RB // 176, 176, 176), lambda i: (layer, jnp.minimum(i, nb - 1), 0, 0))
    return pl.pallas_call(
        functools.partial(rec_kernel, layer),
        name=f'rec{layer}',
        grid=(nb + nd,),
        out_shape=(jax.ShapeDtypeStruct((B, D), BF), jax.ShapeDtypeStruct((1, 3, LC, B), BF), jax.ShapeDtypeStruct((1, LC, B), F32)),
        in_specs=[pl.BlockSpec((B, D), lambda i: (0, 0)), pl.BlockSpec(scale.shape, lambda i: (0, 0, 0)), up, up,
                  pl.BlockSpec((1, 3, RB, B), lambda i: (layer, 0, jnp.minimum(i, nb - 1), 0)),
                  pl.BlockSpec((1, RB, B), lambda i: (layer, jnp.minimum(i, nb - 1), 0)),
                  gate, gate, pl.BlockSpec((1, RB, pcols.shape[2]), lambda i: (layer, jnp.minimum(i, nb - 1), 0)),
                  pl.BlockSpec((1, B), lambda i: (0, 0)),
                  pl.BlockSpec((1, LC, 512), lambda i: (layer, 0, jnp.maximum(i - nb, 0)))],
        out_specs=(pl.BlockSpec((B, 512), lambda i: (0, jnp.maximum(i - nb, 0))),
                   pl.BlockSpec((1, 3, RB, B), lambda i: (0, 0, jnp.minimum(i, nb - 1), 0)),
                   pl.BlockSpec((1, RB, B), lambda i: (0, jnp.minimum(i, nb - 1), 0))),
        scratch_shapes=[pltpu.VMEM((B, D), BF), pltpu.VMEM((LC + 64, B), BF), pltpu.VMEM((B, LC + 64), BF)],
        cost_estimate=pl.CostEstimate(flops=2 * B * D * LC * 3, bytes_accessed=6 * D * LC, transcendentals=0),
    )(x, scale, wxt, wyt, convt, lrut, wa, wi, pcols, tok, wout)


def rope(v, tab_ref):
    return v * tab_ref[0] + pltpu.roll(v, 96, 1) * tab_ref[1] + pltpu.roll(v, 32, 1) * tab_ref[2]


def qkv_kernel(x_ref, sc_ref, wq_ref, wk_ref, wv_ref, tab_ref, q_ref, k_ref, v_ref, n_s):
    i = pl.program_id(0)

    @pl.when(i == 0)
    def _():
        norm_into(n_s, x_ref, sc_ref[...].astype(F32)[2, 0:1, :])

    @pl.when(i < 2)
    def _():
        qf = jnp.dot(n_s[...], wq_ref[...], preferred_element_type=F32)
        for h in range(2):
            q_ref[h] = rope(qf[:, 128 * h:128 * h + 128], tab_ref).astype(BF)

    @pl.when(i == 2)
    def _():
        k_ref[...] = rope(jnp.dot(n_s[...], wk_ref[...], preferred_element_type=F32), tab_ref).astype(BF)
        v_ref[...] = jnp.dot(n_s[...], wv_ref[...], preferred_element_type=F32).astype(BF)


def qkv(x, scale, wq, wk, wv, tab):
    return pl.pallas_call(
        qkv_kernel,
        name='qkv',
        grid=(3,),
        out_shape=(jax.ShapeDtypeStruct((4, B, HD), BF), jax.ShapeDtypeStruct((B, HD), BF), jax.ShapeDtypeStruct((B, HD), BF)),
        in_specs=[pl.BlockSpec((B, D), lambda i: (0, 0)), pl.BlockSpec(scale.shape, lambda i: (0, 0, 0)),
                  pl.BlockSpec((D, 256), lambda i: (0, jnp.minimum(i, 1))),
                  pl.BlockSpec((D, HD), lambda i: (0, 0)), pl.BlockSpec((D, HD), lambda i: (0, 0)),
                  pl.BlockSpec((3, B, HD), lambda i: (0, 0, 0))],
        out_specs=(pl.BlockSpec((2, B, HD), lambda i: (jnp.minimum(i, 1), 0, 0)),
                   pl.BlockSpec((B, HD), lambda i: (0, 0)), pl.BlockSpec((B, HD), lambda i: (0, 0))),
        scratch_shapes=[pltpu.VMEM((B, D), BF)],
        cost_estimate=pl.CostEstimate(flops=2 * B * D * 768, bytes_accessed=2 * D * 768, transcendentals=0),
    )(x, scale, wq, wk, wv, tab)


RA = 8


def attn_kernel(tok_ref, q_ref, kn_ref, vn_ref, slot_ref, k_ref, v_ref, o_ref, ko_ref, vo_ref, so_ref):
    i = pl.program_id(0)
    lane = lax.broadcasted_iota(jnp.int32, (1, W), 1)
    sub = lax.broadcasted_iota(jnp.int32, (16, HD), 0)
    for r in range(RA):
        tp = tok_ref[i * RA + r]
        slot = lax.rem(tp, W)
        base = pl.multiple_of((slot // 16) * 16, 16)
        hit = sub == (slot - base)
        ko_ref[r] = k_ref[r]
        vo_ref[r] = v_ref[r]
        kn = kn_ref[...].astype(F32)[r:r + 1]
        vn = vn_ref[...].astype(F32)[r:r + 1]
        ko_ref[r, pl.ds(base, 16), :] = jnp.where(hit, kn, k_ref[r, pl.ds(base, 16), :].astype(F32)).astype(BF)
        vo_ref[r, pl.ds(base, 16), :] = jnp.where(hit, vn, v_ref[r, pl.ds(base, 16), :].astype(F32)).astype(BF)
        sn = jnp.where(lane == slot, tp, slot_ref[r:r + 1, :])
        so_ref[r:r + 1, :] = sn
        age = tp - sn
        valid = (sn >= 0) & (age >= 0) & (age < W)
        s = lax.dot_general(q_ref[r], ko_ref[r], (((1,), (1,)), ((), ())), preferred_element_type=F32) * (HD ** -0.5)
        s = jnp.where(valid, s, -jnp.inf)
        m = jnp.max(s, axis=-1, keepdims=True)
        e = jnp.exp(s - m)
        p = (e / jnp.sum(e, axis=-1, keepdims=True)).astype(BF)
        o_ref[r] = jnp.dot(p, vo_ref[r], preferred_element_type=F32).astype(BF)


def attend(tok, q, kn, vn, slot_pos, kc, vc):
    cache = pl.BlockSpec((RA, W, HD), lambda i, t: (i, 0, 0))
    row = pl.BlockSpec((RA, HD), lambda i, t: (i, 0))
    slots = pl.BlockSpec((RA, W), lambda i, t: (i, 0))
    heads = pl.BlockSpec((RA, 4, HD), lambda i, t: (i, 0, 0))
    return pl.pallas_call(
        attn_kernel,
        name='attend',
        grid_spec=pltpu.PrefetchScalarGridSpec(
            num_scalar_prefetch=1,
            grid=(B // RA,),
            in_specs=[heads, row, row, slots, cache, cache],
            out_specs=(heads, cache, cache, slots),
        ),
        out_shape=(jax.ShapeDtypeStruct((B, 4, HD), BF), jax.ShapeDtypeStruct(kc.shape, BF), jax.ShapeDtypeStruct(vc.shape, BF), jax.ShapeDtypeStruct(slot_pos.shape, jnp.int32)),
        cost_estimate=pl.CostEstimate(flops=4 * B * 4 * W * HD, bytes_accessed=8 * B * W * HD, transcendentals=0),
    )(tok, q, kn, vn, slot_pos, kc, vc)


def wo_kernel(o_ref, w_ref, out_ref):
    out_ref[...] = jnp.dot(o_ref[...], w_ref[...], preferred_element_type=F32).astype(BF)


def out_proj(o, wo):
    return pl.pallas_call(
        wo_kernel,
        name='wo',
        grid=(D // 1024,),
        out_shape=jax.ShapeDtypeStruct((B, D), BF),
        in_specs=[pl.BlockSpec((B, 512), lambda i: (0, 0)), pl.BlockSpec((512, 1024), lambda i: (0, i))],
        out_specs=pl.BlockSpec((B, 1024), lambda i: (0, i)),
        cost_estimate=pl.CostEstimate(flops=2 * B * D * 512, bytes_accessed=2 * D * 512, transcendentals=0),
    )(o, wo)


def rope_tables(tok_pos):
    quarter = HD // 4
    inv_freq = ROPE_BASE ** (-jnp.arange(quarter, dtype=F32) / quarter)
    angles = tok_pos.astype(F32)[:, None] * inv_freq[None, :]
    cos, sin = jnp.cos(angles), jnp.sin(angles)
    one = jnp.ones_like(cos)
    zero = jnp.zeros_like(cos)
    keep = jnp.concatenate([cos, cos, one, one], axis=1)
    up = jnp.concatenate([-sin, zero, zero, zero], axis=1)
    down = jnp.concatenate([zero, sin, zero, zero], axis=1)
    return jnp.stack([keep, up, down])


def io_specs():
    in_specs = (P('dp', None), P('dp'), P(None, 'dp', None, 'tp'), P(None, 'dp', 'tp'), P('dp', None, None), P('dp', None, None), P('dp', None),
                P(), P(None, None, 'tp'), P(None, 'tp'), P(None, None, 'tp'), P(None, 'tp'), P(None, None, 'tp'), P(None, 'tp'),
                P(None, 'tp', None, None), P(None, 'tp'), P(None, 'tp', None, None), P(None, 'tp'), P(None, 'tp'), P(None, 'tp', None), P(),
                P(None, 'tp'), P(), P(), P('tp', None), P(),
                P(None, None, 'tp'), P(None, 'tp'), P(None, None, 'tp'), P(None, 'tp'), P(None, 'tp', None), P())
    out_specs = (P('dp', None), P(None, 'dp', None, 'tp'), P(None, 'dp', 'tp'), P('dp', None, None), P('dp', None, None), P('dp', None))
    return in_specs, out_specs


def solution(mesh):
    in_specs, out_specs = io_specs()

    def local_step(x_in, tok_pos, conv_state, lru_state, k_cache, v_cache, slot_pos, norm_scale, rec_wx, rec_bx, rec_wy, rec_by, conv_w, conv_b, gate_wa, gate_ba, gate_wi, gate_bi, a_param, rec_wout, rec_bout, attn_wq, attn_wk, attn_wv, attn_wo, attn_bo, mlp_w1, mlp_b1, mlp_w2, mlp_b2, mlp_wd, mlp_bd):
        wxt = jnp.swapaxes(rec_wx, 1, 2)
        wyt = jnp.swapaxes(rec_wy, 1, 2)
        convt = jnp.transpose(conv_state, (0, 2, 3, 1))
        lrut = jnp.swapaxes(lru_state, 1, 2)
        f = lambda v: v.astype(F32)
        pcols = jnp.stack([f(rec_bx), f(rec_by), f(conv_w[:, 0]), f(conv_w[:, 1]), f(conv_w[:, 2]), f(conv_w[:, 3]), f(conv_b), f(gate_ba), f(gate_bi), -8.0 * jax.nn.softplus(a_param)], axis=-1)
        tok_row = tok_pos[None, :]
        tab = rope_tables(tok_pos)

        x = x_in
        convs = []
        lrus = []
        for layer in range(2):
            part, conv_new, lru_new = rec(x, norm_scale, wxt, wyt, convt, lrut, gate_wa, gate_wi, pcols, tok_row, rec_wout, layer)
            convs.append(conv_new)
            lrus.append(lru_new)
            x = all_reduce(part, x, rec_bout, layer, 2 * layer)
            part = mlp(x, norm_scale, mlp_w1, mlp_b1, mlp_w2, mlp_b2, mlp_wd, layer)
            x = all_reduce(part, x, mlp_bd, layer, 2 * layer + 1)
        q, kn, vn = qkv(x, norm_scale, attn_wq, attn_wk, attn_wv, tab)
        o, k_next, v_next, slot_next = attend(tok_pos, jnp.swapaxes(q, 0, 1), kn, vn, slot_pos, k_cache, v_cache)
        part = out_proj(o.reshape(B, 512), attn_wo)
        x = all_reduce(part, x, attn_bo[None, :], 0, 4)
        part = mlp(x, norm_scale, mlp_w1, mlp_b1, mlp_w2, mlp_b2, mlp_wd, 2)
        x = all_reduce(part, x, mlp_bd, 2, 5)
        conv_out = jnp.transpose(jnp.concatenate(convs), (0, 3, 1, 2))
        lru_out = jnp.swapaxes(jnp.concatenate(lrus), 1, 2)
        return (x, conv_out, lru_out, k_next, v_next, slot_next)

    return jax.shard_map(local_step, mesh=mesh, in_specs=in_specs, out_specs=out_specs, check_vma=False)
```

time: 625 us -> 448 us (0.72); the launches traced: 616 us -> 447 us
  Pallas kernels: 0 us -> 426 us
  waiting for transfers between devices: 289 us -> 0 us
  matrix products: 176 us -> 0 us
  other arithmetic: 129 us -> 9.92 us
  between operations: 15.1 us -> 0.79 us
    pallas_call x0 -> x14, Pallas kernels: none -> 426 us  [the longest x6 193 us: all_reduce(): pl.pallas_call(functools.partial(ar_kernel, layer), name=f'ar{cid}', out_...]
    psum x6 -> x0, waiting for transfers between devices: 289 us -> none  [local_step(): lax.psum(part_sum.astype(jnp.bfloat16), 'tp')]
    dot_general x19 -> x0, matrix products: 148 us -> none  [the longest x3 49.8 us: mlp_update(): return jnp.dot(hidden, w_down, preferred_element_type=jnp.float32)]
    select_n x1 -> x0, other arithmetic: 88.4 us -> none  [write_cache(): k_next = jnp.where(target[:, :, None], k_new[:, None, :], k_cache)]
    sub x1 -> x0, matrix products: 27.8 us -> none  [attend(): probs_bf = jax.nn.softmax(scores, axis=-1).astype(jnp.bfloat16)]
    reduce_sum x7 -> x0, other arithmetic: 19.8 us -> none  [the longest x6 16.9 us: rms_norm(): mean_sq = jnp.mean(res_f * res_f, axis=-1, keepdims=True)]
    add x11 -> x0, other arithmetic: 7.61 us -> none  [the longest x2 3.32 us: recurrent_update(): decay_gate * lru_prev]
  transfers between devices with their start and end apart: 6 -> 0, of which waited for: 6 -> 0; matrix products, arithmetic and copies ran while one was open for 1% -> 0% of each run, Pallas kernels for 0% -> 0%
where the time goes in v1:
time: 448 us; the launch traced here: 447 us
  Pallas kernels  426 us (95%)
  local copies, waits for them, and re-layouts  10.2 us (2%)
  other arithmetic  9.92 us (2%)
    pallas_call x6, Pallas kernels, all_reduce(): pl.pallas_call(functools.partial(ar_kernel, layer), name=f'ar{cid}', out_...  193 us
    pallas_call x1, Pallas kernels, attend(): pl.pallas_call(attn_kernel, name='attend', grid_spec=pltpu.PrefetchScalar...  111 us
    pallas_call x3, Pallas kernels, mlp(): pl.pallas_call(functools.partial(mlp_kernel, layer, nb), name=f'mlp{layer...  73.7 us
    pallas_call x2, Pallas kernels, rec(): pl.pallas_call(functools.partial(rec_kernel, layer), name=f'rec{layer}',...  34.3 us

profile of v1, /device:TPU:1, one launch (start us, length us, event | category | flops | bytes accessed | tf_op | source)
XLA Modules:
  0.0 446.6 jit_solution(14686203154045540717)
XLA Ops:
  0.6 0.1 pad.10.clone
  0.7 0.1 pad.13.clone
  0.8 0.7 convert_element_type.68
  1.5 1.3 broadcast_in_dim.13.b_ref
  2.8 0.9 slice_convert_fusion
  3.7 0.7 constant_dynamic-update-slice_fusion.9
  4.4 0.7 constant_dynamic-update-slice_fusion.8
  5.1 0.7 constant_dynamic-update-slice_fusion.3
  5.8 0.7 constant_dynamic-update-slice_fusion.2
  6.5 0.7 constant_dynamic-update-slice_fusion.1
  7.2 0.7 constant_dynamic-update-slice_fusion
  7.9 0.5 multiply_cosine_fusion
  8.5 0.1 maximum_bitcast_fusion.2
  8.6 0.8 pad_maximum_fusion.tab_ref
  9.4 1.1 copy.54.pc_ref
  10.5 17.1 %rec0.1 = (bf16[256,4096]{1,0:T(8,128)(2,1)}, bf16[1,3,704,256]{3,2,1,0:T(8,128)(2,1)}, f32[1,704,256]{2,1,0:T(8,128)}) custom-call(bf16[256,4096]{1,0:T(8,128)(2,1)} %x_ref.1, bf16[3,2,4096]{2,1,0:T(2,128)(2,1)} %sc_ref.11, bf16[2,704,4096]{2,1,0:T(8,128)(2,1)} %bitcast.62, bf16[2,704,4096]{2,1,0:T(8,128)(2,1)} %bitcast.64, ...), custom_call_target="tpu_custom_call" | custom-call | flops 4429185024 | bytes 17301504 | tf_op jit(solution)/shard_map/rec0/pallas_call | solution.py:233
  27.7 33.4 %ar0.1.x_ref = bf16[4,2,32,4096]{3,2,1,0:T(8,128)(2,1)} custom-call(bf16[4,2,32,4096]{3,2,1,0:T(8,128)(2,1)} %bitcast.82, bf16[4,2,32,4096]{3,2,1,0:T(8,128)(2,1)} %bitcast.76, bf16[2,4096]{1,0:T(2,128)(2,1)} %b_ref.7), custom_call_target="tpu_custom_call" | custom-call | flops 1000000000 | bytes 80000000 | tf_op jit(solution)/shard_map/ar0/pallas_call | solution.py:114
  61.1 24.5 %mlp0.1 = bf16[256,4096]{1,0:T(8,128)(2,1)} custom-call(bf16[256,4096]{1,0:T(8,128)(2,1)} %bitcast.68, bf16[3,2,4096]{2,1,0:T(2,128)(2,1)} %sc_ref.11, bf16[3,4096,1536]{2,1,0:T(8,128)(2,1)} %w1_ref.5, bf16[3,1536]{1,0:T(4,128)(2,1)} %b1_ref.5, bf16[3,4096,1536]{2,1,0:T(8,128)(2,1)} %w2_ref.5, bf16[3,1536]{1,0:T(4,128)(2,1)} %b2_ref.5, ...), custom_call_target="tpu_custom_call" | custom-call | flops 9663676416 | bytes 37748736 | tf_op jit(solution)/shard_map/mlp0/pallas_call | solution.py:159
  85.6 32.6 %ar1.1.x_ref = bf16[4,2,32,4096]{3,2,1,0:T(8,128)(2,1)} custom-call(bf16[4,2,32,4096]{3,2,1,0:T(8,128)(2,1)} %bitcast.73, bf16[4,2,32,4096]{3,2,1,0:T(8,128)(2,1)} %ar0.1.x_ref, bf16[3,4096]{1,0:T(4,128)(2,1)} %b_ref.9), custom_call_target="tpu_custom_call" | custom-call | flops 1000000000 | bytes 80000000 | tf_op jit(solution)/shard_map/ar1/pallas_call | solution.py:114
  118.3 17.2 %rec1.1 = (bf16[256,4096]{1,0:T(8,128)(2,1)}, bf16[1,3,704,256]{3,2,1,0:T(8,128)(2,1)}, f32[1,704,256]{2,1,0:T(8,128)}) custom-call(bf16[256,4096]{1,0:T(8,128)(2,1)} %bitcast.69, bf16[3,2,4096]{2,1,0:T(2,128)(2,1)} %sc_ref.11, bf16[2,704,4096]{2,1,0:T(8,128)(2,1)} %bitcast.63, bf16[2,704,4096]{2,1,0:T(8,128)(2,1)} %bitcast.65, ...), custom_call_target="tpu_custom_call" | custom-call | flops 4429185024 | bytes 17301504 | tf_op jit(solution)/shard_map/rec1/pallas_call | solution.py:233
  135.5 0.0 copy-start.2
  135.5 0.0 copy-start.3
  135.5 31.5 %ar2.1.x_ref = bf16[4,2,32,4096]{3,2,1,0:T(8,128)(2,1)} custom-call(bf16[4,2,32,4096]{3,2,1,0:T(8,128)(2,1)} %bitcast.81, bf16[4,2,32,4096]{3,2,1,0:T(8,128)(2,1)} %ar1.1.x_ref, bf16[2,4096]{1,0:T(2,128)(2,1)} %b_ref.7), custom_call_target="tpu_custom_call" | custom-call | flops 1000000000 | bytes 80000000 | tf_op jit(solution)/shard_map/ar2/pallas_call | solution.py:114
  167.0 0.0 copy-start
  167.0 0.0 copy-start.1
  167.0 0.0 copy-done.2
  167.1 0.0 copy-done.3
  167.1 1.2 maximum_bitcast_fusion.1
  168.3 0.4 copy-done
  168.7 0.4 copy-done.1
  169.1 1.5 maximum_bitcast_fusion
  170.6 24.5 %mlp1.1 = bf16[256,4096]{1,0:T(8,128)(2,1)} custom-call(bf16[256,4096]{1,0:T(8,128)(2,1)} %bitcast.66, bf16[3,2,4096]{2,1,0:T(2,128)(2,1)} %sc_ref.11, bf16[3,4096,1536]{2,1,0:T(8,128)(2,1)} %w1_ref.5, bf16[3,1536]{1,0:T(4,128)(2,1)} %b1_ref.5, bf16[3,4096,1536]{2,1,0:T(8,128)(2,1)} %w2_ref.5, bf16[3,1536]{1,0:T(4,128)(2,1)} %b2_ref.5, ...), custom_call_target="tpu_custom_call" | custom-call | flops 9663676416 | bytes 37748736 | tf_op jit(solution)/shard_map/mlp1/pallas_call | solution.py:159
  195.1 32.2 %ar3.1.x_ref = bf16[4,2,32,4096]{3,2,1,0:T(8,128)(2,1)} custom-call(bf16[4,2,32,4096]{3,2,1,0:T(8,128)(2,1)} %bitcast.74, bf16[4,2,32,4096]{3,2,1,0:T(8,128)(2,1)} %ar2.1.x_ref, bf16[3,4096]{1,0:T(4,128)(2,1)} %b_ref.9), custom_call_target="tpu_custom_call" | custom-call | flops 1000000000 | bytes 80000000 | tf_op jit(solution)/shard_map/ar3/pallas_call | solution.py:114
  227.4 7.7 %qkv.1 = (bf16[4,256,128]{2,1,0:T(8,128)(2,1)}, bf16[256,128]{1,0:T(8,128)(2,1)}, bf16[256,128]{1,0:T(8,128)(2,1)}) custom-call(bf16[256,4096]{1,0:T(8,128)(2,1)} %bitcast.70, bf16[3,2,4096]{2,1,0:T(2,128)(2,1)} %sc_ref.11, bf16[4096,512]{1,0:T(8,128)(2,1)} %wq_ref.1, bf16[4096,128]{1,0:T(8,128)(2,1)} %wk_ref.1, bf16[4096,128]{1,0:T(8,128)(2,1)} %wv_ref.1, ...), custom_call_target="tpu_custom_call" | custom-call | flops 1610612736 | bytes 6291456 | tf_op jit(solution)/shard_map/qkv/pallas_call | solution.py:276
  235.1 1.9 copy.69
  236.9 111.4 %attend.1 = (bf16[256,4,128]{2,1,0:T(4,128)(2,1)}, bf16[256,1024,128]{2,1,0:T(8,128)(2,1)}, bf16[256,1024,128]{2,1,0:T(8,128)(2,1)}, s32[256,1024]{1,0:T(8,128)}) custom-call(s32[256]{0:T(256)} %tok_ref.1, bf16[256,4,128]{2,1,0:T(4,128)(2,1)} %bitcast.83, bf16[256,128]{1,0:T(8,128)(2,1)} %get-tuple-element.22.kn_ref, ...), custom_call_target="tpu_custom_call" | custom-call | flops 536870912 | bytes 268435456 | tf_op jit(solution)/shard_map/attend/pallas_call | solution.py:327
  348.4 1.7 copy.68
  350.1 5.0 %wo.1 = bf16[256,4096]{1,0:T(8,128)(2,1)} custom-call(bf16[256,512]{1,0:T(8,128)(2,1)} %bitcast.84, bf16[512,4096]{1,0:T(8,128)(2,1)} %w_ref.1), custom_call_target="tpu_custom_call" | custom-call | flops 1073741824 | bytes 4194304 | tf_op jit(solution)/shard_map/wo/pallas_call | solution.py:346
  355.1 31.4 %ar4.1.x_ref = bf16[4,2,32,4096]{3,2,1,0:T(8,128)(2,1)} custom-call(bf16[4,2,32,4096]{3,2,1,0:T(8,128)(2,1)} %bitcast.77, bf16[4,2,32,4096]{3,2,1,0:T(8,128)(2,1)} %ar3.1.x_ref, bf16[1,4096]{1,0:T(2,128)(2,1)} %broadcast_in_dim.13.b_ref), custom_call_target="tpu_custom_call" | custom-call | flops 1000000000 | bytes 80000000 | tf_op jit(solution)/shard_map/ar4/pallas_call | solution.py:114
  386.5 24.7 %mlp2.1 = bf16[256,4096]{1,0:T(8,128)(2,1)} custom-call(bf16[256,4096]{1,0:T(8,128)(2,1)} %bitcast.67, bf16[3,2,4096]{2,1,0:T(2,128)(2,1)} %sc_ref.11, bf16[3,4096,1536]{2,1,0:T(8,128)(2,1)} %w1_ref.5, bf16[3,1536]{1,0:T(4,128)(2,1)} %b1_ref.5, bf16[3,4096,1536]{2,1,0:T(8,128)(2,1)} %w2_ref.5, bf16[3,1536]{1,0:T(4,128)(2,1)} %b2_ref.5, ...), custom_call_target="tpu_custom_call" | custom-call | flops 9663676416 | bytes 37748736 | tf_op jit(solution)/shard_map/mlp2/pallas_call | solution.py:159
  411.3 32.2 %ar5.1 = bf16[4,2,32,4096]{3,2,1,0:T(8,128)(2,1)} custom-call(bf16[4,2,32,4096]{3,2,1,0:T(8,128)(2,1)} %bitcast.75, bf16[4,2,32,4096]{3,2,1,0:T(8,128)(2,1)} %ar4.1.x_ref, bf16[3,4096]{1,0:T(4,128)(2,1)} %b_ref.9), custom_call_target="tpu_custom_call" | custom-call | flops 1000000000 | bytes 80000000 | tf_op jit(solution)/shard_map/ar5/pallas_call | solution.py:114
  443.5 3.1 copy.80
  (10 shorter events, 0.1 us)
Async XLA Ops:
  135.5 31.6 %copy-start.2 = (f32[1,704,256]{2,1,0:T(8,128)S(1)}, f32[1,704,256]{2,1,0:T(8,128)}, u32[]{:S(2)}) copy-start(f32[1,704,256]{2,1,0:T(8,128)} %get-tuple-element.27) | copy-start | bytes 2162692
  135.5 31.6 %copy-start.3 = (f32[1,704,256]{2,1,0:T(8,128)S(1)}, f32[1,704,256]{2,1,0:T(8,128)}, u32[]{:S(2)}) copy-start(f32[1,704,256]{2,1,0:T(8,128)} %get-tuple-element.28) | copy-start | bytes 2162692
  167.0 1.7 copy-start
  167.0 2.1 copy-start.1

commit v2 on v0

v2 whole, which is shorter than its diff:
```python
import functools

import jax
import jax.numpy as jnp
from jax import lax
from jax.experimental import pallas as pl
from jax.experimental.pallas import tpu as pltpu
from jax.sharding import PartitionSpec as P

ROPE_BASE = 10000.0
NORM_EPS = 1e-6
MESH = pl.DeviceIdType.MESH
BF = jnp.bfloat16
F32 = jnp.float32
ANY = pl.BlockSpec(memory_space=pl.ANY)
VM = pl.BlockSpec(memory_space=pltpu.VMEM)
B = 256
D = 4096
LC = 704
FC = 1536
W = 1024
HD = 128
G = 4
GC = D // G


def rms(x, scale):
    xf = x.astype(F32)
    mean_sq = jnp.mean(xf * xf, axis=-1, keepdims=True)
    return (xf * lax.rsqrt(mean_sq + NORM_EPS) * (1.0 + scale.astype(F32))).astype(BF)


ROPE_DN = (((1,), (1,)), ((), ()))
TN = (((0,), (0,)), ((), ()))
COLS = [pl.ds(g * GC, GC) for g in range(G)]


class Links:
    def __init__(self, part, recv1, recv2, own, n, xown, s1s, s1r, s2s, s2r, s3s, s3r, s4s, s4r):
        self.part, self.recv1, self.recv2, self.own, self.n, self.xown = part, recv1, recv2, own, n, xown
        self.s1s, self.s1r, self.s2s, self.s2r, self.s3s, self.s3r, self.s4s, self.s4r = s1s, s1r, s2s, s2r, s3s, s3r, s4s, s4r
        t = lax.axis_index('tp')
        y, x = t // 4, (t // 2) % 2
        self.c = t % 2
        self.q = 2 * y + x
        self.partner = 2 * self.q + 1 - self.c
        self.chips = [2 * y + (1 - x), 2 * (1 - y) + x, 2 * (1 - y) + (1 - x)]
        self.peers = [2 * qd + self.c for qd in self.chips]

    def enter(self):
        barrier = pltpu.get_barrier_semaphore()
        for dev in [self.partner] + self.peers:
            pl.semaphore_signal(barrier, inc=1, device_id={'tp': dev}, device_id_type=MESH)
        pl.semaphore_wait(barrier, 4)

    def remote(self, src, dst, ss, rs, dev):
        cp = pltpu.make_async_remote_copy(src_ref=src, dst_ref=dst, send_sem=ss, recv_sem=rs, device_id={'tp': dev}, device_id_type=MESH)
        cp.start()
        return cp

    def dots(self, g, lhs, rhs):
        def body(p, carry):
            out = jnp.dot(lhs[...], rhs[:, pl.ds(pl.multiple_of(p * 512, 512), 512)], preferred_element_type=F32)
            self.part[:, :, :, pl.ds(pl.multiple_of(g * GC + p * 512, 512), 512)] = out.astype(BF).reshape(4, 2, 32, 512)
            return carry

        lax.fori_loop(0, GC // 512, body, 0)

    def reduce_scatter(self, produce, bias_row):
        c, q, chips, cp1, cp2 = self.c, self.q, self.chips, [], []

        def pair(g):
            cols = COLS[g]
            cp1[g].wait_recv()
            row = {}
            for k in (2, 0, 1):
                s = self.part[chips[k], c, :, cols].astype(F32) + self.recv1[chips[k], :, cols].astype(F32)
                self.part[chips[k], c, :, cols] = s.astype(BF)
                row[k] = self.remote(self.part.at[chips[k], c, :, cols], self.recv2.at[k, :, cols], self.s2s.at[g, k], self.s2r.at[g, k], self.peers[k])
            self.own[:, cols] = self.part[q, c, :, cols].astype(F32) + self.recv1[q, :, cols].astype(F32)
            cp2.append(row)

        for g in range(G):
            produce(g)
            cp1.append(self.remote(self.part.at[:, 1 - c, :, COLS[g]], self.recv1.at[:, :, COLS[g]], self.s1s.at[g], self.s1r.at[g], self.partner))
            if g >= 1:
                pair(g - 1)
        pair(G - 1)
        for g in range(G):
            cols = COLS[g]
            for k in range(3):
                cp2[g][k].wait_recv()
            tot = self.own[:, cols]
            for k in range(3):
                tot = tot + self.recv2[k, :, cols].astype(F32)
            bias = bias_row[:, g * GC:(g + 1) * GC]
            self.xown[:, cols] = (self.xown[:, cols].astype(F32) + tot.astype(BF).astype(F32) + bias).astype(BF)
        for g in range(G):
            cp1[g].wait_send()
            for k in range(3):
                cp2[g][k].wait_send()

    def place(self, dev, g):
        return self.n.at[pl.ds(pl.multiple_of(dev * 32, 32), 32), COLS[g]]

    def gather_start(self, rows):
        me = 2 * self.q + self.c
        self.n[pl.ds(pl.multiple_of(me * 32, 32), 32), :] = rows
        self.cp3, self.cp4 = [], []
        for g in range(G):
            ref = self.place(me, g)
            row = {}
            for k in (2, 0, 1):
                row[k] = self.remote(ref, ref, self.s3s.at[g, k], self.s3r.at[g, k], self.peers[k])
            row[3] = self.remote(ref, ref, self.s3s.at[g, 3], self.s3r.at[g, 3], self.partner)
            self.cp3.append(row)

    def gather_forward(self, g):
        row = []
        for k in range(3):
            self.cp3[g][k].wait_recv()
            ref = self.place(self.peers[k], g)
            row.append(self.remote(ref, ref, self.s4s.at[g, k], self.s4r.at[g, k], self.partner))
        self.cp4.append(row)

    def gather_ready(self, g):
        self.cp3[g][3].wait_recv()
        for k in range(3):
            self.cp4[g][k].wait_recv()

    def gather_finish(self):
        for g in range(G):
            for k in range(4):
                self.cp3[g][k].wait_send()
            for k in range(3):
                self.cp4[g][k].wait_send()

    def gathered(self, use, fresh=False):
        for g in range(G):
            if not fresh:
                self.gather_forward(g)
            if g >= 1:
                if not fresh:
                    self.gather_ready(g - 1)
                use(g - 1)
        if not fresh:
            self.gather_ready(G - 1)
        use(G - 1)
        if not fresh:
            self.gather_finish()


LINK_SCRATCH = [
    pltpu.VMEM((4, 2, 32, D), BF), pltpu.VMEM((4, 32, D), BF), pltpu.VMEM((3, 32, D), BF),
    pltpu.VMEM((32, D), F32), pltpu.VMEM((B, D), BF), pltpu.VMEM((32, D), BF),
    pltpu.SemaphoreType.DMA((G,)), pltpu.SemaphoreType.DMA((G,)), pltpu.SemaphoreType.DMA((G, 3)), pltpu.SemaphoreType.DMA((G, 3)),
    pltpu.SemaphoreType.DMA((G, 4)), pltpu.SemaphoreType.DMA((G, 4)), pltpu.SemaphoreType.DMA((G, 3)), pltpu.SemaphoreType.DMA((G, 3)),
]
NLINK = len(LINK_SCRATCH)


class Ring:
    def __init__(self, groups, depth):
        self.groups, self.depth, self.issued = groups, depth, 0

    def fill(self, used):
        while self.issued < min(used + self.depth, len(self.groups)):
            for cp in self.groups[self.issued]:
                cp.start()
            self.issued += 1

    def wait(self, k):
        for cp in self.groups[k]:
            cp.wait()


SLOTS = 3


def up_group(k, layer, g, w1, w2, wu, sems):
    s = k % SLOTS
    rows = pl.ds(g * GC, GC)
    return [pltpu.make_async_copy(w1.at[layer, rows, :], wu.at[s, 0], sems.at[s, 0]), pltpu.make_async_copy(w2.at[layer, rows, :], wu.at[s, 1], sems.at[s, 1])]


def down_group(k, layer, g, wd, wdb, sems):
    s = k % SLOTS
    return [pltpu.make_async_copy(wd.at[layer, :, COLS[g]], wdb.at[s], sems.at[s])]


def mlp_up(net, ring, k0, wu, acc, h_s, b1, b2):
    def use(g):
        k = k0 + g
        s = k % SLOTS
        ring.wait(k)
        ng = net.n[:, COLS[g]]

        def body(j, carry):
            lanes = pl.ds(pl.multiple_of(j * 512, 512), 512)
            for half in range(2):
                a = jnp.dot(ng, wu[s, half, :, lanes], preferred_element_type=F32)
                for p in range(2):
                    piece = a[:, 256 * p:256 * p + 256]
                    at = 6 * half + 2 * j + p
                    acc[at] = piece if g == 0 else acc[at] + piece
            return carry

        lax.fori_loop(0, FC // 512, body, 0)
        ring.fill(k + 1)

    net.gathered(use)

    for j in range(FC // 256):
        lanes = slice(256 * j, 256 * j + 256)
        h_s[:, lanes] = (jax.nn.gelu(acc[j] + b1[:, lanes], approximate=True) * (acc[6 + j] + b2[:, lanes])).astype(BF)


def mlp_down(net, ring, k0, wdb, h_s, bias_row):
    def produce(g):
        k = k0 + g
        s = k % SLOTS
        ring.wait(k)
        net.dots(g, h_s, wdb.at[s])
        ring.fill(k + 1)

    net.reduce_scatter(produce, bias_row)


def rope(v, tab_ref):
    return v * tab_ref[0] + pltpu.roll(v, 96, 1) * tab_ref[1] + pltpu.roll(v, 32, 1) * tab_ref[2]


def kernel_a(x_ref, sc_ref, wx, wy, conv, lru, wa_ref, wi_ref, pc_ref, tok_ref, wout, rb_ref, w1, b1_ref, w2, b2_ref, wd, mb_ref, wq, wk, wv, tab_ref,
             q_ref, k_ref, v_ref, xo_ref, conv_out, lru_out, *scratch):
    net = Links(*scratch[:NLINK])
    wu, wdb, wxb, wob, acc, h_s, conv_s, xb_s, lru_s, ht_s, us, ds, xs, os, ss, ts, ls = scratch[NLINK:]
    f = lambda ref: ref[...].astype(F32)

    load_x = pltpu.make_async_copy(x_ref, net.part, ls)
    load_x.start()
    rec_in = [Ring([[pltpu.make_async_copy(wx.at[l, :, COLS[g]], wxb.at[0, :, COLS[g]], xs.at[0, g]), pltpu.make_async_copy(wy.at[l, :, COLS[g]], wxb.at[1, :, COLS[g]], xs.at[1, g])] for g in range(G)], G) for l in range(2)]
    rec_out = [Ring([[pltpu.make_async_copy(wout.at[l, :, COLS[g]], wob.at[:, COLS[g]], os.at[g])] for g in range(G)], G) for l in range(2)]
    state_in = [[pltpu.make_async_copy(conv.at[l], conv_s, ss.at[0]), pltpu.make_async_copy(lru.at[l], lru_s, ss.at[1])] for l in range(2)]
    state_out = [[pltpu.make_async_copy(conv_s.at[1:3], conv_out.at[l, 0:2], ts.at[0]), pltpu.make_async_copy(xb_s, conv_out.at[l, 2], ts.at[1]), pltpu.make_async_copy(lru_s, lru_out.at[l], ts.at[2])] for l in range(2)]
    ups = [up_group(4 * l + g, l, g, w1, w2, wu, us) for l in range(2) for g in range(G)]
    for g in range(G):
        s = (8 + g) % SLOTS
        rows = pl.ds(g * GC, GC)
        ups.append([pltpu.make_async_copy(wq.at[rows, :], wu.at[s, 0, :, 0:512], us.at[s, 0]), pltpu.make_async_copy(wk.at[rows, :], wu.at[s, 0, :, 512:640], us.at[s, 1]),
                    pltpu.make_async_copy(wv.at[rows, :], wu.at[s, 0, :, 640:768], us.at[s, 2])])
    up = Ring(ups, SLOTS)
    down = Ring([down_group(4 * l + g, l, g, wd, wdb, ds) for l in range(2) for g in range(G)], SLOTS)

    rec_in[0].fill(0)
    for cp in state_in[0]:
        cp.start()
    rec_out[0].fill(0)
    net.enter()
    load_x.wait()
    for j in range(8):
        net.n[32 * j:32 * j + 32, :] = rms(net.part[j // 2, j % 2], f(sc_ref)[0, 0:1, :])
    net.xown[...] = net.part[net.q, net.c]
    tok = tok_ref[...]
    fresh = tok == 0

    for layer in range(2):
        def use(g):
            rec_in[layer].wait(g)
            ng = net.n[:, COLS[g]]
            for half in range(2):
                r = lax.dot_general(wxb[half, :, COLS[g]], ng, ROPE_DN, preferred_element_type=F32)
                for h in range(4):
                    piece = r[176 * h:176 * h + 176]
                    acc[4 * half + h, 0:176, :] = piece if g == 0 else acc[4 * half + h, 0:176, :] + piece

        net.gathered(use, fresh=layer == 0)
        if layer == 0:
            up.fill(0)
            down.fill(0)
            rec_in[1].fill(0)
        for cp in state_in[layer]:
            cp.wait()
        for h in range(4):
            rows = slice(176 * h, 176 * h + 176)
            pc = pc_ref[layer, rows, :]
            col = lambda k: pc[:, k:k + 1]
            xb = (acc[h, 0:176, :] + col(0)).astype(BF)
            yb = jax.nn.gelu(acc[4 + h, 0:176, :] + col(1), approximate=True)
            xb_s[rows, :] = xb
            hist = jnp.zeros((176, B), F32)
            for j in range(3):
                hist = hist + jnp.where(tok >= 3 - j, conv_s[j, rows, :].astype(F32), 0.0) * col(5 - j)
            xc = (col(6) + col(2) * xb.astype(F32) + hist).astype(BF)
            rg = jax.nn.sigmoid(lax.dot_general(wa_ref[layer, h], xc, TN, preferred_element_type=F32) + col(7))
            ig = jax.nn.sigmoid(lax.dot_general(wi_ref[layer, h], xc, TN, preferred_element_type=F32) + col(8))
            a = jnp.exp(rg * col(9))
            sc = jnp.sqrt(1.0 - a * a)
            a = jnp.where(fresh, 0.0, a)
            sc = jnp.where(fresh, 1.0, sc)
            hn = a * lru_s[rows, :] + sc * ig * xc.astype(F32)
            lru_s[rows, :] = hn
            ht_s[rows, :] = (hn * yb).astype(BF)
        for cp in state_out[layer]:
            cp.start()
        ht_s[LC:, :] = jnp.zeros((64, B), BF)
        h_s[:, :LC + 64] = ht_s[...].T

        def produce(g):
            rec_out[layer].wait(g)
            net.dots(g, h_s.at[:, :LC], wob.at[:, COLS[g]])

        net.reduce_scatter(produce, f(rb_ref)[layer:layer + 1])
        net.gather_start(rms(net.xown[...], f(sc_ref)[layer, 1:2, :]))
        for cp in state_out[layer]:
            cp.wait()
        if layer == 0:
            rec_out[1].fill(0)
            for cp in state_in[1]:
                cp.start()
        mlp_up(net, up, 4 * layer, wu, acc, h_s, f(b1_ref)[layer:layer + 1], f(b2_ref)[layer:layer + 1])
        mlp_down(net, down, 4 * layer, wdb, h_s, f(mb_ref)[layer:layer + 1])
        net.gather_start(rms(net.xown[...], f(sc_ref)[layer + 1, 0:1, :]))

    xo_ref[...] = net.xown[...]

    def use_q(g):
        k = 8 + g
        up.wait(k)
        ng = net.n[:, COLS[g]]
        for j in range(3):
            a = jnp.dot(ng, wu[k % SLOTS, 0, :, 256 * j:256 * j + 256], preferred_element_type=F32)
            acc[j] = a if g == 0 else acc[j] + a
        up.fill(k + 1)

    net.gathered(use_q)
    for h in range(4):
        q_ref[h] = rope(acc[h // 2, :, 128 * (h % 2):128 * (h % 2) + 128], tab_ref).astype(BF)
    k_ref[...] = rope(acc[2, :, 0:128], tab_ref).astype(BF)
    v_ref[...] = acc[2, :, 128:256].astype(BF)


def first_layers(x, scale, wxt, wyt, convt, lrut, wa, wi, pcols, tok, wout, rb, w1, b1, w2, b2, wd, mb, wq, wk, wv, tab):
    return pl.pallas_call(
        kernel_a,
        name='first_layers',
        out_shape=(jax.ShapeDtypeStruct((4, B, HD), BF), jax.ShapeDtypeStruct((B, HD), BF), jax.ShapeDtypeStruct((B, HD), BF), jax.ShapeDtypeStruct((32, D), BF),
                   jax.ShapeDtypeStruct(convt.shape, BF), jax.ShapeDtypeStruct(lrut.shape, F32)),
        in_specs=[ANY, VM, ANY, ANY, ANY, ANY, VM, VM, VM, VM, ANY, VM, ANY, VM, ANY, VM, ANY, VM, ANY, ANY, ANY, VM],
        out_specs=(VM, VM, VM, VM, ANY, ANY),
        scratch_shapes=LINK_SCRATCH + [
            pltpu.VMEM((SLOTS, 2, GC, FC), BF), pltpu.VMEM((SLOTS, FC, GC), BF), pltpu.VMEM((2, LC, D), BF), pltpu.VMEM((LC, D), BF),
            pltpu.VMEM((12, B, 256), F32), pltpu.VMEM((B, FC), BF), pltpu.VMEM((3, LC, B), BF), pltpu.VMEM((LC, B), BF), pltpu.VMEM((LC, B), F32),
            pltpu.VMEM((LC + 64, B), BF),
            pltpu.SemaphoreType.DMA((SLOTS, 3)), pltpu.SemaphoreType.DMA((SLOTS,)), pltpu.SemaphoreType.DMA((2, G)), pltpu.SemaphoreType.DMA((G,)),
            pltpu.SemaphoreType.DMA((2,)), pltpu.SemaphoreType.DMA((3,)), pltpu.SemaphoreType.DMA,
        ],
        compiler_params=pltpu.CompilerParams(collective_id=0, has_side_effects=True, vmem_limit_bytes=67043328),
        cost_estimate=pl.CostEstimate(flops=30 * 10**9, bytes_accessed=400 * 10**6, transcendentals=0),
    )(x.reshape(4, 2, 32, D), scale, wxt, wyt, convt, lrut, wa, wi, pcols, tok, wout, rb, w1, b1, w2, b2, wd, mb, wq, wk, wv, tab)


def kernel_b(o_ref, x_ref, wo, bo_ref, sc_ref, w1, b1_ref, w2, b2_ref, wd, mb_ref, out_ref, *scratch):
    net = Links(*scratch[:NLINK])
    wu, wdb, wob, acc, h_s, us, ds, os, ls = scratch[NLINK:]
    f = lambda ref: ref[...].astype(F32)
    load_o = Ring([[pltpu.make_async_copy(wo.at[:, COLS[g]], wob.at[:, COLS[g]], os.at[g])] for g in range(G)], G)
    up = Ring([up_group(g, 2, g, w1, w2, wu, us) for g in range(G)], SLOTS)
    down = Ring([down_group(g, 2, g, wd, wdb, ds) for g in range(G)], SLOTS)
    load_o.fill(0)
    up.fill(0)
    down.fill(0)
    net.enter()
    net.xown[...] = x_ref[...]

    def produce(g):
        load_o.wait(g)
        net.dots(g, o_ref, wob.at[:, COLS[g]])

    net.reduce_scatter(produce, f(bo_ref))
    net.gather_start(rms(net.xown[...], f(sc_ref)[2, 1:2, :]))
    mlp_up(net, up, 0, wu, acc, h_s, f(b1_ref)[2:3], f(b2_ref)[2:3])
    mlp_down(net, down, 0, wdb, h_s, f(mb_ref)[2:3])
    net.gather_start(net.xown[...])
    stores = []

    def use(g):
        cp = pltpu.make_async_copy(net.n.at[:, COLS[g]], out_ref.at[:, COLS[g]], ls.at[g])
        cp.start()
        stores.append(cp)

    net.gathered(use)
    for cp in stores:
        cp.wait()


def last_layer(o, x_own, wo, bo, scale, w1, b1, w2, b2, wd, mb):
    return pl.pallas_call(
        kernel_b,
        name='last_layer',
        out_shape=jax.ShapeDtypeStruct((B, D), BF),
        in_specs=[VM, VM, ANY, VM, VM, ANY, VM, ANY, VM, ANY, VM],
        out_specs=ANY,
        scratch_shapes=LINK_SCRATCH + [
            pltpu.VMEM((SLOTS, 2, GC, FC), BF), pltpu.VMEM((SLOTS, FC, GC), BF), pltpu.VMEM((512, D), BF),
            pltpu.VMEM((12, B, 256), F32), pltpu.VMEM((B, FC), BF),
            pltpu.SemaphoreType.DMA((SLOTS, 3)), pltpu.SemaphoreType.DMA((SLOTS,)), pltpu.SemaphoreType.DMA((G,)), pltpu.SemaphoreType.DMA((G,)),
        ],
        compiler_params=pltpu.CompilerParams(collective_id=1, has_side_effects=True, vmem_limit_bytes=67043328),
        cost_estimate=pl.CostEstimate(flops=12 * 10**9, bytes_accessed=200 * 10**6, transcendentals=0),
    )(o, x_own, wo, bo, scale, w1, b1, w2, b2, wd, mb)


RA = 8


def attn_kernel(tok_ref, q_ref, kn_ref, vn_ref, slot_ref, k_ref, v_ref, o_ref, ko_ref, vo_ref, so_ref, s_s):
    i = pl.program_id(0)
    lane = lax.broadcasted_iota(jnp.int32, (1, W), 1)
    sub = lax.broadcasted_iota(jnp.int32, (16, HD), 0)
    kn = kn_ref[...].astype(F32)
    vn = vn_ref[...].astype(F32)
    ko_ref[...] = k_ref[...]
    vo_ref[...] = v_ref[...]
    for r in range(RA):
        tp = tok_ref[i * RA + r]
        slot = lax.rem(tp, W)
        base = pl.multiple_of((slot // 16) * 16, 16)
        hit = sub == (slot - base)
        ko_ref[r, pl.ds(base, 16), :] = jnp.where(hit, kn[r:r + 1], k_ref[r, pl.ds(base, 16), :].astype(F32)).astype(BF)
        vo_ref[r, pl.ds(base, 16), :] = jnp.where(hit, vn[r:r + 1], v_ref[r, pl.ds(base, 16), :].astype(F32)).astype(BF)
        so_ref[r:r + 1, :] = jnp.where(lane == slot, tp, slot_ref[r:r + 1, :])
    for r in range(RA):
        tp = tok_ref[i * RA + r]
        sn = so_ref[r:r + 1, :]
        age = tp - sn
        valid = (sn >= 0) & (age >= 0) & (age < W)
        s = lax.dot_general(q_ref[r], ko_ref[r], (((1,), (1,)), ((), ())), preferred_element_type=F32) * (HD ** -0.5)
        s_s[4 * r:4 * r + 4, :] = jnp.where(valid, s, -jnp.inf)
    s = s_s[...]
    e = jnp.exp(s - jnp.max(s, axis=-1, keepdims=True))
    s_s[...] = e / jnp.sum(e, axis=-1, keepdims=True)
    for r in range(RA):
        o_ref[r] = jnp.dot(s_s[4 * r:4 * r + 4, :].astype(BF), vo_ref[r], preferred_element_type=F32).astype(BF)


def attend(tok, q, kn, vn, slot_pos, kc, vc):
    cache = pl.BlockSpec((RA, W, HD), lambda i, t: (i, 0, 0))
    row = pl.BlockSpec((RA, HD), lambda i, t: (i, 0))
    slots = pl.BlockSpec((RA, W), lambda i, t: (i, 0))
    heads = pl.BlockSpec((RA, 4, HD), lambda i, t: (i, 0, 0))
    return pl.pallas_call(
        attn_kernel,
        name='attend',
        grid_spec=pltpu.PrefetchScalarGridSpec(
            num_scalar_prefetch=1,
            grid=(B // RA,),
            in_specs=[heads, row, row, slots, cache, cache],
            out_specs=(heads, cache, cache, slots),
            scratch_shapes=[pltpu.VMEM((4 * RA, W), F32)],
        ),
        out_shape=(jax.ShapeDtypeStruct((B, 4, HD), BF), jax.ShapeDtypeStruct(kc.shape, BF), jax.ShapeDtypeStruct(vc.shape, BF), jax.ShapeDtypeStruct(slot_pos.shape, jnp.int32)),
        cost_estimate=pl.CostEstimate(flops=4 * B * 4 * W * HD, bytes_accessed=8 * B * W * HD, transcendentals=0),
    )(tok, q, kn, vn, slot_pos, kc, vc)


def rope_tables(tok_pos):
    quarter = HD // 4
    inv_freq = ROPE_BASE ** (-jnp.arange(quarter, dtype=F32) / quarter)
    angles = tok_pos.astype(F32)[:, None] * inv_freq[None, :]
    cos, sin = jnp.cos(angles), jnp.sin(angles)
    one = jnp.ones_like(cos)
    zero = jnp.zeros_like(cos)
    keep = jnp.concatenate([cos, cos, one, one], axis=1)
    up = jnp.concatenate([-sin, zero, zero, zero], axis=1)
    down = jnp.concatenate([zero, sin, zero, zero], axis=1)
    return jnp.stack([keep, up, down])


def io_specs():
    in_specs = (P('dp', None), P('dp'), P(None, 'dp', None, 'tp'), P(None, 'dp', 'tp'), P('dp', None, None), P('dp', None, None), P('dp', None),
                P(), P(None, None, 'tp'), P(None, 'tp'), P(None, None, 'tp'), P(None, 'tp'), P(None, None, 'tp'), P(None, 'tp'),
                P(None, 'tp', None, None), P(None, 'tp'), P(None, 'tp', None, None), P(None, 'tp'), P(None, 'tp'), P(None, 'tp', None), P(),
                P(None, 'tp'), P(), P(), P('tp', None), P(),
                P(None, None, 'tp'), P(None, 'tp'), P(None, None, 'tp'), P(None, 'tp'), P(None, 'tp', None), P())
    out_specs = (P('dp', None), P(None, 'dp', None, 'tp'), P(None, 'dp', 'tp'), P('dp', None, None), P('dp', None, None), P('dp', None))
    return in_specs, out_specs


def solution(mesh):
    in_specs, out_specs = io_specs()

    def local_step(x_in, tok_pos, conv_state, lru_state, k_cache, v_cache, slot_pos, norm_scale, rec_wx, rec_bx, rec_wy, rec_by, conv_w, conv_b, gate_wa, gate_ba, gate_wi, gate_bi, a_param, rec_wout, rec_bout, attn_wq, attn_wk, attn_wv, attn_wo, attn_bo, mlp_w1, mlp_b1, mlp_w2, mlp_b2, mlp_wd, mlp_bd):
        wxt = jnp.swapaxes(rec_wx, 1, 2)
        wyt = jnp.swapaxes(rec_wy, 1, 2)
        convt = jnp.transpose(conv_state, (0, 2, 3, 1))
        lrut = jnp.swapaxes(lru_state, 1, 2)
        f = lambda v: v.astype(F32)
        pcols = jnp.stack([f(rec_bx), f(rec_by), f(conv_w[:, 0]), f(conv_w[:, 1]), f(conv_w[:, 2]), f(conv_w[:, 3]), f(conv_b), f(gate_ba), f(gate_bi), -8.0 * jax.nn.softplus(a_param)], axis=-1)
        tok_row = tok_pos[None, :]
        tab = rope_tables(tok_pos)

        q, kn, vn, x_own, convs, lrus = first_layers(x_in, norm_scale, wxt, wyt, convt, lrut, gate_wa, gate_wi, pcols, tok_row, rec_wout, rec_bout, mlp_w1, mlp_b1, mlp_w2, mlp_b2, mlp_wd, mlp_bd, attn_wq, attn_wk, attn_wv, tab)
        o, k_next, v_next, slot_next = attend(tok_pos, jnp.swapaxes(q, 0, 1), kn, vn, slot_pos, k_cache, v_cache)
        x = last_layer(o.reshape(B, 512), x_own, attn_wo, attn_bo[None, :], norm_scale, mlp_w1, mlp_b1, mlp_w2, mlp_b2, mlp_wd, mlp_bd)
        conv_out = jnp.transpose(convs, (0, 3, 1, 2))
        lru_out = jnp.swapaxes(lrus, 1, 2)
        return (x, conv_out, lru_out, k_next, v_next, slot_next)

    return jax.shard_map(local_step, mesh=mesh, in_specs=in_specs, out_specs=out_specs, check_vma=False)
```

time: 625 us -> 339 us (0.54); the launches traced: 616 us -> 338 us
  Pallas kernels: 0 us -> 318 us
  waiting for transfers between devices: 289 us -> 0 us
  matrix products: 176 us -> 0 us
  other arithmetic: 129 us -> 7.2 us
  between operations: 15.1 us -> 0.72 us
  local copies, waits for them, and re-layouts: 5.58 us -> 11.9 us
    pallas_call x0 -> x3, Pallas kernels: none -> 318 us  [the longest x1 150 us: first_layers(): pl.pallas_call(kernel_a, name='first_layers', out_shape=(jax.ShapeDtypeSt...]
    psum x6 -> x0, waiting for transfers between devices: 289 us -> none  [local_step(): lax.psum(part_sum.astype(jnp.bfloat16), 'tp')]
    dot_general x19 -> x0, matrix products: 148 us -> none  [the longest x3 49.8 us: mlp_update(): return jnp.dot(hidden, w_down, preferred_element_type=jnp.float32)]
    select_n x1 -> x0, other arithmetic: 88.4 us -> none  [write_cache(): k_next = jnp.where(target[:, :, None], k_new[:, None, :], k_cache)]
    sub x1 -> x0, matrix products: 27.8 us -> none  [attend(): probs_bf = jax.nn.softmax(scores, axis=-1).astype(jnp.bfloat16)]
    reduce_sum x7 -> x0, other arithmetic: 19.8 us -> none  [the longest x6 16.9 us: rms_norm(): mean_sq = jnp.mean(res_f * res_f, axis=-1, keepdims=True)]
    add x11 -> x0, other arithmetic: 7.61 us -> none  [the longest x2 3.32 us: recurrent_update(): decay_gate * lru_prev]
  transfers between devices with their start and end apart: 6 -> 0, of which waited for: 6 -> 0; matrix products, arithmetic and copies ran while one was open for 1% -> 0% of each run, Pallas kernels for 0% -> 0%
where the time goes in v2:
time: 339 us; the launch traced here: 338 us
  Pallas kernels  318 us (94%)
  local copies, waits for them, and re-layouts  11.9 us (4%)
  other arithmetic  7.2 us (2%)
    pallas_call x1, Pallas kernels, first_layers(): pl.pallas_call(kernel_a, name='first_layers', out_shape=(jax.ShapeDtypeSt...  150 us
    pallas_call x1, Pallas kernels, attend(): pl.pallas_call(attn_kernel, name='attend', grid_spec=pltpu.PrefetchScalar...  97.6 us
    pallas_call x1, Pallas kernels, last_layer(): pl.pallas_call(kernel_b, name='last_layer', out_shape=jax.ShapeDtypeStruc...  70 us
    unnamed x12, local copies, waits for them, and re-layouts  7.46 us

profile of v2, /device:TPU:1, one launch (start us, length us, event | category | flops | bytes accessed | tf_op | source)
XLA Modules:
  0.0 337.9 jit_solution(6574816835415916353)
XLA Ops:
  0.6 0.1 pad.6.clone
  0.7 0.1 pad.9.clone
  0.8 0.7 convert_element_type.68
  1.5 1.3 broadcast_in_dim.13.bo_ref
  2.8 0.9 slice_convert_fusion
  3.7 0.7 constant_dynamic-update-slice_fusion.9
  4.4 0.7 constant_dynamic-update-slice_fusion.8
  5.1 0.7 constant_dynamic-update-slice_fusion.3
  5.8 0.7 constant_dynamic-update-slice_fusion.2
  6.5 0.7 constant_dynamic-update-slice_fusion.1
  7.2 0.7 constant_dynamic-update-slice_fusion
  7.9 0.5 multiply_cosine_fusion
  8.5 0.1 maximum_bitcast_fusion
  8.6 0.8 pad_maximum_fusion.tab_ref
  9.4 1.1 copy.54.pc_ref
  10.5 150.5 %first_layers.1 = (bf16[4,256,128]{2,1,0:T(8,128)(2,1)}, bf16[256,128]{1,0:T(8,128)(2,1)}, bf16[256,128]{1,0:T(8,128)(2,1)}, bf16[32,4096]{1,0:T(8,128)(2,1)}, b...) custom-call(bf16[4,2,32,4096]{3,2,1,0:T(8,128)(2,1)} %bitcast.52, bf16[3,2,4096]{2,1,0:T(2,128)(2,1)} %sc_ref.3, ...), custom_call_target="tpu_custom_call" | custom-call | flops 30000001024 | bytes 400000000 | tf_op jit(solution)/shard_map/first_layers/pallas_call | solution.py:343
  161.1 1.9 copy.68
  162.9 97.6 %attend.1 = (bf16[256,4,128]{2,1,0:T(4,128)(2,1)}, bf16[256,1024,128]{2,1,0:T(8,128)(2,1)}, bf16[256,1024,128]{2,1,0:T(8,128)(2,1)}, s32[256,1024]{1,0:T(8,128)}) custom-call(s32[256]{0:T(256)} %tok_ref.1, bf16[256,4,128]{2,1,0:T(4,128)(2,1)} %bitcast.55, bf16[256,128]{1,0:T(8,128)(2,1)} %get-tuple-element.17.kn_ref, ...), custom_call_target="tpu_custom_call" | custom-call | flops 536870912 | bytes 268435456 | tf_op jit(solution)/shard_map/attend/pallas_call | solution.py:451
  260.5 1.7 copy.67
  262.2 70.0 %last_layer.1 = bf16[256,4096]{1,0:T(8,128)(2,1)} custom-call(bf16[256,512]{1,0:T(8,128)(2,1)} %bitcast.56, bf16[32,4096]{1,0:T(8,128)(2,1)} %get-tuple-element.20.x_ref, bf16[512,4096]{1,0:T(8,128)(2,1)} %wo.1, bf16[1,4096]{1,0:T(2,128)(2,1)} %broadcast_in_dim.13.bo_ref, bf16[3,2,4096]{2,1,0:T(2,128)(2,1)} %sc_ref.3, bf16[3,4096,1536]{2,1,0:T(8,128)(2,1)} %w1.3, ...), custom_call_target="tpu_custom_call" | custom-call | flops 12000000000 | bytes 200000000 | tf_op jit(solution)/shard_map/last_layer/pallas_call | solution.py:397
  332.2 0.0 copy-start
  332.2 0.0 copy-start.1
  332.2 3.3 copy.81
  335.5 0.0 copy-done
  335.5 1.3 copy.82
  336.8 0.0 copy-done.1
  336.8 1.1 copy.83
  (10 shorter events, 0.1 us)
Async XLA Ops:
  332.2 3.3 copy-start
  332.2 4.6 %copy-start.1 = (f32[2,704,256]{2,1,0:T(8,128)S(1)}, f32[2,704,256]{2,1,0:T(8,128)}, u32[]{:S(2)}) copy-start(f32[2,704,256]{2,1,0:T(8,128)} %get-tuple-element.22) | copy-start | bytes 4325380

commit v3 on v2

v3 whole, which is shorter than its diff:
```python
import functools

import jax
import jax.numpy as jnp
from jax import lax
from jax.experimental import pallas as pl
from jax.experimental.pallas import tpu as pltpu
from jax.sharding import PartitionSpec as P

ROPE_BASE = 10000.0
NORM_EPS = 1e-6
MESH = pl.DeviceIdType.MESH
BF = jnp.bfloat16
F32 = jnp.float32
ANY = pl.BlockSpec(memory_space=pl.ANY)
VM = pl.BlockSpec(memory_space=pltpu.VMEM)
B = 256
D = 4096
LC = 704
FC = 1536
W = 1024
HD = 128
G = 8
KC = 1024
NK = D // KC
GC = D // G


def rms(x, scale):
    xf = x.astype(F32)
    mean_sq = jnp.mean(xf * xf, axis=-1, keepdims=True)
    return (xf * lax.rsqrt(mean_sq + NORM_EPS) * (1.0 + scale.astype(F32))).astype(BF)


NT = (((1,), (1,)), ((), ()))
TN = (((0,), (0,)), ((), ()))
COLS = [pl.ds(g * GC, GC) for g in range(G)]
KCOLS = [pl.ds(k * KC, KC) for k in range(NK)]
PIECES = {1: (0, 1024), 3: (1024, 1024), 5: (2048, 1024), 6: (3072, 512), 7: (3584, 512)}


def chunk(g):
    return pl.ds(pl.multiple_of(g * GC, GC), GC)


class Links:
    def __init__(self, part, recv1, recv2, own, n, xown, s1s, s1r, s2s, s2r, s3s, s3r, s4s, s4r):
        self.part, self.recv1, self.recv2, self.own, self.n, self.xown = part, recv1, recv2, own, n, xown
        self.s1s, self.s1r, self.s2s, self.s2r, self.s3s, self.s3r, self.s4s, self.s4r = s1s, s1r, s2s, s2r, s3s, s3r, s4s, s4r
        t = lax.axis_index('tp')
        y, x = t // 4, (t // 2) % 2
        self.c = t % 2
        self.q = 2 * y + x
        self.partner = 2 * self.q + 1 - self.c
        self.chips = [2 * y + (1 - x), 2 * (1 - y) + x, 2 * (1 - y) + (1 - x)]
        self.peers = [2 * qd + self.c for qd in self.chips]

    def enter(self):
        barrier = pltpu.get_barrier_semaphore()
        for dev in [self.partner] + self.peers:
            pl.semaphore_signal(barrier, inc=1, device_id={'tp': dev}, device_id_type=MESH)
        pl.semaphore_wait(barrier, 4)

    def remote(self, src, dst, ss, rs, dev):
        return pltpu.make_async_remote_copy(src_ref=src, dst_ref=dst, send_sem=ss, recv_sem=rs, device_id={'tp': dev}, device_id_type=MESH)

    def dots(self, g, lhs, rhs):
        out = jnp.dot(lhs[...], rhs[...], preferred_element_type=F32)
        self.part[:, :, :, chunk(g)] = out.astype(BF).reshape(4, 2, 32, GC)

    def to_partner(self, g):
        return self.remote(self.part.at[:, 1 - self.c, :, chunk(g)], self.recv1.at[:, :, chunk(g)], self.s1s.at[g], self.s1r.at[g], self.partner)

    def to_owner(self, g, k):
        return self.remote(self.part.at[self.chips[k], self.c, :, chunk(g)], self.recv2.at[k, :, chunk(g)], self.s2s.at[g, k], self.s2r.at[g, k], self.peers[k])

    def reduce_scatter(self, produce, bias_ref, layer):
        c, q, chips = self.c, self.q, self.chips

        def pair(g):
            cols = chunk(g)
            self.to_partner(g).wait_recv()
            for k in (2, 0, 1):
                s = self.part[chips[k], c, :, cols].astype(F32) + self.recv1[chips[k], :, cols].astype(F32)
                self.part[chips[k], c, :, cols] = s.astype(BF)
                self.to_owner(g, k).start()
            self.own[:, cols] = self.part[q, c, :, cols].astype(F32) + self.recv1[q, :, cols].astype(F32)

        def step(k, carry):
            produce(k, 0)
            self.to_partner(2 * k).start()

            @pl.when(k > 0)
            def _():
                pair(2 * k - 1)

            produce(k, 1)
            self.to_partner(2 * k + 1).start()
            pair(2 * k)
            return carry

        lax.fori_loop(0, NK, step, 0)
        pair(G - 1)

        def final(g, carry):
            cols = chunk(g)
            for k in range(3):
                self.to_owner(g, k).wait_recv()
            tot = self.own[:, cols]
            for k in range(3):
                tot = tot + self.recv2[k, :, cols].astype(F32)
            bias = bias_ref[:, cols].astype(F32)[layer:layer + 1]
            self.xown[:, cols] = (self.xown[:, cols].astype(F32) + tot.astype(BF).astype(F32) + bias).astype(BF)
            return carry

        lax.fori_loop(0, G, final, 0)

        def sent(g, carry):
            self.to_partner(g).wait_send()
            for k in range(3):
                self.to_owner(g, k).wait_send()
            return carry

        lax.fori_loop(0, G, sent, 0)

    def place(self, dev, g):
        return self.n.at[pl.ds(pl.multiple_of(dev * 32, 32), 32), chunk(g)]

    def from_own(self, g, k):
        ref = self.place(2 * self.q + self.c, g)
        return self.remote(ref, ref, self.s3s.at[g, k], self.s3r.at[g, k], self.peers[k] if k < 3 else self.partner)

    def pass_on(self, g, k):
        ref = self.place(self.peers[k], g)
        return self.remote(ref, ref, self.s4s.at[g, k], self.s4r.at[g, k], self.partner)

    def gather_start(self, rows):
        self.n[pl.ds(pl.multiple_of((2 * self.q + self.c) * 32, 32), 32), :] = rows

        def send(g, carry):
            for k in (2, 0, 1, 3):
                self.from_own(g, k).start()
            return carry

        lax.fori_loop(0, G, send, 0)

    def gather_forward(self, g):
        for k in range(3):
            self.from_own(g, k).wait_recv()
            self.pass_on(g, k).start()

    def gather_ready(self, g):
        self.from_own(g, 3).wait_recv()
        for k in range(3):
            self.pass_on(g, k).wait_recv()

    def gather_finish(self):
        def sent(g, carry):
            for k in range(4):
                self.from_own(g, k).wait_send()
            for k in range(3):
                self.pass_on(g, k).wait_send()
            return carry

        lax.fori_loop(0, G, sent, 0)

    def gathered(self, use_piece, fresh=False):
        def use(g):
            if g in PIECES:
                use_piece(*PIECES[g])

        for g in range(G):
            if not fresh:
                self.gather_forward(g)
            if g >= 1:
                if not fresh:
                    self.gather_ready(g - 1)
                use(g - 1)
        if not fresh:
            self.gather_ready(G - 1)
        use(G - 1)
        if not fresh:
            self.gather_finish()


LINK_SCRATCH = [
    pltpu.VMEM((4, 2, 32, D), BF), pltpu.VMEM((4, 32, D), BF), pltpu.VMEM((3, 32, D), BF),
    pltpu.VMEM((32, D), F32), pltpu.VMEM((B, D), BF), pltpu.VMEM((32, D), BF),
    pltpu.SemaphoreType.DMA((G,)), pltpu.SemaphoreType.DMA((G,)), pltpu.SemaphoreType.DMA((G, 3)), pltpu.SemaphoreType.DMA((G, 3)),
    pltpu.SemaphoreType.DMA((G, 4)), pltpu.SemaphoreType.DMA((G, 4)), pltpu.SemaphoreType.DMA((G, 3)), pltpu.SemaphoreType.DMA((G, 3)),
]
NLINK = len(LINK_SCRATCH)


class Stream:
    def __init__(self, group, total, depth):
        self.group, self.total, self.depth = group, total, depth

    def begin(self):
        for k in range(self.depth):
            self.group(k).start()

    def wait(self, k):
        self.group(k).wait()

    def done(self, k):
        @pl.when(k + self.depth < self.total)
        def _():
            self.group(k + self.depth).start()


class Ring:
    def __init__(self, groups, depth):
        self.groups, self.depth, self.issued = groups, depth, 0

    def fill(self, used):
        while self.issued < min(used + self.depth, len(self.groups)):
            for cp in self.groups[self.issued]:
                cp.start()
            self.issued += 1

    def wait(self, k):
        for cp in self.groups[k]:
            cp.wait()


SLOTS = 3


def up_group(k, layer, g, w1, w2, wu, sems):
    s = k % SLOTS
    rows = KCOLS[g]
    return [pltpu.make_async_copy(w1.at[layer, rows, :], wu.at[s, 0], sems.at[s, 0]), pltpu.make_async_copy(w2.at[layer, rows, :], wu.at[s, 1], sems.at[s, 1])]


def down_stream(first, count, wd, wdb, sems):
    def group(k):
        s = lax.rem(k, SLOTS)
        return pltpu.make_async_copy(wd.at[first + k // NK, :, pl.ds(pl.multiple_of(lax.rem(k, NK) * KC, KC), KC)], wdb.at[s], sems.at[s])

    return Stream(group, count * NK, SLOTS)


def wide_stream(src, dst, sems):
    def group(k):
        cols = pl.ds(pl.multiple_of(k * KC, KC), KC)
        return pltpu.make_async_copy(src.at[:, cols], dst.at[:, cols], sems.at[k])

    return Stream(group, NK, NK)


def mlp_up(net, ring, k0, wu, acc, h_s, b1_ref, b2_ref, layer):
    def use(start, size):
        k = k0 + start // KC
        s = k % SLOTS
        off = start % KC
        if off == 0:
            ring.wait(k)
        ng = net.n[:, start:start + size]
        last = start + size == D

        def body(j, carry):
            lanes = pl.ds(pl.multiple_of(j * 512, 512), 512)
            for p in range(2):
                pieces = []
                for half in range(2):
                    sub = pl.ds(pl.multiple_of(j * 512 + p * 256, 256), 256)
                    a = jnp.dot(ng, wu[s, half, off:off + size, sub], preferred_element_type=F32)
                    at = 6 * half + 2 * j + p
                    a = a if start == 0 else acc[at] + a
                    if last:
                        pieces.append(a)
                    else:
                        acc[at] = a
                if last:
                    b1 = b1_ref[:, sub].astype(F32)[layer:layer + 1]
                    b2 = b2_ref[:, sub].astype(F32)[layer:layer + 1]
                    h_s[:, sub] = (jax.nn.gelu(pieces[0] + b1, approximate=True) * (pieces[1] + b2)).astype(BF)
            return carry

        lax.fori_loop(0, FC // 512, body, 0)
        if off + size == KC:
            ring.fill(k + 1)

    net.gathered(use)


def mlp_down(net, stream, k0, wdb, h_s, bias_ref, layer):
    def produce(k, u):
        if u == 0:
            stream.wait(k0 + k)
        net.dots(2 * k + u, h_s, wdb.at[lax.rem(k0 + k, SLOTS), :, u * GC:u * GC + GC])
        if u == 1:
            stream.done(k0 + k)

    net.reduce_scatter(produce, bias_ref, layer)


def rope(v, tab_ref):
    keep_ref, turn_ref = tab_ref
    lane = lax.broadcasted_iota(jnp.int32, v.shape, 1)
    return v * keep_ref[...] + jnp.where(lane < 32, pltpu.roll(v, 96, 1), pltpu.roll(v, 32, 1)) * turn_ref[...]


def kernel_a(x_ref, sc_ref, wx, wy, conv, lru, wa_ref, wi_ref, bx_ref, by_ref, cw_ref, cb_ref, ba_ref, bi_ref, sp_ref, tok_ref, wout, rb_ref, w1, b1_ref, w2, b2_ref, wd, mb_ref, wq, wk, wv, keep_ref, turn_ref,
             q_ref, k_ref, v_ref, xo_ref, conv_out, lru_out, *scratch):
    net = Links(*scratch[:NLINK])
    wu, wdb, wxb, wob, acc, h_s, conv_s, xb_s, lru_s, ht_s, prow, pcol, us, ds, xs, os, ss, ts, ls = scratch[NLINK:]
    f = lambda ref: ref[...].astype(F32)

    load_x = pltpu.make_async_copy(x_ref, net.part, ls)
    load_x.start()
    rec_in = [Ring([[pltpu.make_async_copy(wx.at[l, :, KCOLS[g]], wxb.at[0, :, KCOLS[g]], xs.at[0, g]), pltpu.make_async_copy(wy.at[l, :, KCOLS[g]], wxb.at[1, :, KCOLS[g]], xs.at[1, g])] for g in range(NK)], NK) for l in range(2)]
    rec_out = [wide_stream(wout.at[l], wob, os) for l in range(2)]
    state_in = [[pltpu.make_async_copy(conv.at[l], conv_s, ss.at[0]), pltpu.make_async_copy(lru.at[l], lru_s, ss.at[1])] for l in range(2)]
    state_out = [[pltpu.make_async_copy(conv_s.at[1:3], conv_out.at[l, 0:2], ts.at[0]), pltpu.make_async_copy(xb_s, conv_out.at[l, 2], ts.at[1]), pltpu.make_async_copy(lru_s, lru_out.at[l], ts.at[2])] for l in range(2)]
    ups = [up_group(4 * l + g, l, g, w1, w2, wu, us) for l in range(2) for g in range(NK)]
    for g in range(NK):
        s = (8 + g) % SLOTS
        rows = KCOLS[g]
        ups.append([pltpu.make_async_copy(wq.at[rows, :], wu.at[s, 0, :, 0:512], us.at[s, 0]), pltpu.make_async_copy(wk.at[rows, :], wu.at[s, 0, :, 512:640], us.at[s, 1]),
                    pltpu.make_async_copy(wv.at[rows, :], wu.at[s, 0, :, 640:768], us.at[s, 2])])
    up = Ring(ups, SLOTS)
    down = down_stream(0, 2, wd, wdb, ds)

    rec_in[0].fill(0)
    for cp in state_in[0]:
        cp.start()
    rec_out[0].begin()
    net.enter()
    load_x.wait()
    for j in range(8):
        net.n[32 * j:32 * j + 32, :] = rms(net.part[j // 2, j % 2], f(sc_ref)[0, 0:1, :])
    net.xown[...] = net.part[net.q, net.c]
    tok = tok_ref[...]
    fresh = tok == 0

    for layer in range(2):
        def use(start, size):
            if start % KC == 0:
                rec_in[layer].wait(start // KC)
            ng = net.n[:, start:start + size]
            for half in range(2):
                r = lax.dot_general(wxb[half, :, start:start + size], ng, NT, preferred_element_type=F32)
                for h in range(4):
                    piece = r[176 * h:176 * h + 176]
                    acc[4 * half + h, 0:176, :] = piece if start == 0 else acc[4 * half + h, 0:176, :] + piece

        net.gathered(use, fresh=layer == 0)
        if layer == 0:
            up.fill(0)
            down.begin()
            rec_in[1].fill(0)
        row = lambda ref: ref[...].astype(F32)[layer:layer + 1]
        cw = cw_ref[...].astype(F32)
        params = [row(bx_ref), row(by_ref)] + [cw[layer, j:j + 1, :] for j in range(4)] + [row(cb_ref), row(ba_ref), row(bi_ref), row(sp_ref)]
        for j, p in enumerate(params):
            prow[j:j + 1, 0:LC] = p
        pcol[...] = prow[...].T
        for cp in state_in[layer]:
            cp.wait()
        for h in range(4):
            rows = slice(176 * h, 176 * h + 176)
            pc = pcol[rows, :]
            col = lambda k: pc[:, k:k + 1]
            xb = (acc[h, 0:176, :] + col(0)).astype(BF)
            yb = jax.nn.gelu(acc[4 + h, 0:176, :] + col(1), approximate=True)
            xb_s[rows, :] = xb
            hist = jnp.zeros((176, B), F32)
            for j in range(3):
                hist = hist + jnp.where(tok >= 3 - j, conv_s[j, rows, :].astype(F32), 0.0) * col(5 - j)
            xc = (col(6) + col(2) * xb.astype(F32) + hist).astype(BF)
            rg = jax.nn.sigmoid(lax.dot_general(wa_ref[layer, h], xc, TN, preferred_element_type=F32) + col(7))
            ig = jax.nn.sigmoid(lax.dot_general(wi_ref[layer, h], xc, TN, preferred_element_type=F32) + col(8))
            a = jnp.exp(rg * col(9))
            sc = jnp.sqrt(1.0 - a * a)
            a = jnp.where(fresh, 0.0, a)
            sc = jnp.where(fresh, 1.0, sc)
            hn = a * lru_s[rows, :] + sc * ig * xc.astype(F32)
            lru_s[rows, :] = hn
            ht_s[rows, :] = (hn * yb).astype(BF)
        for cp in state_out[layer]:
            cp.start()
        ht_s[LC:, :] = jnp.zeros((64, B), BF)
        h_s[:, :LC + 64] = ht_s[...].T

        def produce(k, u):
            if u == 0:
                rec_out[layer].wait(k)
            net.dots(2 * k + u, h_s.at[:, :LC], wob.at[:, chunk(2 * k + u)])

        net.reduce_scatter(produce, rb_ref, layer)
        net.gather_start(rms(net.xown[...], f(sc_ref)[layer, 1:2, :]))
        for cp in state_out[layer]:
            cp.wait()
        if layer == 0:
            rec_out[1].begin()
            for cp in state_in[1]:
                cp.start()
        mlp_up(net, up, 4 * layer, wu, acc, h_s, b1_ref, b2_ref, layer)
        mlp_down(net, down, 4 * layer, wdb, h_s, mb_ref, layer)
        net.gather_start(rms(net.xown[...], f(sc_ref)[layer + 1, 0:1, :]))

    xo_ref[...] = net.xown[...]

    def use_q(start, size):
        k = 8 + start // KC
        off = start % KC
        if off == 0:
            up.wait(k)
        ng = net.n[:, start:start + size]
        for j in range(3):
            a = jnp.dot(ng, wu[k % SLOTS, 0, off:off + size, 256 * j:256 * j + 256], preferred_element_type=F32)
            acc[j] = a if start == 0 else acc[j] + a
        if off + size == KC:
            up.fill(k + 1)

    net.gathered(use_q)
    for h in range(4):
        q_ref[:, 128 * h:128 * h + 128] = rope(acc[h // 2, :, 128 * (h % 2):128 * (h % 2) + 128], (keep_ref, turn_ref)).astype(BF)
    k_ref[...] = rope(acc[2, :, 0:128], (keep_ref, turn_ref)).astype(BF)
    v_ref[...] = acc[2, :, 128:256].astype(BF)


def first_layers(x, scale, wxt, wyt, convt, lrut, wa, wi, bx, by, cw, cb, ba, bi, sp, tok, wout, rb, w1, b1, w2, b2, wd, mb, wq, wk, wv, keep, turn):
    return pl.pallas_call(
        kernel_a,
        name='first_layers',
        out_shape=(jax.ShapeDtypeStruct((B, 4 * HD), BF), jax.ShapeDtypeStruct((B, HD), BF), jax.ShapeDtypeStruct((B, HD), BF), jax.ShapeDtypeStruct((32, D), BF),
                   jax.ShapeDtypeStruct(convt.shape, BF), jax.ShapeDtypeStruct(lrut.shape, F32)),
        in_specs=[ANY, VM, ANY, ANY, ANY, ANY, VM, VM] + [VM] * 7 + [VM, ANY, VM, ANY, VM, ANY, VM, ANY, VM, ANY, ANY, ANY, VM, VM],
        out_specs=(VM, VM, VM, VM, ANY, ANY),
        scratch_shapes=LINK_SCRATCH + [
            pltpu.VMEM((SLOTS, 2, KC, FC), BF), pltpu.VMEM((SLOTS, FC, KC), BF), pltpu.VMEM((2, LC, D), BF), pltpu.VMEM((LC, D), BF),
            pltpu.VMEM((12, B, 256), F32), pltpu.VMEM((B, FC), BF), pltpu.VMEM((3, LC, B), BF), pltpu.VMEM((LC, B), BF), pltpu.VMEM((LC, B), F32),
            pltpu.VMEM((LC + 64, B), BF), pltpu.VMEM((16, LC + 64), F32), pltpu.VMEM((LC + 64, 16), F32),
            pltpu.SemaphoreType.DMA((SLOTS, 3)), pltpu.SemaphoreType.DMA((SLOTS,)), pltpu.SemaphoreType.DMA((2, NK)), pltpu.SemaphoreType.DMA((NK,)),
            pltpu.SemaphoreType.DMA((2,)), pltpu.SemaphoreType.DMA((3,)), pltpu.SemaphoreType.DMA,
        ],
        compiler_params=pltpu.CompilerParams(collective_id=0, has_side_effects=True, vmem_limit_bytes=67043328),
        cost_estimate=pl.CostEstimate(flops=30 * 10**9, bytes_accessed=400 * 10**6, transcendentals=0),
    )(x.reshape(4, 2, 32, D), scale, wxt, wyt, convt, lrut, wa, wi, bx, by, cw, cb, ba, bi, sp, tok, wout, rb, w1, b1, w2, b2, wd, mb, wq, wk, wv, keep, turn)


def kernel_b(o_ref, x_ref, wo, bo_ref, sc_ref, w1, b1_ref, w2, b2_ref, wd, mb_ref, out_ref, *scratch):
    net = Links(*scratch[:NLINK])
    wu, wdb, wob, acc, h_s, us, ds, os, ls = scratch[NLINK:]
    f = lambda ref: ref[...].astype(F32)
    load_o = wide_stream(wo, wob, os)
    up = Ring([up_group(g, 2, g, w1, w2, wu, us) for g in range(NK)], SLOTS)
    down = down_stream(2, 1, wd, wdb, ds)
    load_o.begin()
    up.fill(0)
    down.begin()
    net.enter()
    net.xown[...] = x_ref[...]

    def produce(k, u):
        if u == 0:
            load_o.wait(k)
        net.dots(2 * k + u, o_ref, wob.at[:, chunk(2 * k + u)])

    net.reduce_scatter(produce, bo_ref, 0)
    net.gather_start(rms(net.xown[...], f(sc_ref)[2, 1:2, :]))
    mlp_up(net, up, 0, wu, acc, h_s, b1_ref, b2_ref, 2)
    mlp_down(net, down, 0, wdb, h_s, mb_ref, 2)
    net.gather_start(net.xown[...])
    stores = []

    def use(start, size):
        cp = pltpu.make_async_copy(net.n.at[:, start:start + size], out_ref.at[:, start:start + size], ls.at[len(stores)])
        cp.start()
        stores.append(cp)

    net.gathered(use)
    for cp in stores:
        cp.wait()


def last_layer(o, x_own, wo, bo, scale, w1, b1, w2, b2, wd, mb):
    return pl.pallas_call(
        kernel_b,
        name='last_layer',
        out_shape=jax.ShapeDtypeStruct((B, D), BF),
        in_specs=[VM, VM, ANY, VM, VM, ANY, VM, ANY, VM, ANY, VM],
        out_specs=ANY,
        scratch_shapes=LINK_SCRATCH + [
            pltpu.VMEM((SLOTS, 2, KC, FC), BF), pltpu.VMEM((SLOTS, FC, KC), BF), pltpu.VMEM((512, D), BF),
            pltpu.VMEM((12, B, 256), F32), pltpu.VMEM((B, FC), BF),
            pltpu.SemaphoreType.DMA((SLOTS, 3)), pltpu.SemaphoreType.DMA((SLOTS,)), pltpu.SemaphoreType.DMA((G,)), pltpu.SemaphoreType.DMA((G,)),
        ],
        compiler_params=pltpu.CompilerParams(collective_id=1, has_side_effects=True, vmem_limit_bytes=67043328),
        cost_estimate=pl.CostEstimate(flops=12 * 10**9, bytes_accessed=200 * 10**6, transcendentals=0),
    )(o, x_own, wo, bo, scale, w1, b1, w2, b2, wd, mb)


RA = 8
NB = 6
STEPS = B // RA


def attn_kernel(tok_ref, q_ref, kn_ref, vn_ref, slot_ref, k_ref, v_ref, o_ref, ko_ref, vo_ref, so_ref, kb, vb, s_s, q_s, o_s, isem, osem):
    lane = lax.broadcasted_iota(jnp.int32, (1, W), 1)
    sub = lax.broadcasted_iota(jnp.int32, (16, HD), 0)

    def copies(step, out):
        b = lax.rem(step, NB)
        rows = pl.ds(pl.multiple_of(step * RA, RA), RA)
        if out:
            return [pltpu.make_async_copy(kb.at[b], ko_ref.at[rows], osem.at[0, b]), pltpu.make_async_copy(vb.at[b], vo_ref.at[rows], osem.at[1, b])]
        return [pltpu.make_async_copy(k_ref.at[rows], kb.at[b], isem.at[0, b]), pltpu.make_async_copy(v_ref.at[rows], vb.at[b], isem.at[1, b])]

    def start(step):
        for cp in copies(step, False):
            cp.start()

    lax.fori_loop(0, NB - 2, lambda step, c: (start(step), c)[1], 0)

    def step_fn(i, carry):
        b = lax.rem(i, NB)
        rows = pl.ds(pl.multiple_of(i * RA, RA), RA)
        ahead = i + NB - 2

        @pl.when(ahead < STEPS)
        def _():
            @pl.when(ahead >= NB)
            def _():
                for cp in copies(ahead - NB, True):
                    cp.wait()
            start(ahead)

        for cp in copies(i, False):
            cp.wait()
        kn = kn_ref[rows, :].astype(F32)
        vn = vn_ref[rows, :].astype(F32)
        for h in range(4):
            q_s[pl.ds(h, RA, stride=4), :] = q_ref[rows, 128 * h:128 * h + 128].astype(F32)
        slots = slot_ref[rows, :]
        new_rows = []
        for r in range(RA):
            tp = tok_ref[i * RA + r]
            slot = lax.rem(tp, W)
            base = pl.multiple_of((slot // 16) * 16, 16)
            hit = sub == (slot - base)
            spot = pl.ds(base, 16)
            kb[b, r, spot, :] = jnp.where(hit, kn[r:r + 1], kb[b, r, spot, :].astype(F32)).astype(BF)
            vb[b, r, spot, :] = jnp.where(hit, vn[r:r + 1], vb[b, r, spot, :].astype(F32)).astype(BF)
            sn = jnp.where(lane == slot, tp, slots[r:r + 1])
            new_rows.append((tp, sn))
        for r in range(RA):
            tp, sn = new_rows[r]
            so_ref[pl.ds(i * RA + r, 1), :] = sn
            age = tp - sn
            valid = (sn >= 0) & (age >= 0) & (age < W)
            s = lax.dot_general(q_s[4 * r:4 * r + 4, :].astype(BF), kb[b, r], NT, preferred_element_type=F32) * (HD ** -0.5)
            s_s[4 * r:4 * r + 4, :] = jnp.where(valid, s, -jnp.inf)
        s = s_s[...]
        e = jnp.exp(s - jnp.max(s, axis=-1, keepdims=True))
        s_s[...] = e / jnp.sum(e, axis=-1, keepdims=True)
        for r in range(RA):
            o_s[4 * r:4 * r + 4, :] = jnp.dot(s_s[4 * r:4 * r + 4, :].astype(BF), vb[b, r], preferred_element_type=F32)
        for h in range(4):
            o_ref[rows, 128 * h:128 * h + 128] = o_s[pl.ds(h, RA, stride=4), :].astype(BF)
        for cp in copies(i, True):
            cp.start()
        return carry

    lax.fori_loop(0, STEPS, step_fn, 0)
    for step in range(STEPS - NB, STEPS):
        for cp in copies(step, True):
            cp.wait()


def attend(tok, q, kn, vn, slot_pos, kc, vc):
    return pl.pallas_call(
        attn_kernel,
        name='attend',
        in_specs=[pl.BlockSpec(memory_space=pltpu.SMEM), VM, VM, VM, VM, ANY, ANY],
        out_specs=(VM, ANY, ANY, VM),
        out_shape=(jax.ShapeDtypeStruct((B, 4 * HD), BF), jax.ShapeDtypeStruct(kc.shape, BF), jax.ShapeDtypeStruct(vc.shape, BF), jax.ShapeDtypeStruct(slot_pos.shape, jnp.int32)),
        scratch_shapes=[pltpu.VMEM((NB, RA, W, HD), BF), pltpu.VMEM((NB, RA, W, HD), BF), pltpu.VMEM((4 * RA, W), F32), pltpu.VMEM((4 * RA, HD), F32), pltpu.VMEM((4 * RA, HD), F32),
                        pltpu.SemaphoreType.DMA((2, NB)), pltpu.SemaphoreType.DMA((2, NB))],
        cost_estimate=pl.CostEstimate(flops=4 * B * 4 * W * HD, bytes_accessed=8 * B * W * HD, transcendentals=0),
    )(tok, q, kn, vn, slot_pos, kc, vc)


def rope_tables(tok_pos):
    quarter = HD // 4
    lane = lax.broadcasted_iota(jnp.int32, (1, HD), 1)
    inv_freq = ROPE_BASE ** (-(lane % quarter).astype(F32) / quarter)
    angles = tok_pos.astype(F32)[:, None] * inv_freq
    cos, sin = jnp.cos(angles), jnp.sin(angles)
    return jnp.where(lane < 2 * quarter, cos, 1.0), jnp.where(lane < quarter, -sin, jnp.where(lane < 2 * quarter, sin, 0.0))


def io_specs():
    in_specs = (P('dp', None), P('dp'), P(None, 'dp', None, 'tp'), P(None, 'dp', 'tp'), P('dp', None, None), P('dp', None, None), P('dp', None),
                P(), P(None, None, 'tp'), P(None, 'tp'), P(None, None, 'tp'), P(None, 'tp'), P(None, None, 'tp'), P(None, 'tp'),
                P(None, 'tp', None, None), P(None, 'tp'), P(None, 'tp', None, None), P(None, 'tp'), P(None, 'tp'), P(None, 'tp', None), P(),
                P(None, 'tp'), P(), P(), P('tp', None), P(),
                P(None, None, 'tp'), P(None, 'tp'), P(None, None, 'tp'), P(None, 'tp'), P(None, 'tp', None), P())
    out_specs = (P('dp', None), P(None, 'dp', None, 'tp'), P(None, 'dp', 'tp'), P('dp', None, None), P('dp', None, None), P('dp', None))
    return in_specs, out_specs


def solution(mesh):
    in_specs, out_specs = io_specs()

    def local_step(x_in, tok_pos, conv_state, lru_state, k_cache, v_cache, slot_pos, norm_scale, rec_wx, rec_bx, rec_wy, rec_by, conv_w, conv_b, gate_wa, gate_ba, gate_wi, gate_bi, a_param, rec_wout, rec_bout, attn_wq, attn_wk, attn_wv, attn_wo, attn_bo, mlp_w1, mlp_b1, mlp_w2, mlp_b2, mlp_wd, mlp_bd):
        wxt = jnp.swapaxes(rec_wx, 1, 2)
        wyt = jnp.swapaxes(rec_wy, 1, 2)
        convt = jnp.transpose(conv_state, (0, 2, 3, 1))
        lrut = jnp.swapaxes(lru_state, 1, 2)
        tok_row = tok_pos[None, :]
        tab = rope_tables(tok_pos)

        q, kn, vn, x_own, convs, lrus = first_layers(x_in, norm_scale, wxt, wyt, convt, lrut, gate_wa, gate_wi, rec_bx, rec_by, conv_w, conv_b, gate_ba, gate_bi, -8.0 * jax.nn.softplus(a_param), tok_row, rec_wout, rec_bout, mlp_w1, mlp_b1, mlp_w2, mlp_b2, mlp_wd, mlp_bd, attn_wq, attn_wk, attn_wv, *tab)
        o, k_next, v_next, slot_next = attend(tok_pos, q, kn, vn, slot_pos, k_cache, v_cache)
        x = last_layer(o, x_own, attn_wo, attn_bo[None, :], norm_scale, mlp_w1, mlp_b1, mlp_w2, mlp_b2, mlp_wd, mlp_bd)
        conv_out = jnp.transpose(convs, (0, 3, 1, 2))
        lru_out = jnp.swapaxes(lrus, 1, 2)
        return (x, conv_out, lru_out, k_next, v_next, slot_next)

    return jax.shard_map(local_step, mesh=mesh, in_specs=in_specs, out_specs=out_specs, check_vma=False)
```

time: 339 us -> 321 us (0.947)
  Pallas kernels: 318 us -> 309 us
  local copies, waits for them, and re-layouts: 11.9 us -> 7.04 us
  other arithmetic: 7.2 us -> 3.26 us
    pallas_call x1, Pallas kernels: 97.6 us -> 90.2 us  [attend(): pl.pallas_call(attn_kernel, name='attend', in_specs=[pl.BlockSpec(memory_...]
    unnamed x5 -> x0, other arithmetic: 3.46 us -> none
    unnamed x12 -> x7, local copies, waits for them, and re-layouts: 7.46 us -> 5.73 us
where the time goes in v3:
time: 321 us; the launch traced here: 320 us
  Pallas kernels  309 us (96%)
  local copies, waits for them, and re-layouts  7.04 us (2%)
  other arithmetic  3.26 us (1%)
    pallas_call x1, Pallas kernels, first_layers(): pl.pallas_call(kernel_a, name='first_layers', out_shape=(jax.ShapeDtypeSt...  150 us
    pallas_call x1, Pallas kernels, attend(): pl.pallas_call(attn_kernel, name='attend', in_specs=[pl.BlockSpec(memory_...  90.2 us
    pallas_call x1, Pallas kernels, last_layer(): pl.pallas_call(kernel_b, name='last_layer', out_shape=jax.ShapeDtypeStruc...  69.5 us

profile of v3, /device:TPU:1, one launch (start us, length us, event | category | flops | bytes accessed | tf_op | source)
XLA Modules:
  0.0 320.3 jit_solution(18297448697506276814)
XLA Ops:
  0.6 0.7 convert_element_type.11
  1.3 1.3 fusion.4.sp_ref
  2.6 1.3 broadcast_in_dim.40.bo_ref
  4.0 1.3 fusion.2
  5.2 149.6 %first_layers.1 = (bf16[256,512]{1,0:T(8,128)(2,1)}, bf16[256,128]{1,0:T(8,128)(2,1)}, bf16[256,128]{1,0:T(8,128)(2,1)}, bf16[32,4096]{1,0:T(8,128)(2,1)}, bf16[...) custom-call(bf16[4,2,32,4096]{3,2,1,0:T(8,128)(2,1)} %bitcast.12, bf16[3,2,4096]{2,1,0:T(2,128)(2,1)} %sc_ref.3, ...), custom_call_target="tpu_custom_call" | custom-call | flops 30000001024 | bytes 400000000 | tf_op jit(solution)/shard_map/first_layers/pallas_call | solution.py:426
  154.8 90.2 %attend.1 = (bf16[256,512]{1,0:T(8,128)(2,1)}, bf16[256,1024,128]{2,1,0:T(8,128)(2,1)}, bf16[256,1024,128]{2,1,0:T(8,128)(2,1)}, s32[256,1024]{1,0:T(8,128)}) custom-call(s32[256]{0:T(256)} %tok_ref.1, bf16[256,512]{1,0:T(8,128)(2,1)} %get-tuple-element.16.q_ref, bf16[256,128]{1,0:T(8,128)(2,1)} %get-tuple-element.17.kn_ref, ...), custom_call_target="tpu_custom_call" | custom-call | flops 536870912 | bytes 268435456 | tf_op jit(solution)/shard_map/attend/pallas_call | solution.py:575
  245.0 69.5 %last_layer.1 = bf16[256,4096]{1,0:T(8,128)(2,1)} custom-call(bf16[256,512]{1,0:T(8,128)(2,1)} %get-tuple-element.19.o_ref, bf16[32,4096]{1,0:T(8,128)(2,1)} %get-tuple-element.20.x_ref, bf16[512,4096]{1,0:T(8,128)(2,1)} %wo.1, bf16[1,4096]{1,0:T(2,128)(2,1)} %broadcast_in_dim.40.bo_ref, bf16[3,2,4096]{2,1,0:T(2,128)(2,1)} %sc_ref.3, ...), custom_call_target="tpu_custom_call" | custom-call | flops 12000000000 | bytes 200000000 | tf_op jit(solution)/shard_map/last_layer/pallas_call | solution.py:481
  314.5 0.0 copy-start
  314.5 0.0 copy-start.1
  314.5 3.3 %copy.41 = bf16[256,4096]{1,0:T(8,128)(2,1)} copy(bf16[256,4096]{1,0:T(8,128)(2,1)} %last_layer.1) | data formatting | bytes 4194304
  317.8 0.0 copy-done
  317.8 1.3 copy.42
  319.2 0.0 copy-done.1
  319.2 1.1 copy.43
  (2 shorter events, 0.0 us)
Async XLA Ops:
  314.5 3.3 %copy-start = (bf16[2,3,704,256]{3,2,1,0:T(8,128)(2,1)S(1)}, bf16[2,3,704,256]{3,2,1,0:T(8,128)(2,1)}, u32[]{:S(2)}) copy-start(bf16[2,3,704,256]{3,2,1,0:T(8,128)(2,1)} %get-tuple-element.21) | copy-start | bytes 6488068
  314.5 4.6 %copy-start.1 = (f32[2,704,256]{2,1,0:T(8,128)S(1)}, f32[2,704,256]{2,1,0:T(8,128)}, u32[]{:S(2)}) copy-start(f32[2,704,256]{2,1,0:T(8,128)} %get-tuple-element.22) | copy-start | bytes 4325380

commit v4 on v3

v4 whole, which is shorter than its diff:
```python
import functools

import jax
import jax.numpy as jnp
from jax import lax
from jax.experimental import pallas as pl
from jax.experimental.pallas import tpu as pltpu
from jax.sharding import PartitionSpec as P

ROPE_BASE = 10000.0
NORM_EPS = 1e-6
MESH = pl.DeviceIdType.MESH
BF = jnp.bfloat16
F32 = jnp.float32
ANY = pl.BlockSpec(memory_space=pl.ANY)
VM = pl.BlockSpec(memory_space=pltpu.VMEM)
B = 256
D = 4096
LC = 704
FC = 1536
W = 1024
HD = 128
G = 4
HB = 128
OR = 16
GC = D // G


def rms(x, scale):
    xf = x.astype(F32)
    mean_sq = jnp.mean(xf * xf, axis=-1, keepdims=True)
    return (xf * lax.rsqrt(mean_sq + NORM_EPS) * (1.0 + scale.astype(F32))).astype(BF)


NT = (((1,), (1,)), ((), ()))
TN = (((0,), (0,)), ((), ()))
DMA = pltpu.SemaphoreType.DMA


def chunk(g):
    return pl.ds(pl.multiple_of(g * GC, GC), GC)


class Links:
    def __init__(self, part, recv1, recv2, own, n, xown, s1s, s1r, s2s, s2r, s3s, s3r, s4s, s4r):
        self.part, self.recv1, self.recv2, self.own, self.n, self.xown = part, recv1, recv2, own, n, xown
        self.s1s, self.s1r, self.s2s, self.s2r, self.s3s, self.s3r, self.s4s, self.s4r = s1s, s1r, s2s, s2r, s3s, s3r, s4s, s4r
        t = lax.axis_index('tp')
        y, x = t // 4, (t // 2) % 2
        self.c = t % 2
        self.q = 2 * y + x
        self.partner = 2 * self.q + 1 - self.c
        self.chips = [2 * y + (1 - x), 2 * (1 - y) + x, 2 * (1 - y) + (1 - x)]
        self.peers = [2 * qd + self.c for qd in self.chips]

    def enter(self):
        barrier = pltpu.get_barrier_semaphore()
        for dev in [self.partner] + self.peers:
            pl.semaphore_signal(barrier, inc=1, device_id={'tp': dev}, device_id_type=MESH)
        pl.semaphore_wait(barrier, 4)

    def remote(self, src, dst, ss, rs, dev):
        return pltpu.make_async_remote_copy(src_ref=src, dst_ref=dst, send_sem=ss, recv_sem=rs, device_id={'tp': dev}, device_id_type=MESH)

    def to_partner(self, h, g):
        return self.remote(self.part.at[h, :, 1 - self.c, :, chunk(g)], self.recv1.at[h, :, :, chunk(g)], self.s1s.at[h, g], self.s1r.at[h, g], self.partner)

    def to_owner(self, h, g, k):
        return self.remote(self.part.at[h, self.chips[k], self.c, :, chunk(g)], self.recv2.at[h, k, :, chunk(g)], self.s2s.at[h, g, k], self.s2r.at[h, g, k], self.peers[k])

    def place(self, h, dev, g):
        return self.n.at[h, pl.ds(pl.multiple_of(dev * OR, OR), OR), chunk(g)]

    def from_own(self, h, g, k):
        ref = self.place(h, 2 * self.q + self.c, g)
        return self.remote(ref, ref, self.s3s.at[h, g, k], self.s3r.at[h, g, k], self.peers[k] if k < 3 else self.partner)

    def pass_on(self, h, g, k):
        ref = self.place(h, self.peers[k], g)
        return self.remote(ref, ref, self.s4s.at[h, g, k], self.s4r.at[h, g, k], self.partner)

    def scatter(self, h, lhs, rhs, before=None, after=None):
        c, q, chips, part = self.c, self.q, self.chips, self.part

        def pair(g):
            cols = chunk(g)
            self.to_partner(h, g).wait_recv()
            for k in (2, 0, 1):
                s = part[h, chips[k], c, :, cols].astype(F32) + self.recv1[h, chips[k], :, cols].astype(F32)
                part[h, chips[k], c, :, cols] = s.astype(BF)
                self.to_owner(h, g, k).start()
            self.own[h, :, cols] = part[h, q, c, :, cols].astype(F32) + self.recv1[h, q, :, cols].astype(F32)

        def step(g, carry):
            if before is not None:
                before(g)
            left = lhs()
            for p in range(2):
                cols = pl.ds(pl.multiple_of(g * GC + p * 512, 512), 512)
                out = jnp.dot(left, rhs(g, p), preferred_element_type=F32)
                part[h, :, :, :, cols] = out.astype(BF).reshape(4, 2, OR, 512)
            if after is not None:
                after(g)
            self.to_partner(h, g).start()

            @pl.when(g > 0)
            def _():
                pair(g - 1)

            return carry

        lax.fori_loop(0, G, step, 0)
        pair(G - 1)

    def finish(self, h, bias_ref, layer, scale):
        def final(g, carry):
            cols = chunk(g)
            tot = self.own[h, :, cols]
            for k in range(3):
                self.to_owner(h, g, k).wait_recv()
                tot = tot + self.recv2[h, k, :, cols].astype(F32)
            bias = bias_ref[:, cols].astype(F32)[layer:layer + 1]
            self.xown[h, :, cols] = (self.xown[h, :, cols].astype(F32) + tot.astype(BF).astype(F32) + bias).astype(BF)
            return carry

        lax.fori_loop(0, G, final, 0)

        def sent(g, carry):
            self.to_partner(h, g).wait_send()
            for k in range(3):
                self.to_owner(h, g, k).wait_send()
            return carry

        lax.fori_loop(0, G, sent, 0)
        rows = self.xown[h]
        self.n[h, pl.ds(pl.multiple_of((2 * self.q + self.c) * OR, OR), OR), :] = rows if scale is None else rms(rows, scale)

        def send(i, carry):
            for k in (2, 0, 1, 3):
                self.from_own(h, order(h, i), k).start()
            return carry

        lax.fori_loop(0, G, send, 0)

    def gathered(self, h, use, fresh=False):
        def step(i, carry):
            if not fresh:
                @pl.when(i < G)
                def _():
                    g = order(h, i)
                    for k in range(3):
                        self.from_own(h, g, k).wait_recv()
                        self.pass_on(h, g, k).start()

            @pl.when(i > 0)
            def _():
                g = order(h, i - 1)
                if not fresh:
                    self.from_own(h, g, 3).wait_recv()
                    for k in range(3):
                        self.pass_on(h, g, k).wait_recv()
                use(i - 1, g)

            return carry

        lax.fori_loop(0, G + 1, step, 0)
        if fresh:
            return

        def sent(g, carry):
            for k in range(4):
                self.from_own(h, g, k).wait_send()
            for k in range(3):
                self.pass_on(h, g, k).wait_send()
            return carry

        lax.fori_loop(0, G, sent, 0)


def order(h, i):
    return lax.rem(i + 2 * h, G)


LINK_SCRATCH = [
    pltpu.VMEM((2, 4, 2, OR, D), BF), pltpu.VMEM((2, 4, OR, D), BF), pltpu.VMEM((2, 3, OR, D), BF),
    pltpu.VMEM((2, OR, D), F32), pltpu.VMEM((2, HB, D), BF), pltpu.VMEM((2, OR, D), BF),
    DMA((2, G)), DMA((2, G)), DMA((2, G, 3)), DMA((2, G, 3)), DMA((2, G, 4)), DMA((2, G, 4)), DMA((2, G, 3)), DMA((2, G, 3)),
]
NLINK = len(LINK_SCRATCH)

SLOTS = 5
SLAB = 512
LOADS = 12


class Slabs:
    def __init__(self, groups, wu):
        self.groups, self.wu = groups, wu

    def start(self, load):
        for j, group in enumerate(self.groups):
            @pl.when((load >= LOADS * j) & (load < LOADS * (j + 1)))
            def _():
                for cp in group(load - LOADS * j, load):
                    cp.start()

    def begin(self):
        def body(load, carry):
            self.start(load)
            return carry

        lax.fori_loop(0, SLOTS, body, 0)

    def use(self, h, j, i, body):
        load = LOADS * j + 4 * h + i

        @pl.when(i >= 4 * h)
        def _():
            for cp in self.groups[j](load - LOADS * j, load):
                cp.wait()

        body(lax.rem(load, SLOTS))

        @pl.when((i < 4) | (h == 1))
        def _():
            self.start(load + SLOTS)


def slab_rows(k):
    return pl.ds(pl.multiple_of(lax.rem(k, 8) * SLAB, SLAB), SLAB)


def mlp_slabs(layer, w1, w2, wu, sems):
    def group(k, load):
        s = lax.rem(load, SLOTS)
        return [pltpu.make_async_copy(w1.at[layer, slab_rows(k), :], wu.at[s, 0], sems.at[s, 0]), pltpu.make_async_copy(w2.at[layer, slab_rows(k), :], wu.at[s, 1], sems.at[s, 1])]

    return group


def qkv_slabs(wq, wk, wv, wu, sems):
    def group(k, load):
        s = lax.rem(load, SLOTS)
        return [pltpu.make_async_copy(w.at[slab_rows(k), :], wu.at[s, 0, :, lo:hi], sems.at[s, j]) for j, (w, lo, hi) in enumerate(((wq, 0, 512), (wk, 512, 640), (wv, 640, 768)))]

    return group


def wide(src, dst, sems, g):
    return pltpu.make_async_copy(src.at[:, chunk(g)], dst.at[:, chunk(g)], sems.at[g])


def mlp_up(net, h, slabs, j, acc, h_s, b1_ref, b2_ref, layer):
    acc[...] = jnp.zeros_like(acc)

    def use(i, g):
        for e in range(2):
            def body(slot):
                ng = net.n[h, :, pl.ds(pl.multiple_of(g * GC + e * SLAB, SLAB), SLAB)]
                for half in range(2):
                    for lo in range(0, FC, 512):
                        acc[half, :, lo:lo + 512] += jnp.dot(ng, slabs.wu[slot, half, :, lo:lo + 512], preferred_element_type=F32)

            slabs.use(h, j, 2 * i + e, body)

    net.gathered(h, use)
    b1 = b1_ref[...].astype(F32)[layer:layer + 1]
    b2 = b2_ref[...].astype(F32)[layer:layer + 1]
    for lo in range(0, FC, 256):
        lanes = slice(lo, lo + 256)
        h_s[:, lanes] = (jax.nn.gelu(acc[0, :, lanes] + b1[:, lanes], approximate=True) * (acc[1, :, lanes] + b2[:, lanes])).astype(BF)


def mlp(net, slabs, j, acc, h_s, b1_ref, b2_ref, wd, wdb, ds, layer, last):
    for h in range(2):
        mlp_up(net, h, slabs, j, acc, h_s, b1_ref, b2_ref, layer)

        def before(g):
            if h == 0:
                wide(wd.at[layer], wdb, ds, g).wait()

        def after(g):
            if h == 1 and not last:
                wide(wd.at[layer + 1], wdb, ds, g).start()

        net.scatter(h, lambda: h_s[...], lambda g, p: wdb[:, pl.ds(pl.multiple_of(g * GC + p * 512, 512), 512)], before, after)


def rope(v, keep, turn):
    lane = lax.broadcasted_iota(jnp.int32, v.shape, 1)
    return v * keep + jnp.where(lane < 32, pltpu.roll(v, 96, 1), pltpu.roll(v, 32, 1)) * turn


def kernel_a(x_ref, sc_ref, wx, wy, conv, lru, wa_ref, wi_ref, bx_ref, by_ref, cw_ref, cb_ref, ba_ref, bi_ref, sp_ref, tok_ref, wout, rb_ref, w1, b1_ref, w2, b2_ref, wd, mb_ref, wq, wk, wv, keep_ref, turn_ref,
             q_ref, k_ref, v_ref, xo_ref, conv_out, lru_out, *scratch):
    net = Links(*scratch[:NLINK])
    wu, wdb, wxb, wob, acc, accr, h_s, conv_s, xb_s, lru_s, ht_s, prow, pcol, us, ds, xs, os, ss, ts, ls = scratch[NLINK:]
    scale = lambda l, j: sc_ref[...].astype(F32)[l, j:j + 1, :]
    rec_in = lambda l, g: [pltpu.make_async_copy(w.at[l, :, chunk(g)], wxb.at[j, :, chunk(g)], xs.at[j, g]) for j, w in enumerate((wx, wy))]
    state_in = lambda l: [pltpu.make_async_copy(conv.at[l], conv_s, ss.at[0]), pltpu.make_async_copy(lru.at[l], lru_s, ss.at[1])]
    state_out = lambda l: [pltpu.make_async_copy(conv_s.at[1:3], conv_out.at[l, 0:2], ts.at[0]), pltpu.make_async_copy(xb_s, conv_out.at[l, 2], ts.at[1]), pltpu.make_async_copy(lru_s, lru_out.at[l], ts.at[2])]
    slabs = Slabs([mlp_slabs(0, w1, w2, wu, us), mlp_slabs(1, w1, w2, wu, us), qkv_slabs(wq, wk, wv, wu, us)], wu)

    load_x = pltpu.make_async_copy(x_ref, net.part, ls)
    load_x.start()

    def load_rec(l):
        for g in range(G):
            for cp in rec_in(l, g):
                cp.start()

    load_rec(0)
    for cp in state_in(0):
        cp.start()
    for g in range(G):
        wide(wout.at[0], wob, os, g).start()
    net.enter()
    load_x.wait()
    for h in range(2):
        for chip in range(4):
            net.n[h, 2 * OR * chip:2 * OR * (chip + 1), :] = rms(net.part[h, chip].reshape(2 * OR, D), scale(0, 0))
        net.xown[h] = net.part[h, net.q, net.c]
    tok = tok_ref[...]

    for layer in range(2):
        row = lambda ref: ref[...].astype(F32)[layer:layer + 1]
        cw = cw_ref[...].astype(F32)
        params = [row(bx_ref), row(by_ref)] + [cw[layer, j:j + 1, :] for j in range(4)] + [row(cb_ref), row(ba_ref), row(bi_ref), row(sp_ref)]
        for j, p in enumerate(params):
            prow[j:j + 1, 0:LC] = p
        pcol[...] = prow[...].T

        for h in range(2):
            lanes = slice(HB * h, HB * (h + 1))
            accr[...] = jnp.zeros_like(accr)

            def use(i, g):
                if h == 0:
                    for cp in rec_in(layer, g):
                        cp.wait()
                ng = net.n[h, :, chunk(g)]
                for half in range(2):
                    accr[half] += lax.dot_general(wxb[half, :, chunk(g)], ng, NT, preferred_element_type=F32)

            net.gathered(h, use, fresh=layer == 0)
            if h == 0:
                for cp in state_in(layer):
                    cp.wait()
            elif layer == 0:
                slabs.begin()
                for g in range(G):
                    wide(wd.at[0], wdb, ds, g).start()
            tk = tok[:, lanes]
            fresh = tk == 0
            for b in range(4):
                rows = slice(176 * b, 176 * b + 176)
                pc = pcol[rows, :]
                col = lambda k: pc[:, k:k + 1]
                xb = (accr[0, rows, :] + col(0)).astype(BF)
                yb = jax.nn.gelu(accr[1, rows, :] + col(1), approximate=True)
                xb_s[rows, lanes] = xb
                hist = jnp.zeros((176, HB), F32)
                for j in range(3):
                    hist = hist + jnp.where(tk >= 3 - j, conv_s[j, rows, lanes].astype(F32), 0.0) * col(5 - j)
                xc = (col(6) + col(2) * xb.astype(F32) + hist).astype(BF)
                rg = jax.nn.sigmoid(lax.dot_general(wa_ref[layer, b], xc, TN, preferred_element_type=F32) + col(7))
                ig = jax.nn.sigmoid(lax.dot_general(wi_ref[layer, b], xc, TN, preferred_element_type=F32) + col(8))
                a = jnp.exp(rg * col(9))
                sc = jnp.sqrt(1.0 - a * a)
                a = jnp.where(fresh, 0.0, a)
                sc = jnp.where(fresh, 1.0, sc)
                hn = a * lru_s[rows, lanes] + sc * ig * xc.astype(F32)
                lru_s[rows, lanes] = hn
                ht_s[rows, :] = (hn * yb).astype(BF)
            ht_s[LC:, :] = jnp.zeros((64, HB), BF)
            h_s[:, :LC + 64] = ht_s[...].T

            def before(g):
                if h == 0:
                    wide(wout.at[layer], wob, os, g).wait()

            net.scatter(h, lambda: h_s[:, :LC], lambda g, p: wob[:, pl.ds(pl.multiple_of(g * GC + p * 512, 512), 512)], before)
        for cp in state_out(layer):
            cp.start()
        if layer == 0:
            load_rec(1)
            for g in range(G):
                wide(wout.at[1], wob, os, g).start()
        for h in range(2):
            net.finish(h, rb_ref, layer, scale(layer, 1))
        for cp in state_out(layer):
            cp.wait()
        if layer == 0:
            for cp in state_in(1):
                cp.start()
        mlp(net, slabs, layer, acc, h_s, b1_ref, b2_ref, wd, wdb, ds, layer, layer == 1)
        for h in range(2):
            net.finish(h, mb_ref, layer, scale(layer + 1, 0))

    xo_ref[...] = net.xown[...]
    for h in range(2):
        acc[...] = jnp.zeros_like(acc)

        def use_q(i, g):
            for e in range(2):
                def body(slot):
                    ng = net.n[h, :, pl.ds(pl.multiple_of(g * GC + e * SLAB, SLAB), SLAB)]
                    acc[0, :, 0:768] += jnp.dot(ng, wu[slot, 0, :, 0:768], preferred_element_type=F32)

                slabs.use(h, 2, 2 * i + e, body)

        net.gathered(h, use_q)
        keep, turn = keep_ref[h], turn_ref[h]
        for b in range(4):
            q_ref[h, :, HD * b:HD * (b + 1)] = rope(acc[0, :, HD * b:HD * (b + 1)], keep, turn).astype(BF)
        k_ref[h] = rope(acc[0, :, 512:640], keep, turn).astype(BF)
        v_ref[h] = acc[0, :, 640:768].astype(BF)


def first_layers(x, scale, wxt, wyt, convt, lrut, wa, wi, bx, by, cw, cb, ba, bi, sp, tok, wout, rb, w1, b1, w2, b2, wd, mb, wq, wk, wv, keep, turn):
    return pl.pallas_call(
        kernel_a,
        name='first_layers',
        out_shape=(jax.ShapeDtypeStruct((2, HB, 4 * HD), BF), jax.ShapeDtypeStruct((2, HB, HD), BF), jax.ShapeDtypeStruct((2, HB, HD), BF), jax.ShapeDtypeStruct((2, OR, D), BF),
                   jax.ShapeDtypeStruct(convt.shape, BF), jax.ShapeDtypeStruct(lrut.shape, F32)),
        in_specs=[ANY, VM, ANY, ANY, ANY, ANY, VM, VM] + [VM] * 7 + [VM, ANY, VM, ANY, VM, ANY, VM, ANY, VM, ANY, ANY, ANY, VM, VM],
        out_specs=(VM, VM, VM, VM, ANY, ANY),
        scratch_shapes=LINK_SCRATCH + [
            pltpu.VMEM((SLOTS, 2, SLAB, FC), BF), pltpu.VMEM((FC, D), BF), pltpu.VMEM((2, LC, D), BF), pltpu.VMEM((LC, D), BF),
            pltpu.VMEM((2, HB, FC), F32), pltpu.VMEM((2, LC, HB), F32), pltpu.VMEM((HB, FC), BF), pltpu.VMEM((3, LC, B), BF), pltpu.VMEM((LC, B), BF), pltpu.VMEM((LC, B), F32),
            pltpu.VMEM((LC + 64, HB), BF), pltpu.VMEM((16, LC + 64), F32), pltpu.VMEM((LC + 64, 16), F32),
            DMA((SLOTS, 3)), DMA((G,)), DMA((2, G)), DMA((G,)), DMA((2,)), DMA((3,)), DMA,
        ],
        compiler_params=pltpu.CompilerParams(collective_id=0, has_side_effects=True, vmem_limit_bytes=67043328),
        cost_estimate=pl.CostEstimate(flops=30 * 10**9, bytes_accessed=400 * 10**6, transcendentals=0),
    )(x.reshape(2, 4, 2, OR, D), scale, wxt, wyt, convt, lrut, wa, wi, bx, by, cw, cb, ba, bi, sp, tok, wout, rb, w1, b1, w2, b2, wd, mb, wq, wk, wv, keep.reshape(2, HB, HD), turn.reshape(2, HB, HD))


def kernel_b(o_ref, x_ref, wo, bo_ref, sc_ref, w1, b1_ref, w2, b2_ref, wd, mb_ref, out_ref, *scratch):
    net = Links(*scratch[:NLINK])
    wu, wdb, wob, acc, h_s, us, ds, os, ls = scratch[NLINK:]
    for g in range(G):
        wide(wo, wob, os, g).start()
    slabs = Slabs([mlp_slabs(2, w1, w2, wu, us)], wu)
    slabs.begin()
    for g in range(G):
        wide(wd.at[2], wdb, ds, g).start()
    net.enter()
    net.xown[...] = x_ref[...]
    for h in range(2):
        def before(g):
            if h == 0:
                wide(wo, wob, os, g).wait()

        net.scatter(h, lambda: o_ref[h], lambda g, p: wob[:, pl.ds(pl.multiple_of(g * GC + p * 512, 512), 512)], before)
    for h in range(2):
        net.finish(h, bo_ref, 0, sc_ref[...].astype(F32)[2, 1:2, :])
    mlp(net, slabs, 0, acc, h_s, b1_ref, b2_ref, wd, wdb, ds, 2, True)
    for h in range(2):
        net.finish(h, mb_ref, 2, None)
    store = lambda h, g: pltpu.make_async_copy(net.n.at[h, :, chunk(g)], out_ref.at[h, :, chunk(g)], ls.at[h, g])
    for h in range(2):
        net.gathered(h, lambda i, g: store(h, g).start())
    for h in range(2):
        for g in range(G):
            store(h, g).wait()


def last_layer(o, x_own, wo, bo, scale, w1, b1, w2, b2, wd, mb):
    out = pl.pallas_call(
        kernel_b,
        name='last_layer',
        out_shape=jax.ShapeDtypeStruct((2, HB, D), BF),
        in_specs=[VM, VM, ANY, VM, VM, ANY, VM, ANY, VM, ANY, VM],
        out_specs=ANY,
        scratch_shapes=LINK_SCRATCH + [
            pltpu.VMEM((SLOTS, 2, SLAB, FC), BF), pltpu.VMEM((FC, D), BF), pltpu.VMEM((4 * HD, D), BF),
            pltpu.VMEM((2, HB, FC), F32), pltpu.VMEM((HB, FC), BF),
            DMA((SLOTS, 3)), DMA((G,)), DMA((G,)), DMA((2, G)),
        ],
        compiler_params=pltpu.CompilerParams(collective_id=1, has_side_effects=True, vmem_limit_bytes=67043328),
        cost_estimate=pl.CostEstimate(flops=12 * 10**9, bytes_accessed=200 * 10**6, transcendentals=0),
    )(o.reshape(2, HB, 4 * HD), x_own, wo, bo, scale, w1, b1, w2, b2, wd, mb)
    return out.reshape(B, D)


RA = 8
NB = 6
STEPS = B // RA


def attn_kernel(tok_ref, q_ref, kn_ref, vn_ref, slot_ref, k_ref, v_ref, o_ref, ko_ref, vo_ref, so_ref, kb, vb, s_s, q_s, o_s, isem, osem):
    lane = lax.broadcasted_iota(jnp.int32, (1, W), 1)
    sub = lax.broadcasted_iota(jnp.int32, (16, HD), 0)

    def copies(step, out):
        b = lax.rem(step, NB)
        rows = pl.ds(pl.multiple_of(step * RA, RA), RA)
        if out:
            return [pltpu.make_async_copy(kb.at[b], ko_ref.at[rows], osem.at[0, b]), pltpu.make_async_copy(vb.at[b], vo_ref.at[rows], osem.at[1, b])]
        return [pltpu.make_async_copy(k_ref.at[rows], kb.at[b], isem.at[0, b]), pltpu.make_async_copy(v_ref.at[rows], vb.at[b], isem.at[1, b])]

    def start(step):
        for cp in copies(step, False):
            cp.start()

    lax.fori_loop(0, NB - 2, lambda step, c: (start(step), c)[1], 0)

    def step_fn(i, carry):
        b = lax.rem(i, NB)
        rows = pl.ds(pl.multiple_of(i * RA, RA), RA)
        ahead = i + NB - 2

        @pl.when(ahead < STEPS)
        def _():
            @pl.when(ahead >= NB)
            def _():
                for cp in copies(ahead - NB, True):
                    cp.wait()
            start(ahead)

        for cp in copies(i, False):
            cp.wait()
        kn = kn_ref[rows, :].astype(F32)
        vn = vn_ref[rows, :].astype(F32)
        for h in range(4):
            q_s[pl.ds(h, RA, stride=4), :] = q_ref[rows, 128 * h:128 * h + 128].astype(F32)
        slots = slot_ref[rows, :]
        new_rows = []
        for r in range(RA):
            tp = tok_ref[i * RA + r]
            slot = lax.rem(tp, W)
            base = pl.multiple_of((slot // 16) * 16, 16)
            hit = sub == (slot - base)
            spot = pl.ds(base, 16)
            kb[b, r, spot, :] = jnp.where(hit, kn[r:r + 1], kb[b, r, spot, :].astype(F32)).astype(BF)
            vb[b, r, spot, :] = jnp.where(hit, vn[r:r + 1], vb[b, r, spot, :].astype(F32)).astype(BF)
            sn = jnp.where(lane == slot, tp, slots[r:r + 1])
            new_rows.append((tp, sn))
        for r in range(RA):
            tp, sn = new_rows[r]
            so_ref[pl.ds(i * RA + r, 1), :] = sn
            age = tp - sn
            valid = (sn >= 0) & (age >= 0) & (age < W)
            s = lax.dot_general(q_s[4 * r:4 * r + 4, :].astype(BF), kb[b, r], NT, preferred_element_type=F32) * (HD ** -0.5)
            s_s[4 * r:4 * r + 4, :] = jnp.where(valid, s, -jnp.inf)
        s = s_s[...]
        e = jnp.exp(s - jnp.max(s, axis=-1, keepdims=True))
        s_s[...] = e / jnp.sum(e, axis=-1, keepdims=True)
        for r in range(RA):
            o_s[4 * r:4 * r + 4, :] = jnp.dot(s_s[4 * r:4 * r + 4, :].astype(BF), vb[b, r], preferred_element_type=F32)
        for h in range(4):
            o_ref[rows, 128 * h:128 * h + 128] = o_s[pl.ds(h, RA, stride=4), :].astype(BF)
        for cp in copies(i, True):
            cp.start()
        return carry

    lax.fori_loop(0, STEPS, step_fn, 0)
    for step in range(STEPS - NB, STEPS):
        for cp in copies(step, True):
            cp.wait()


def attend(tok, q, kn, vn, slot_pos, kc, vc):
    return pl.pallas_call(
        attn_kernel,
        name='attend',
        in_specs=[pl.BlockSpec(memory_space=pltpu.SMEM), VM, VM, VM, VM, ANY, ANY],
        out_specs=(VM, ANY, ANY, VM),
        out_shape=(jax.ShapeDtypeStruct((B, 4 * HD), BF), jax.ShapeDtypeStruct(kc.shape, BF), jax.ShapeDtypeStruct(vc.shape, BF), jax.ShapeDtypeStruct(slot_pos.shape, jnp.int32)),
        scratch_shapes=[pltpu.VMEM((NB, RA, W, HD), BF), pltpu.VMEM((NB, RA, W, HD), BF), pltpu.VMEM((4 * RA, W), F32), pltpu.VMEM((4 * RA, HD), F32), pltpu.VMEM((4 * RA, HD), F32),
                        pltpu.SemaphoreType.DMA((2, NB)), pltpu.SemaphoreType.DMA((2, NB))],
        cost_estimate=pl.CostEstimate(flops=4 * B * 4 * W * HD, bytes_accessed=8 * B * W * HD, transcendentals=0),
    )(tok, q, kn, vn, slot_pos, kc, vc)


def rope_tables(tok_pos):
    quarter = HD // 4
    lane = lax.broadcasted_iota(jnp.int32, (1, HD), 1)
    inv_freq = ROPE_BASE ** (-(lane % quarter).astype(F32) / quarter)
    angles = tok_pos.astype(F32)[:, None] * inv_freq
    cos, sin = jnp.cos(angles), jnp.sin(angles)
    return jnp.where(lane < 2 * quarter, cos, 1.0), jnp.where(lane < quarter, -sin, jnp.where(lane < 2 * quarter, sin, 0.0))


def io_specs():
    in_specs = (P('dp', None), P('dp'), P(None, 'dp', None, 'tp'), P(None, 'dp', 'tp'), P('dp', None, None), P('dp', None, None), P('dp', None),
                P(), P(None, None, 'tp'), P(None, 'tp'), P(None, None, 'tp'), P(None, 'tp'), P(None, None, 'tp'), P(None, 'tp'),
                P(None, 'tp', None, None), P(None, 'tp'), P(None, 'tp', None, None), P(None, 'tp'), P(None, 'tp'), P(None, 'tp', None), P(),
                P(None, 'tp'), P(), P(), P('tp', None), P(),
                P(None, None, 'tp'), P(None, 'tp'), P(None, None, 'tp'), P(None, 'tp'), P(None, 'tp', None), P())
    out_specs = (P('dp', None), P(None, 'dp', None, 'tp'), P(None, 'dp', 'tp'), P('dp', None, None), P('dp', None, None), P('dp', None))
    return in_specs, out_specs


def solution(mesh):
    in_specs, out_specs = io_specs()

    def local_step(x_in, tok_pos, conv_state, lru_state, k_cache, v_cache, slot_pos, norm_scale, rec_wx, rec_bx, rec_wy, rec_by, conv_w, conv_b, gate_wa, gate_ba, gate_wi, gate_bi, a_param, rec_wout, rec_bout, attn_wq, attn_wk, attn_wv, attn_wo, attn_bo, mlp_w1, mlp_b1, mlp_w2, mlp_b2, mlp_wd, mlp_bd):
        wxt = jnp.swapaxes(rec_wx, 1, 2)
        wyt = jnp.swapaxes(rec_wy, 1, 2)
        convt = jnp.transpose(conv_state, (0, 2, 3, 1))
        lrut = jnp.swapaxes(lru_state, 1, 2)
        tok_row = tok_pos[None, :]
        tab = rope_tables(tok_pos)

        q, kn, vn, x_own, convs, lrus = first_layers(x_in, norm_scale, wxt, wyt, convt, lrut, gate_wa, gate_wi, rec_bx, rec_by, conv_w, conv_b, gate_ba, gate_bi, -8.0 * jax.nn.softplus(a_param), tok_row, rec_wout, rec_bout, mlp_w1, mlp_b1, mlp_w2, mlp_b2, mlp_wd, mlp_bd, attn_wq, attn_wk, attn_wv, *tab)
        o, k_next, v_next, slot_next = attend(tok_pos, q.reshape(B, 4 * HD), kn.reshape(B, HD), vn.reshape(B, HD), slot_pos, k_cache, v_cache)
        x = last_layer(o, x_own, attn_wo, attn_bo[None, :], norm_scale, mlp_w1, mlp_b1, mlp_w2, mlp_b2, mlp_wd, mlp_bd)
        conv_out = jnp.transpose(convs, (0, 3, 1, 2))
        lru_out = jnp.swapaxes(lrus, 1, 2)
        return (x, conv_out, lru_out, k_next, v_next, slot_next)

    return jax.shard_map(local_step, mesh=mesh, in_specs=in_specs, out_specs=out_specs, check_vma=False)
```

time: 321 us -> 298 us (0.928)
  Pallas kernels: 309 us -> 287 us
    pallas_call x1, Pallas kernels: 150 us -> 136 us  [first_layers(): pl.pallas_call(kernel_a, name='first_layers', out_shape=(jax.ShapeDtypeSt...]
    pallas_call x1, Pallas kernels: 69.5 us -> 60.7 us  [last_layer(): pl.pallas_call(kernel_b, name='last_layer', out_shape=jax.ShapeDtypeStruc...]
where the time goes in v4:
time: 298 us
  Pallas kernels  287 us (96%)
  local copies, waits for them, and re-layouts  7.04 us (2%)
  other arithmetic  3.26 us (1%)
    pallas_call x1, Pallas kernels, first_layers(): pl.pallas_call(kernel_a, name='first_layers', out_shape=(jax.ShapeDtypeSt...  136 us
    pallas_call x1, Pallas kernels, attend(): pl.pallas_call(attn_kernel, name='attend', in_specs=[pl.BlockSpec(memory_...  90.2 us
    pallas_call x1, Pallas kernels, last_layer(): pl.pallas_call(kernel_b, name='last_layer', out_shape=jax.ShapeDtypeStruc...  60.7 us

profile of v4, /device:TPU:1, one launch (start us, length us, event | category | flops | bytes accessed | tf_op | source)
XLA Modules:
  0.0 298.2 jit_solution(17228156470107710202)
XLA Ops:
  0.6 0.7 convert_bitcast_fusion
  1.3 1.3 fusion.4.sp_ref
  2.6 1.3 broadcast_in_dim.40.bo_ref
  4.0 1.3 fusion.2
  5.2 136.3 %first_layers.1 = (bf16[2,128,512]{2,1,0:T(8,128)(2,1)}, bf16[2,128,128]{2,1,0:T(8,128)(2,1)}, bf16[2,128,128]{2,1,0:T(8,128)(2,1)}, bf16[2,16,4096]{2,1,0:T(8,1...) custom-call(bf16[2,4,2,16,4096]{4,3,2,1,0:T(8,128)(2,1)} %bitcast.20, bf16[3,2,4096]{2,1,0:T(2,128)(2,1)} %sc_ref.3, ...), custom_call_target="tpu_custom_call" | custom-call | flops 30000001024 | bytes 400000000 | tf_op jit(solution)/shard_map/first_layers/pallas_call | solution.py:421
  141.5 90.2 %attend.1 = (bf16[256,512]{1,0:T(8,128)(2,1)}, bf16[256,1024,128]{2,1,0:T(8,128)(2,1)}, bf16[256,1024,128]{2,1,0:T(8,128)(2,1)}, s32[256,1024]{1,0:T(8,128)}) custom-call(s32[256]{0:T(256)} %tok_ref.1, bf16[256,512]{1,0:T(8,128)(2,1)} %bitcast.23, bf16[256,128]{1,0:T(8,128)(2,1)} %bitcast.25, bf16[256,128]{1,0:T(8,128)(2,1)} %bitcast.26, ...), custom_call_target="tpu_custom_call" | custom-call | flops 536870912 | bytes 268435456 | tf_op jit(solution)/shard_map/attend/pallas_call | solution.py:565
  231.7 60.7 %last_layer.1 = bf16[2,128,4096]{2,1,0:T(8,128)(2,1)} custom-call(bf16[2,128,512]{2,1,0:T(8,128)(2,1)} %bitcast.24, bf16[2,16,4096]{2,1,0:T(8,128)(2,1)} %get-tuple-element.20.x_ref, bf16[512,4096]{1,0:T(8,128)(2,1)} %wo.1, bf16[1,4096]{1,0:T(2,128)(2,1)} %broadcast_in_dim.40.bo_ref, bf16[3,2,4096]{2,1,0:T(2,128)(2,1)} %sc_ref.3, bf16[3,4096,1536]{2,1,0:T(8,128)(2,1)} %w1.3, ...), custom_call_target="tpu_custom_call" | custom-call | flops 12000000000 | bytes 200000000 | tf_op jit(solution)/shard_map/last_layer/pallas_call | solution.py:470
  292.5 0.0 copy-start
  292.5 0.0 copy-start.1
  292.5 3.3 %copy.41 = bf16[256,4096]{1,0:T(8,128)(2,1)} copy(bf16[256,4096]{1,0:T(8,128)(2,1)} %bitcast.17) | data formatting | bytes 4194304
  295.8 0.0 copy-done
  295.8 1.3 copy.42
  297.1 0.0 copy-done.1
  297.1 1.1 copy.43
  (2 shorter events, 0.0 us)
Async XLA Ops:
  292.5 3.3 %copy-start = (bf16[2,3,704,256]{3,2,1,0:T(8,128)(2,1)S(1)}, bf16[2,3,704,256]{3,2,1,0:T(8,128)(2,1)}, u32[]{:S(2)}) copy-start(bf16[2,3,704,256]{3,2,1,0:T(8,128)(2,1)} %get-tuple-element.21) | copy-start | bytes 6488068
  292.5 4.6 %copy-start.1 = (f32[2,704,256]{2,1,0:T(8,128)S(1)}, f32[2,704,256]{2,1,0:T(8,128)}, u32[]{:S(2)}) copy-start(f32[2,704,256]{2,1,0:T(8,128)} %get-tuple-element.22) | copy-start | bytes 4325380

commit v5 on v4

--- a/solution.py
+++ b/solution.py
@@ -20,7 +20,7 @@
 FC = 1536
 W = 1024
 HD = 128
-G = 4
+G = 2
 HB = 128
 OR = 16
 GC = D // G
@@ -41,10 +41,18 @@
     return pl.ds(pl.multiple_of(g * GC, GC), GC)
 
 
+SLAB = 512
+PER = GC // SLAB
+
+
+def piece(g, e):
+    return pl.ds(pl.multiple_of(g * GC + e * SLAB, SLAB), SLAB)
+
+
 class Links:
-    def __init__(self, part, recv1, recv2, own, n, xown, s1s, s1r, s2s, s2r, s3s, s3r, s4s, s4r):
+    def __init__(self, part, recv1, recv2, own, n, xown, s1s, s1r, s2s, s2r, s3s, s3r, s4s, s4r, s5s, s5r):
         self.part, self.recv1, self.recv2, self.own, self.n, self.xown = part, recv1, recv2, own, n, xown
-        self.s1s, self.s1r, self.s2s, self.s2r, self.s3s, self.s3r, self.s4s, self.s4r = s1s, s1r, s2s, s2r, s3s, s3r, s4s, s4r
+        self.s1s, self.s1r, self.s2s, self.s2r, self.s3s, self.s3r, self.s4s, self.s4r, self.s5s, self.s5r = s1s, s1r, s2s, s2r, s3s, s3r, s4s, s4r, s5s, s5r
         t = lax.axis_index('tp')
         y, x = t // 4, (t // 2) % 2
         self.c = t % 2
@@ -73,7 +81,11 @@
 
     def from_own(self, h, g, k):
         ref = self.place(h, 2 * self.q + self.c, g)
-        return self.remote(ref, ref, self.s3s.at[h, g, k], self.s3r.at[h, g, k], self.peers[k] if k < 3 else self.partner)
+        return self.remote(ref, ref, self.s3s.at[h, g, k], self.s3r.at[h, g, k], self.peers[k])
+
+    def own_pair(self, h):
+        ref = self.n.at[h, pl.ds(pl.multiple_of((2 * self.q + self.c) * OR, OR), OR)]
+        return self.remote(ref, ref, self.s5s.at[h], self.s5r.at[h], self.partner)
 
     def pass_on(self, h, g, k):
         ref = self.place(h, self.peers[k], g)
@@ -94,11 +106,13 @@
         def step(g, carry):
             if before is not None:
                 before(g)
-            left = lhs()
-            for p in range(2):
-                cols = pl.ds(pl.multiple_of(g * GC + p * 512, 512), 512)
-                out = jnp.dot(left, rhs(g, p), preferred_element_type=F32)
-                part[h, :, :, :, cols] = out.astype(BF).reshape(4, 2, OR, 512)
+            def tile(p, carry):
+                cols = piece(g, p)
+                out = jnp.dot(lhs(), rhs(cols), preferred_element_type=F32)
+                part[h, :, :, :, cols] = out.astype(BF).reshape(4, 2, OR, SLAB)
+                return carry
+
+            lax.fori_loop(0, PER, tile, 0)
             if after is not None:
                 after(g)
             self.to_partner(h, g).start()
@@ -135,8 +149,10 @@
         rows = self.xown[h]
         self.n[h, pl.ds(pl.multiple_of((2 * self.q + self.c) * OR, OR), OR), :] = rows if scale is None else rms(rows, scale)
 
+        self.own_pair(h).start()
+
         def send(i, carry):
-            for k in (2, 0, 1, 3):
+            for k in (2, 0, 1):
                 self.from_own(h, order(h, i), k).start()
             return carry
 
@@ -156,7 +172,10 @@
             def _():
                 g = order(h, i - 1)
                 if not fresh:
-                    self.from_own(h, g, 3).wait_recv()
+                    @pl.when(i == 1)
+                    def _():
+                        self.own_pair(h).wait_recv()
+
                     for k in range(3):
                         self.pass_on(h, g, k).wait_recv()
                 use(i - 1, g)
@@ -167,10 +186,11 @@
         if fresh:
             return
 
+        self.own_pair(h).wait_send()
+
         def sent(g, carry):
-            for k in range(4):
+            for k in range(3):
                 self.from_own(h, g, k).wait_send()
-            for k in range(3):
                 self.pass_on(h, g, k).wait_send()
             return carry
 
@@ -178,18 +198,17 @@
 
 
 def order(h, i):
-    return lax.rem(i + 2 * h, G)
+    return lax.rem(i + (G // 2) * h, G)
 
 
 LINK_SCRATCH = [
     pltpu.VMEM((2, 4, 2, OR, D), BF), pltpu.VMEM((2, 4, OR, D), BF), pltpu.VMEM((2, 3, OR, D), BF),
     pltpu.VMEM((2, OR, D), F32), pltpu.VMEM((2, HB, D), BF), pltpu.VMEM((2, OR, D), BF),
-    DMA((2, G)), DMA((2, G)), DMA((2, G, 3)), DMA((2, G, 3)), DMA((2, G, 4)), DMA((2, G, 4)), DMA((2, G, 3)), DMA((2, G, 3)),
+    DMA((2, G)), DMA((2, G)), DMA((2, G, 3)), DMA((2, G, 3)), DMA((2, G, 3)), DMA((2, G, 3)), DMA((2, G, 3)), DMA((2, G, 3)), DMA((2,)), DMA((2,)),
 ]
 NLINK = len(LINK_SCRATCH)
 
 SLOTS = 5
-SLAB = 512
 LOADS = 12
 
 
@@ -254,14 +273,17 @@
     acc[...] = jnp.zeros_like(acc)
 
     def use(i, g):
-        for e in range(2):
+        def one(e, carry):
             def body(slot):
-                ng = net.n[h, :, pl.ds(pl.multiple_of(g * GC + e * SLAB, SLAB), SLAB)]
+                ng = net.n[h, :, piece(g, e)]
                 for half in range(2):
                     for lo in range(0, FC, 512):
                         acc[half, :, lo:lo + 512] += jnp.dot(ng, slabs.wu[slot, half, :, lo:lo + 512], preferred_element_type=F32)
 
-            slabs.use(h, j, 2 * i + e, body)
+            slabs.use(h, j, PER * i + e, body)
+            return carry
+
+        lax.fori_loop(0, PER, one, 0)
 
     net.gathered(h, use)
     b1 = b1_ref[...].astype(F32)[layer:layer + 1]
@@ -283,7 +305,7 @@
             if h == 1 and not last:
                 wide(wd.at[layer + 1], wdb, ds, g).start()
 
-        net.scatter(h, lambda: h_s[...], lambda g, p: wdb[:, pl.ds(pl.multiple_of(g * GC + p * 512, 512), 512)], before, after)
+        net.scatter(h, lambda: h_s[...], lambda cols: wdb[:, cols], before, after)
 
 
 def rope(v, keep, turn):
@@ -338,9 +360,14 @@
                 if h == 0:
                     for cp in rec_in(layer, g):
                         cp.wait()
-                ng = net.n[h, :, chunk(g)]
-                for half in range(2):
-                    accr[half] += lax.dot_general(wxb[half, :, chunk(g)], ng, NT, preferred_element_type=F32)
+
+                def one(e, carry):
+                    cols = pl.ds(pl.multiple_of(g * GC + e * 1024, 1024), 1024)
+                    for half in range(2):
+                        accr[half] += lax.dot_general(wxb[half, :, cols], net.n[h, :, cols], NT, preferred_element_type=F32)
+                    return carry
+
+                lax.fori_loop(0, GC // 1024, one, 0)
 
             net.gathered(h, use, fresh=layer == 0)
             if h == 0:
@@ -379,7 +406,7 @@
                 if h == 0:
                     wide(wout.at[layer], wob, os, g).wait()
 
-            net.scatter(h, lambda: h_s[:, :LC], lambda g, p: wob[:, pl.ds(pl.multiple_of(g * GC + p * 512, 512), 512)], before)
+            net.scatter(h, lambda: h_s[:, :LC], lambda cols: wob[:, cols], before)
         for cp in state_out(layer):
             cp.start()
         if layer == 0:
@@ -402,12 +429,14 @@
         acc[...] = jnp.zeros_like(acc)
 
         def use_q(i, g):
-            for e in range(2):
+            def one(e, carry):
                 def body(slot):
-                    ng = net.n[h, :, pl.ds(pl.multiple_of(g * GC + e * SLAB, SLAB), SLAB)]
-                    acc[0, :, 0:768] += jnp.dot(ng, wu[slot, 0, :, 0:768], preferred_element_type=F32)
-
-                slabs.use(h, 2, 2 * i + e, body)
+                    acc[0, :, 0:768] += jnp.dot(net.n[h, :, piece(g, e)], wu[slot, 0, :, 0:768], preferred_element_type=F32)
+
+                slabs.use(h, 2, PER * i + e, body)
+                return carry
+
+            lax.fori_loop(0, PER, one, 0)
 
         net.gathered(h, use_q)
         keep, turn = keep_ref[h], turn_ref[h]
@@ -452,7 +481,7 @@
             if h == 0:
                 wide(wo, wob, os, g).wait()
 
-        net.scatter(h, lambda: o_ref[h], lambda g, p: wob[:, pl.ds(pl.multiple_of(g * GC + p * 512, 512), 512)], before)
+        net.scatter(h, lambda: o_ref[h], lambda cols: wob[:, cols], before)
     for h in range(2):
         net.finish(h, bo_ref, 0, sc_ref[...].astype(F32)[2, 1:2, :])
     mlp(net, slabs, 0, acc, h_s, b1_ref, b2_ref, wd, wdb, ds, 2, True)

time: 298 us -> 316 us (1.060)
  Pallas kernels: 287 us -> 304 us
    pallas_call x1, Pallas kernels: 136 us -> 148 us  [first_layers(): pl.pallas_call(kernel_a, name='first_layers', out_shape=(jax.ShapeDtypeSt...]
    pallas_call x1, Pallas kernels: 60.7 us -> 65.8 us  [last_layer(): pl.pallas_call(kernel_b, name='last_layer', out_shape=jax.ShapeDtypeStruc...]
where the time goes in v5:
time: 316 us; the launch traced here: 315 us
  Pallas kernels  304 us (96%)
  local copies, waits for them, and re-layouts  7.04 us (2%)
  other arithmetic  3.26 us (1%)
    pallas_call x1, Pallas kernels, first_layers(): pl.pallas_call(kernel_a, name='first_layers', out_shape=(jax.ShapeDtypeSt...  148 us
    pallas_call x1, Pallas kernels, attend(): pl.pallas_call(attn_kernel, name='attend', in_specs=[pl.BlockSpec(memory_...  90.2 us
    pallas_call x1, Pallas kernels, last_layer(): pl.pallas_call(kernel_b, name='last_layer', out_shape=jax.ShapeDtypeStruc...  65.8 us

profile of v5, /device:TPU:1, one launch (start us, length us, event | category | flops | bytes accessed | tf_op | source)
XLA Modules:
  0.0 315.5 jit_solution(3713226007442995060)
XLA Ops:
  0.6 0.7 convert_bitcast_fusion
  1.3 1.3 fusion.4.sp_ref
  2.6 1.3 broadcast_in_dim.40.bo_ref
  4.0 1.3 fusion.2
  5.2 148.4 %first_layers.1 = (bf16[2,128,512]{2,1,0:T(8,128)(2,1)}, bf16[2,128,128]{2,1,0:T(8,128)(2,1)}, bf16[2,128,128]{2,1,0:T(8,128)(2,1)}, bf16[2,16,4096]{2,1,0:T(8,1...) custom-call(bf16[2,4,2,16,4096]{4,3,2,1,0:T(8,128)(2,1)} %bitcast.20, bf16[3,2,4096]{2,1,0:T(2,128)(2,1)} %sc_ref.3, ...), custom_call_target="tpu_custom_call" | custom-call | flops 30000001024 | bytes 400000000 | tf_op jit(solution)/shard_map/first_layers/pallas_call | solution.py:450
  153.6 90.2 %attend.1 = (bf16[256,512]{1,0:T(8,128)(2,1)}, bf16[256,1024,128]{2,1,0:T(8,128)(2,1)}, bf16[256,1024,128]{2,1,0:T(8,128)(2,1)}, s32[256,1024]{1,0:T(8,128)}) custom-call(s32[256]{0:T(256)} %tok_ref.1, bf16[256,512]{1,0:T(8,128)(2,1)} %bitcast.23, bf16[256,128]{1,0:T(8,128)(2,1)} %bitcast.25, bf16[256,128]{1,0:T(8,128)(2,1)} %bitcast.26, ...), custom_call_target="tpu_custom_call" | custom-call | flops 536870912 | bytes 268435456 | tf_op jit(solution)/shard_map/attend/pallas_call | solution.py:594
  243.9 65.8 %last_layer.1 = bf16[2,128,4096]{2,1,0:T(8,128)(2,1)} custom-call(bf16[2,128,512]{2,1,0:T(8,128)(2,1)} %bitcast.24, bf16[2,16,4096]{2,1,0:T(8,128)(2,1)} %get-tuple-element.20.x_ref, bf16[512,4096]{1,0:T(8,128)(2,1)} %wo.1, bf16[1,4096]{1,0:T(2,128)(2,1)} %broadcast_in_dim.40.bo_ref, bf16[3,2,4096]{2,1,0:T(2,128)(2,1)} %sc_ref.3, bf16[3,4096,1536]{2,1,0:T(8,128)(2,1)} %w1.3, ...), custom_call_target="tpu_custom_call" | custom-call | flops 12000000000 | bytes 200000000 | tf_op jit(solution)/shard_map/last_layer/pallas_call | solution.py:499
  309.7 0.0 copy-start
  309.7 0.0 copy-start.1
  309.7 3.3 %copy.41 = bf16[256,4096]{1,0:T(8,128)(2,1)} copy(bf16[256,4096]{1,0:T(8,128)(2,1)} %bitcast.17) | data formatting | bytes 4194304
  313.0 0.0 copy-done
  313.0 1.3 copy.42
  314.4 0.0 copy-done.1
  314.4 1.1 copy.43
  (2 shorter events, 0.0 us)
Async XLA Ops:
  309.7 3.3 %copy-start = (bf16[2,3,704,256]{3,2,1,0:T(8,128)(2,1)S(1)}, bf16[2,3,704,256]{3,2,1,0:T(8,128)(2,1)}, u32[]{:S(2)}) copy-start(bf16[2,3,704,256]{3,2,1,0:T(8,128)(2,1)} %get-tuple-element.21) | copy-start | bytes 6488068
  309.7 4.6 %copy-start.1 = (f32[2,704,256]{2,1,0:T(8,128)S(1)}, f32[2,704,256]{2,1,0:T(8,128)}, u32[]{:S(2)}) copy-start(f32[2,704,256]{2,1,0:T(8,128)} %get-tuple-element.22) | copy-start | bytes 4325380

commit v6 on v5

--- a/solution.py
+++ b/solution.py
@@ -20,7 +20,7 @@
 FC = 1536
 W = 1024
 HD = 128
-G = 2
+G = 4
 HB = 128
 OR = 16
 GC = D // G
@@ -94,7 +94,7 @@
     def scatter(self, h, lhs, rhs, before=None, after=None):
         c, q, chips, part = self.c, self.q, self.chips, self.part
 
-        def pair(g):
+        def pair(g, carry):
             cols = chunk(g)
             self.to_partner(h, g).wait_recv()
             for k in (2, 0, 1):
@@ -102,6 +102,7 @@
                 part[h, chips[k], c, :, cols] = s.astype(BF)
                 self.to_owner(h, g, k).start()
             self.own[h, :, cols] = part[h, q, c, :, cols].astype(F32) + self.recv1[h, q, :, cols].astype(F32)
+            return carry
 
         def step(g, carry):
             if before is not None:
@@ -116,15 +117,10 @@
             if after is not None:
                 after(g)
             self.to_partner(h, g).start()
-
-            @pl.when(g > 0)
-            def _():
-                pair(g - 1)
-
             return carry
 
         lax.fori_loop(0, G, step, 0)
-        pair(G - 1)
+        lax.fori_loop(0, G, pair, 0)
 
     def finish(self, h, bias_ref, layer, scale):
         def final(g, carry):
@@ -139,6 +135,18 @@
 
         lax.fori_loop(0, G, final, 0)
 
+        rows = self.xown[h]
+        self.n[h, pl.ds(pl.multiple_of((2 * self.q + self.c) * OR, OR), OR), :] = rows if scale is None else rms(rows, scale)
+
+        self.own_pair(h).start()
+
+        def send(i, carry):
+            for k in (2, 0, 1):
+                self.from_own(h, order(h, i), k).start()
+            return carry
+
+        lax.fori_loop(0, G, send, 0)
+
         def sent(g, carry):
             self.to_partner(h, g).wait_send()
             for k in range(3):
@@ -146,27 +154,23 @@
             return carry
 
         lax.fori_loop(0, G, sent, 0)
-        rows = self.xown[h]
-        self.n[h, pl.ds(pl.multiple_of((2 * self.q + self.c) * OR, OR), OR), :] = rows if scale is None else rms(rows, scale)
-
-        self.own_pair(h).start()
-
-        def send(i, carry):
-            for k in (2, 0, 1):
-                self.from_own(h, order(h, i), k).start()
-            return carry
-
-        lax.fori_loop(0, G, send, 0)
 
     def gathered(self, h, use, fresh=False):
+        def forward(i, carry):
+            g = order(h, i)
+            for k in range(3):
+                self.from_own(h, g, k).wait_recv()
+                self.pass_on(h, g, k).start()
+            return carry
+
+        if h == 1 and not fresh:
+            lax.fori_loop(0, G, forward, 0)
+
         def step(i, carry):
-            if not fresh:
+            if h == 0 and not fresh:
                 @pl.when(i < G)
                 def _():
-                    g = order(h, i)
-                    for k in range(3):
-                        self.from_own(h, g, k).wait_recv()
-                        self.pass_on(h, g, k).start()
+                    forward(i, 0)
 
             @pl.when(i > 0)
             def _():

time: 316 us -> 306 us (0.968)
  Pallas kernels: 304 us -> 295 us
    pallas_call x1, Pallas kernels: 148 us -> 141 us  [first_layers(): pl.pallas_call(kernel_a, name='first_layers', out_shape=(jax.ShapeDtypeSt...]
where the time goes in v6:
time: 306 us
  Pallas kernels  295 us (96%)
  local copies, waits for them, and re-layouts  7.04 us (2%)
  other arithmetic  3.26 us (1%)
    pallas_call x1, Pallas kernels, first_layers(): pl.pallas_call(kernel_a, name='first_layers', out_shape=(jax.ShapeDtypeSt...  141 us
    pallas_call x1, Pallas kernels, attend(): pl.pallas_call(attn_kernel, name='attend', in_specs=[pl.BlockSpec(memory_...  90.2 us
    pallas_call x1, Pallas kernels, last_layer(): pl.pallas_call(kernel_b, name='last_layer', out_shape=jax.ShapeDtypeStruc...  63.9 us

profile of v6, /device:TPU:1, one launch (start us, length us, event | category | flops | bytes accessed | tf_op | source)
XLA Modules:
  0.0 305.8 jit_solution(13688513161702122566)
XLA Ops:
  0.6 0.7 convert_bitcast_fusion
  1.3 1.3 fusion.4.sp_ref
  2.6 1.3 broadcast_in_dim.40.bo_ref
  4.0 1.3 fusion.2
  5.2 140.7 %first_layers.1 = (bf16[2,128,512]{2,1,0:T(8,128)(2,1)}, bf16[2,128,128]{2,1,0:T(8,128)(2,1)}, bf16[2,128,128]{2,1,0:T(8,128)(2,1)}, bf16[2,16,4096]{2,1,0:T(8,1...) custom-call(bf16[2,4,2,16,4096]{4,3,2,1,0:T(8,128)(2,1)} %bitcast.20, bf16[3,2,4096]{2,1,0:T(2,128)(2,1)} %sc_ref.3, ...), custom_call_target="tpu_custom_call" | custom-call | flops 30000001024 | bytes 400000000 | tf_op jit(solution)/shard_map/first_layers/pallas_call | solution.py:454
  145.9 90.2 %attend.1 = (bf16[256,512]{1,0:T(8,128)(2,1)}, bf16[256,1024,128]{2,1,0:T(8,128)(2,1)}, bf16[256,1024,128]{2,1,0:T(8,128)(2,1)}, s32[256,1024]{1,0:T(8,128)}) custom-call(s32[256]{0:T(256)} %tok_ref.1, bf16[256,512]{1,0:T(8,128)(2,1)} %bitcast.23, bf16[256,128]{1,0:T(8,128)(2,1)} %bitcast.25, bf16[256,128]{1,0:T(8,128)(2,1)} %bitcast.26, ...), custom_call_target="tpu_custom_call" | custom-call | flops 536870912 | bytes 268435456 | tf_op jit(solution)/shard_map/attend/pallas_call | solution.py:598
  236.1 63.9 %last_layer.1 = bf16[2,128,4096]{2,1,0:T(8,128)(2,1)} custom-call(bf16[2,128,512]{2,1,0:T(8,128)(2,1)} %bitcast.24, bf16[2,16,4096]{2,1,0:T(8,128)(2,1)} %get-tuple-element.20.x_ref, bf16[512,4096]{1,0:T(8,128)(2,1)} %wo.1, bf16[1,4096]{1,0:T(2,128)(2,1)} %broadcast_in_dim.40.bo_ref, bf16[3,2,4096]{2,1,0:T(2,128)(2,1)} %sc_ref.3, bf16[3,4096,1536]{2,1,0:T(8,128)(2,1)} %w1.3, ...), custom_call_target="tpu_custom_call" | custom-call | flops 12000000000 | bytes 200000000 | tf_op jit(solution)/shard_map/last_layer/pallas_call | solution.py:503
  300.0 0.0 copy-start
  300.0 0.0 copy-start.1
  300.0 3.3 %copy.41 = bf16[256,4096]{1,0:T(8,128)(2,1)} copy(bf16[256,4096]{1,0:T(8,128)(2,1)} %bitcast.17) | data formatting | bytes 4194304
  303.3 0.0 copy-done
  303.3 1.3 copy.42
  304.7 0.0 copy-done.1
  304.7 1.1 copy.43
  (2 shorter events, 0.0 us)
Async XLA Ops:
  300.0 3.3 %copy-start = (bf16[2,3,704,256]{3,2,1,0:T(8,128)(2,1)S(1)}, bf16[2,3,704,256]{3,2,1,0:T(8,128)(2,1)}, u32[]{:S(2)}) copy-start(bf16[2,3,704,256]{3,2,1,0:T(8,128)(2,1)} %get-tuple-element.21) | copy-start | bytes 6488068
  300.0 4.6 %copy-start.1 = (f32[2,704,256]{2,1,0:T(8,128)S(1)}, f32[2,704,256]{2,1,0:T(8,128)}, u32[]{:S(2)}) copy-start(f32[2,704,256]{2,1,0:T(8,128)} %get-tuple-element.22) | copy-start | bytes 4325380

commit v7 on v6

--- a/solution.py
+++ b/solution.py
@@ -45,6 +45,11 @@
 PER = GC // SLAB
 
 
+def unrolled(count, body):
+    for e in range(count):
+        body(e, None)
+
+
 def piece(g, e):
     return pl.ds(pl.multiple_of(g * GC + e * SLAB, SLAB), SLAB)
 
@@ -113,7 +118,7 @@
                 part[h, :, :, :, cols] = out.astype(BF).reshape(4, 2, OR, SLAB)
                 return carry
 
-            lax.fori_loop(0, PER, tile, 0)
+            unrolled(PER, tile)
             if after is not None:
                 after(g)
             self.to_partner(h, g).start()
@@ -163,11 +168,8 @@
                 self.pass_on(h, g, k).start()
             return carry
 
-        if h == 1 and not fresh:
-            lax.fori_loop(0, G, forward, 0)
-
         def step(i, carry):
-            if h == 0 and not fresh:
+            if not fresh:
                 @pl.when(i < G)
                 def _():
                     forward(i, 0)
@@ -287,7 +289,7 @@
             slabs.use(h, j, PER * i + e, body)
             return carry
 
-        lax.fori_loop(0, PER, one, 0)
+        unrolled(PER, one)
 
     net.gathered(h, use)
     b1 = b1_ref[...].astype(F32)[layer:layer + 1]
@@ -371,7 +373,7 @@
                         accr[half] += lax.dot_general(wxb[half, :, cols], net.n[h, :, cols], NT, preferred_element_type=F32)
                     return carry
 
-                lax.fori_loop(0, GC // 1024, one, 0)
+                unrolled(GC // 1024, one)
 
             net.gathered(h, use, fresh=layer == 0)
             if h == 0:
@@ -440,7 +442,7 @@
                 slabs.use(h, 2, PER * i + e, body)
                 return carry
 
-            lax.fori_loop(0, PER, one, 0)
+            unrolled(PER, one)
 
         net.gathered(h, use_q)
         keep, turn = keep_ref[h], turn_ref[h]

time: 306 us -> 297 us (0.971)
  Pallas kernels: 295 us -> 286 us
    pallas_call x1, Pallas kernels: 141 us -> 135 us  [first_layers(): pl.pallas_call(kernel_a, name='first_layers', out_shape=(jax.ShapeDtypeSt...]
where the time goes in v7:
time: 297 us
  Pallas kernels  286 us (96%)
  local copies, waits for them, and re-layouts  7.04 us (2%)
  other arithmetic  3.26 us (1%)
    pallas_call x1, Pallas kernels, first_layers(): pl.pallas_call(kernel_a, name='first_layers', out_shape=(jax.ShapeDtypeSt...  135 us
    pallas_call x1, Pallas kernels, attend(): pl.pallas_call(attn_kernel, name='attend', in_specs=[pl.BlockSpec(memory_...  90.2 us
    pallas_call x1, Pallas kernels, last_layer(): pl.pallas_call(kernel_b, name='last_layer', out_shape=jax.ShapeDtypeStruc...  60.9 us

profile of v7, /device:TPU:1, one launch (start us, length us, event | category | flops | bytes accessed | tf_op | source)
XLA Modules:
  0.0 297.2 jit_solution(7104377030464013948)
XLA Ops:
  0.6 0.7 convert_bitcast_fusion
  1.3 1.3 fusion.4.sp_ref
  2.6 1.3 broadcast_in_dim.40.bo_ref
  4.0 1.3 fusion.2
  5.2 135.1 %first_layers.1 = (bf16[2,128,512]{2,1,0:T(8,128)(2,1)}, bf16[2,128,128]{2,1,0:T(8,128)(2,1)}, bf16[2,128,128]{2,1,0:T(8,128)(2,1)}, bf16[2,16,4096]{2,1,0:T(8,1...) custom-call(bf16[2,4,2,16,4096]{4,3,2,1,0:T(8,128)(2,1)} %bitcast.20, bf16[3,2,4096]{2,1,0:T(2,128)(2,1)} %sc_ref.3, ...), custom_call_target="tpu_custom_call" | custom-call | flops 30000001024 | bytes 400000000 | tf_op jit(solution)/shard_map/first_layers/pallas_call | solution.py:456
  140.3 90.2 %attend.1 = (bf16[256,512]{1,0:T(8,128)(2,1)}, bf16[256,1024,128]{2,1,0:T(8,128)(2,1)}, bf16[256,1024,128]{2,1,0:T(8,128)(2,1)}, s32[256,1024]{1,0:T(8,128)}) custom-call(s32[256]{0:T(256)} %tok_ref.1, bf16[256,512]{1,0:T(8,128)(2,1)} %bitcast.23, bf16[256,128]{1,0:T(8,128)(2,1)} %bitcast.25, bf16[256,128]{1,0:T(8,128)(2,1)} %bitcast.26, ...), custom_call_target="tpu_custom_call" | custom-call | flops 536870912 | bytes 268435456 | tf_op jit(solution)/shard_map/attend/pallas_call | solution.py:600
  230.5 60.9 %last_layer.1 = bf16[2,128,4096]{2,1,0:T(8,128)(2,1)} custom-call(bf16[2,128,512]{2,1,0:T(8,128)(2,1)} %bitcast.24, bf16[2,16,4096]{2,1,0:T(8,128)(2,1)} %get-tuple-element.20.x_ref, bf16[512,4096]{1,0:T(8,128)(2,1)} %wo.1, bf16[1,4096]{1,0:T(2,128)(2,1)} %broadcast_in_dim.40.bo_ref, bf16[3,2,4096]{2,1,0:T(2,128)(2,1)} %sc_ref.3, bf16[3,4096,1536]{2,1,0:T(8,128)(2,1)} %w1.3, ...), custom_call_target="tpu_custom_call" | custom-call | flops 12000000000 | bytes 200000000 | tf_op jit(solution)/shard_map/last_layer/pallas_call | solution.py:505
  291.4 0.0 copy-start
  291.4 0.0 copy-start.1
  291.4 3.3 %copy.41 = bf16[256,4096]{1,0:T(8,128)(2,1)} copy(bf16[256,4096]{1,0:T(8,128)(2,1)} %bitcast.17) | data formatting | bytes 4194304
  294.7 0.0 copy-done
  294.7 1.3 copy.42
  296.1 0.0 copy-done.1
  296.1 1.1 copy.43
  (2 shorter events, 0.0 us)
Async XLA Ops:
  291.4 3.3 %copy-start = (bf16[2,3,704,256]{3,2,1,0:T(8,128)(2,1)S(1)}, bf16[2,3,704,256]{3,2,1,0:T(8,128)(2,1)}, u32[]{:S(2)}) copy-start(bf16[2,3,704,256]{3,2,1,0:T(8,128)(2,1)} %get-tuple-element.21) | copy-start | bytes 6488068
  291.4 4.6 %copy-start.1 = (f32[2,704,256]{2,1,0:T(8,128)S(1)}, f32[2,704,256]{2,1,0:T(8,128)}, u32[]{:S(2)}) copy-start(f32[2,704,256]{2,1,0:T(8,128)} %get-tuple-element.22) | copy-start | bytes 4325380

commit v8 on v7

--- a/solution.py
+++ b/solution.py
@@ -160,7 +160,7 @@
 
         lax.fori_loop(0, G, sent, 0)
 
-    def gathered(self, h, use, fresh=False):
+    def gathered(self, h, use):
         def forward(i, carry):
             g = order(h, i)
             for k in range(3):
@@ -169,29 +169,25 @@
             return carry
 
         def step(i, carry):
-            if not fresh:
-                @pl.when(i < G)
-                def _():
-                    forward(i, 0)
+            @pl.when(i < G)
+            def _():
+                forward(i, 0)
 
             @pl.when(i > 0)
             def _():
                 g = order(h, i - 1)
-                if not fresh:
-                    @pl.when(i == 1)
-                    def _():
-                        self.own_pair(h).wait_recv()
-
-                    for k in range(3):
-                        self.pass_on(h, g, k).wait_recv()
+
+                @pl.when(i == 1)
+                def _():
+                    self.own_pair(h).wait_recv()
+
+                for k in range(3):
+                    self.pass_on(h, g, k).wait_recv()
                 use(i - 1, g)
 
             return carry
 
         lax.fori_loop(0, G + 1, step, 0)
-        if fresh:
-            return
-
         self.own_pair(h).wait_send()
 
         def sent(g, carry):
@@ -357,40 +353,47 @@
         for j, p in enumerate(params):
             prow[j:j + 1, 0:LC] = p
         pcol[...] = prow[...].T
+        accr[...] = jnp.zeros_like(accr)
+
+        def use_both(g, carry):
+            for cp in rec_in(layer, g):
+                cp.wait()
+            ng = net.n[:, :, chunk(g)].reshape(B, GC)
+            for half in range(2):
+                r = lax.dot_general(wxb[half, :, chunk(g)], ng, NT, preferred_element_type=F32)
+                accr[0, half] += r[:, :HB]
+                accr[1, half] += r[:, HB:]
+            return carry
+
+        if layer == 0:
+            lax.fori_loop(0, G, use_both, 0)
+            slabs.begin()
+            for g in range(G):
+                wide(wd.at[0], wdb, ds, g).start()
 
         for h in range(2):
             lanes = slice(HB * h, HB * (h + 1))
-            accr[...] = jnp.zeros_like(accr)
 
             def use(i, g):
                 if h == 0:
                     for cp in rec_in(layer, g):
                         cp.wait()
-
-                def one(e, carry):
-                    cols = pl.ds(pl.multiple_of(g * GC + e * 1024, 1024), 1024)
-                    for half in range(2):
-                        accr[half] += lax.dot_general(wxb[half, :, cols], net.n[h, :, cols], NT, preferred_element_type=F32)
-                    return carry
-
-                unrolled(GC // 1024, one)
-
-            net.gathered(h, use, fresh=layer == 0)
+                for half in range(2):
+                    accr[h, half] += lax.dot_general(wxb[half, :, chunk(g)], net.n[h, :, chunk(g)], NT, preferred_element_type=F32)
+
+            if layer == 1:
+                net.gathered(h, use)
             if h == 0:
                 for cp in state_in(layer):
                     cp.wait()
-            elif layer == 0:
-                slabs.begin()
-                for g in range(G):
-                    wide(wd.at[0], wdb, ds, g).start()
             tk = tok[:, lanes]
             fresh = tk == 0
             for b in range(4):
                 rows = slice(176 * b, 176 * b + 176)
                 pc = pcol[rows, :]
                 col = lambda k: pc[:, k:k + 1]
-                xb = (accr[0, rows, :] + col(0)).astype(BF)
-                yb = jax.nn.gelu(accr[1, rows, :] + col(1), approximate=True)
+                xb = (accr[h, 0, rows, :] + col(0)).astype(BF)
+                yb = jax.nn.gelu(accr[h, 1, rows, :] + col(1), approximate=True)
                 xb_s[rows, lanes] = xb
                 hist = jnp.zeros((176, HB), F32)
                 for j in range(3):
@@ -462,7 +465,7 @@
         out_specs=(VM, VM, VM, VM, ANY, ANY),
         scratch_shapes=LINK_SCRATCH + [
             pltpu.VMEM((SLOTS, 2, SLAB, FC), BF), pltpu.VMEM((FC, D), BF), pltpu.VMEM((2, LC, D), BF), pltpu.VMEM((LC, D), BF),
-            pltpu.VMEM((2, HB, FC), F32), pltpu.VMEM((2, LC, HB), F32), pltpu.VMEM((HB, FC), BF), pltpu.VMEM((3, LC, B), BF), pltpu.VMEM((LC, B), BF), pltpu.VMEM((LC, B), F32),
+            pltpu.VMEM((2, HB, FC), F32), pltpu.VMEM((2, 2, LC, HB), F32), pltpu.VMEM((HB, FC), BF), pltpu.VMEM((3, LC, B), BF), pltpu.VMEM((LC, B), BF), pltpu.VMEM((LC, B), F32),
             pltpu.VMEM((LC + 64, HB), BF), pltpu.VMEM((16, LC + 64), F32), pltpu.VMEM((LC + 64, 16), F32),
             DMA((SLOTS, 3)), DMA((G,)), DMA((2, G)), DMA((G,)), DMA((2,)), DMA((3,)), DMA,
         ],

time: 297 us -> 295 us (level)
  no operation moved by 1% of the time
where the time goes in v8:
time: 295 us
  Pallas kernels  284 us (96%)
  local copies, waits for them, and re-layouts  7.04 us (2%)
  other arithmetic  3.26 us (1%)
    pallas_call x1, Pallas kernels, first_layers(): pl.pallas_call(kernel_a, name='first_layers', out_shape=(jax.ShapeDtypeSt...  133 us
    pallas_call x1, Pallas kernels, attend(): pl.pallas_call(attn_kernel, name='attend', in_specs=[pl.BlockSpec(memory_...  90.2 us
    pallas_call x1, Pallas kernels, last_layer(): pl.pallas_call(kernel_b, name='last_layer', out_shape=jax.ShapeDtypeStruc...  60.9 us

profile of v8, /device:TPU:1, one launch (start us, length us, event | category | flops | bytes accessed | tf_op | source)
XLA Modules:
  0.0 295.0 jit_solution(8849409771152637183)
XLA Ops:
  0.6 0.7 convert_bitcast_fusion
  1.3 1.3 fusion.4.sp_ref
  2.6 1.3 broadcast_in_dim.40.bo_ref
  4.0 1.3 fusion.2
  5.2 133.0 %first_layers.1 = (bf16[2,128,512]{2,1,0:T(8,128)(2,1)}, bf16[2,128,128]{2,1,0:T(8,128)(2,1)}, bf16[2,128,128]{2,1,0:T(8,128)(2,1)}, bf16[2,16,4096]{2,1,0:T(8,1...) custom-call(bf16[2,4,2,16,4096]{4,3,2,1,0:T(8,128)(2,1)} %bitcast.20, bf16[3,2,4096]{2,1,0:T(2,128)(2,1)} %sc_ref.3, ...), custom_call_target="tpu_custom_call" | custom-call | flops 30000001024 | bytes 400000000 | tf_op jit(solution)/shard_map/first_layers/pallas_call | solution.py:459
  138.2 90.2 %attend.1 = (bf16[256,512]{1,0:T(8,128)(2,1)}, bf16[256,1024,128]{2,1,0:T(8,128)(2,1)}, bf16[256,1024,128]{2,1,0:T(8,128)(2,1)}, s32[256,1024]{1,0:T(8,128)}) custom-call(s32[256]{0:T(256)} %tok_ref.1, bf16[256,512]{1,0:T(8,128)(2,1)} %bitcast.23, bf16[256,128]{1,0:T(8,128)(2,1)} %bitcast.25, bf16[256,128]{1,0:T(8,128)(2,1)} %bitcast.26, ...), custom_call_target="tpu_custom_call" | custom-call | flops 536870912 | bytes 268435456 | tf_op jit(solution)/shard_map/attend/pallas_call | solution.py:603
  228.4 60.9 %last_layer.1 = bf16[2,128,4096]{2,1,0:T(8,128)(2,1)} custom-call(bf16[2,128,512]{2,1,0:T(8,128)(2,1)} %bitcast.24, bf16[2,16,4096]{2,1,0:T(8,128)(2,1)} %get-tuple-element.20.x_ref, bf16[512,4096]{1,0:T(8,128)(2,1)} %wo.1, bf16[1,4096]{1,0:T(2,128)(2,1)} %broadcast_in_dim.40.bo_ref, bf16[3,2,4096]{2,1,0:T(2,128)(2,1)} %sc_ref.3, bf16[3,4096,1536]{2,1,0:T(8,128)(2,1)} %w1.3, ...), custom_call_target="tpu_custom_call" | custom-call | flops 12000000000 | bytes 200000000 | tf_op jit(solution)/shard_map/last_layer/pallas_call | solution.py:508
  289.3 0.0 copy-start
  289.3 0.0 copy-start.1
  289.3 3.3 %copy.41 = bf16[256,4096]{1,0:T(8,128)(2,1)} copy(bf16[256,4096]{1,0:T(8,128)(2,1)} %bitcast.17) | data formatting | bytes 4194304
  292.6 0.0 copy-done
  292.6 1.3 copy.42
  293.9 0.0 copy-done.1
  293.9 1.1 copy.43
  (2 shorter events, 0.0 us)
Async XLA Ops:
  289.3 3.3 %copy-start = (bf16[2,3,704,256]{3,2,1,0:T(8,128)(2,1)S(1)}, bf16[2,3,704,256]{3,2,1,0:T(8,128)(2,1)}, u32[]{:S(2)}) copy-start(bf16[2,3,704,256]{3,2,1,0:T(8,128)(2,1)} %get-tuple-element.21) | copy-start | bytes 6488068
  289.3 4.6 %copy-start.1 = (f32[2,704,256]{2,1,0:T(8,128)S(1)}, f32[2,704,256]{2,1,0:T(8,128)}, u32[]{:S(2)}) copy-start(f32[2,704,256]{2,1,0:T(8,128)} %get-tuple-element.22) | copy-start | bytes 4325380
